TPU v7x, 32 devices: a whole 2x2x4 slice. The times are simulated.
32 devices in a mesh: dp: 4 (over z), ctx: 8 (over y, x, core).
Axes of the slice: x: 2, y: 2, z: 4, core: 2. Of those that a mesh axis runs over, the one named last changes fastest.
Arguments:
- block_input: bfloat16 [4096, 2048], P(('dp', 'ctx')), may hold values from -8 to 8
- out_cotangent: float32 [4096, 2048], P(('dp', 'ctx')), may hold values from -6 to 6
- group_perm: int32 [4, 16], P('dp'), may hold values from 0 to 15, each once within a row
- attn_norm_gain: bfloat16 [2048], replicated, may hold values from 0.5 to 1.5
- attn_norm_bias: bfloat16 [2048], replicated, may hold values from -2 to 2
- qkv_weight: bfloat16 [3, 2048, 2048], P(None, 'dp', 'ctx'), may hold values from -0.198873782 to 0.198873782
- qkv_bias: bfloat16 [3, 2048], replicated, may hold values from -3 to 3
- out_weight: bfloat16 [2048, 2048], P('ctx', 'dp'), may hold values from -3 to 3
- mlp_norm_gain: bfloat16 [2048], replicated, may hold values from 0.5 to 1.5
- mlp_norm_bias: bfloat16 [2048], replicated, may hold values from -2 to 2
- gateup_weight: bfloat16 [2, 2048, 5632], P(None, 'dp', 'ctx'), may hold values from -0.125 to 0.125
- down_weight: bfloat16 [5632, 2048], P('ctx', 'dp'), may hold values from -0.078125 to 0.078125
Outputs:
- block_output: bfloat16 [4096, 2048], P(('dp', 'ctx'))
- input_grad: float32 [4096, 2048], P(('dp', 'ctx'))
- attn_norm_gain_grad: float32 [2048], replicated
- attn_norm_bias_grad: float32 [2048], replicated
- qkv_weight_grad: float32 [3, 2048, 2048], P(None, 'dp', 'ctx')
- qkv_bias_grad: float32 [3, 2048], replicated
- out_weight_grad: float32 [2048, 2048], P('ctx', 'dp')
- mlp_norm_gain_grad: float32 [2048], replicated
- mlp_norm_bias_grad: float32 [2048], replicated
- gateup_weight_grad: float32 [2, 2048, 5632], P(None, 'dp', 'ctx')
- down_weight_grad: float32 [5632, 2048], P('ctx', 'dp')
Inputs may be any that keep to these rules, and one draw needn't show every extreme that they name: `group_perm`: each row names every block 0 to 15 once; device c of ctx holds the blocks of 64 tokens named at entries 2 c and 2 c + 1 of its sequence's row, in that order.
All inputs are finite; a program needn't handle non-finite values.
Results may differ from a plain program's by a relative error of at most 0.025.
Values may be sent and summed in bfloat16 or wider, within the bound.
A program may use at most 192 MiB of HBM per device.

v0:
```python
import math

import jax
import jax.numpy as jnp
from jax import lax
from jax.sharding import PartitionSpec as P

D = 2048
HEADS = 32
HEAD_DIM = 64
ROT = 16


eps_norm = 1e-05
rope_base = 10000.0
neg_big = -1e30


def apply_layer_norm(values, gain_vec, bias_vec):
    mean_val = jnp.mean(values, axis=-1, keepdims=True)
    centred = values - mean_val
    variance = jnp.mean(centred * centred, axis=-1, keepdims=True)
    rscale = lax.rsqrt(variance + eps_norm)
    normed = centred * rscale
    return (normed * gain_vec + bias_vec, normed, rscale)


def layer_norm_backward(grad_out, normed, rscale, gain_vec):
    gain_grad = jnp.sum(grad_out * normed, axis=0)
    bias_grad = jnp.sum(grad_out, axis=0)
    scaled = grad_out * gain_vec
    grad_in = rscale * (
        scaled
        - jnp.mean(scaled, axis=-1, keepdims=True)
        - normed * jnp.mean(scaled * normed, axis=-1, keepdims=True)
    )
    return (grad_in, gain_grad, bias_grad)


def rope_tables(positions):
    half_rot = ROT // 2
    exponent = jnp.arange(half_rot, dtype=jnp.float32) * (2.0 / ROT)
    inverse = jnp.exp(-exponent * math.log(rope_base))
    angle_val = positions.astype(jnp.float32)[:, None] * inverse[None, :]
    return (jnp.cos(angle_val)[:, None, :], jnp.sin(angle_val)[:, None, :])


def rotate(tensor, cosine, sine_val):
    half_rot = ROT // 2
    first_half = tensor[..., :half_rot]
    second = tensor[..., half_rot:ROT]
    remainder = tensor[..., ROT:]
    return jnp.concatenate(
        [
            first_half * cosine - second * sine_val,
            second * cosine + first_half * sine_val,
            remainder,
        ],
        axis=-1,
    )


def unrotate(tensor, cosine, sine_val):
    half_rot = ROT // 2
    first_half = tensor[..., :half_rot]
    second = tensor[..., half_rot:ROT]
    remainder = tensor[..., ROT:]
    return jnp.concatenate(
        [
            first_half * cosine + second * sine_val,
            second * cosine - first_half * sine_val,
            remainder,
        ],
        axis=-1,
    )


def group_positions(group_order, count, half_group):
    row_ids = jnp.arange(count, dtype=jnp.int32)
    group_ids = row_ids // half_group
    matches = group_ids[:, None] == jnp.arange(group_order.shape[0], dtype=jnp.int32)[None, :]
    group_start = jnp.sum(jnp.where(matches, group_order[None, :], 0), axis=1)
    return group_start * half_group + row_ids % half_group


def gather_pair(first, second):
    return (
        lax.all_gather(first, "dp", axis=1, tiled=True),
        lax.all_gather(second, "dp", axis=1, tiled=True),
    )


def shard_pair(first, second):
    return (
        lax.psum_scatter(first.astype(jnp.bfloat16), "dp", scatter_dimension=1, tiled=True).astype(
            jnp.float32
        ),
        lax.psum_scatter(second.astype(jnp.bfloat16), "dp", scatter_dimension=1, tiled=True).astype(
            jnp.float32
        ),
    )


def per_device(
    block_input,
    out_cotangent,
    group_perm,
    attn_norm_gain,
    attn_norm_bias,
    qkv_weight,
    qkv_bias,
    out_weight,
    mlp_norm_gain,
    mlp_norm_bias,
    gateup_weight,
    down_weight,
):
    f32 = jnp.float32
    bf16 = jnp.bfloat16
    tok_rows = block_input.shape[0]
    cycle_size = lax.axis_size("ctx")
    cycle_index = lax.axis_index("ctx")
    seq_len = tok_rows * cycle_size
    half_group = tok_rows // 2
    group_order = group_perm[0]
    score_scale = 1.0 / math.sqrt(HEAD_DIM)
    first_norm_scale = attn_norm_gain.astype(f32)
    first_norm_bias = attn_norm_bias.astype(f32)
    second_norm_scale = mlp_norm_gain.astype(f32)
    second_norm_bias = mlp_norm_bias.astype(f32)
    qkv_shift = qkv_bias.astype(f32)
    inputs_wide_float = block_input.astype(f32)
    first_normalized_rows, first_centered_scaled, first_inverse_deviation = apply_layer_norm(
        inputs_wide_float, first_norm_scale, first_norm_bias
    )
    normed_one_b = first_normalized_rows.astype(bf16)
    cot_b = out_cotangent.astype(bf16)
    rows_all, cot_all = (
        lax.all_gather(normed_one_b, "ctx", axis=0, tiled=True),
        lax.all_gather(cot_b, "ctx", axis=0, tiled=True),
    )
    attn_pair = gather_pair(qkv_weight, out_weight)
    qkv_local, out_local = (attn_pair[0], attn_pair[1])
    all_pos = group_positions(group_order, seq_len, half_group)
    cos_all, sin_all = rope_tables(all_pos)
    local_heads = HEADS // cycle_size
    width_local = local_heads * HEAD_DIM
    head_first = cycle_index * width_local
    shift_local = lax.dynamic_slice_in_dim(qkv_shift, head_first, width_local, 1)
    query_raw = jnp.dot(rows_all, qkv_local[0], preferred_element_type=f32) + shift_local[0]
    key_raw = jnp.dot(rows_all, qkv_local[1], preferred_element_type=f32) + shift_local[1]
    value_raw = jnp.dot(rows_all, qkv_local[2], preferred_element_type=f32) + shift_local[2]
    query = rotate(query_raw.reshape(seq_len, local_heads, HEAD_DIM), cos_all, sin_all).astype(bf16)
    keys_b = rotate(key_raw.reshape(seq_len, local_heads, HEAD_DIM), cos_all, sin_all).astype(bf16)
    values_b = value_raw.reshape(seq_len, local_heads, HEAD_DIM).astype(bf16)
    query_block = min(512, seq_len)
    block_count = seq_len // query_block
    query_blocks = query.reshape(block_count, query_block, local_heads, HEAD_DIM)
    pos_blocks = all_pos.reshape(block_count, query_block)

    def forward_block(inputs):
        query_blk, pos_blk = inputs
        scores = (
            jnp.einsum("rhd,nhd->hrn", query_blk, keys_b, preferred_element_type=f32) * score_scale
        )
        visible = all_pos[None, None, :] <= pos_blk[None, :, None]
        scores = jnp.where(visible, scores, neg_big)
        peak = jnp.max(scores, axis=-1)
        probs = jnp.where(visible, jnp.exp(scores - peak[..., None]), 0.0)
        total = jnp.sum(probs, axis=-1)
        accum = jnp.einsum("hrn,nhd->rhd", probs.astype(bf16), values_b, preferred_element_type=f32)
        return ((accum / total.T[:, :, None]).astype(bf16), peak + jnp.log(total))

    attn_blocks, lse_blocks = lax.map(forward_block, (query_blocks, pos_blocks))
    attn_local = attn_blocks.reshape(seq_len, width_local)
    residual_stream = inputs_wide_float + lax.psum_scatter(
        jnp.dot(attn_local, out_local, preferred_element_type=f32).astype(jnp.bfloat16),
        "ctx",
        scatter_dimension=0,
        tiled=True,
    ).astype(jnp.float32)
    second_normalized_rows, second_centered_scaled, second_inverse_deviation = apply_layer_norm(
        residual_stream, second_norm_scale, second_norm_bias
    )
    normed_two_b = second_normalized_rows.astype(bf16)
    mlp_all = lax.all_gather(normed_two_b, "ctx", axis=0, tiled=True)
    mlp_pair = gather_pair(gateup_weight, down_weight)
    gateup_local, down_local = (mlp_pair[0], mlp_pair[1])
    gate_val = jnp.dot(mlp_all, gateup_local[0], preferred_element_type=f32)
    up_val = jnp.dot(mlp_all, gateup_local[1], preferred_element_type=f32)
    sigma = jax.nn.sigmoid(gate_val)
    hidden_b = (gate_val * sigma * up_val).astype(bf16)
    down_term = jnp.dot(hidden_b, down_local, preferred_element_type=f32)
    hidden_grad = jnp.dot(cot_all, down_local.T, preferred_element_type=f32)
    gate_grad = (hidden_grad * up_val * sigma * (1.0 + gate_val * (1.0 - sigma))).astype(bf16)
    up_grad = (hidden_grad * gate_val * sigma).astype(bf16)
    normed_two_term = jnp.dot(gate_grad, gateup_local[0].T, preferred_element_type=f32) + jnp.dot(
        up_grad, gateup_local[1].T, preferred_element_type=f32
    )
    down_sum, second_normalized_gradient = (
        lax.psum_scatter(
            down_term.astype(jnp.bfloat16), "ctx", scatter_dimension=0, tiled=True
        ).astype(jnp.float32),
        lax.psum_scatter(
            normed_two_term.astype(jnp.bfloat16), "ctx", scatter_dimension=0, tiled=True
        ).astype(jnp.float32),
    )
    block_output = (residual_stream + down_sum).astype(bf16)
    down_w_grad = jnp.dot(hidden_b.T, cot_all, preferred_element_type=f32)
    gateup_w_grad = jnp.einsum(
        "td,ktf->kdf", mlp_all, jnp.stack([gate_grad, up_grad]), preferred_element_type=f32
    )
    gateup_grads, down_grads = shard_pair(gateup_w_grad, down_w_grad)
    residual_slice, second_norm_scale_gradient, second_norm_bias_gradient = layer_norm_backward(
        second_normalized_gradient,
        second_centered_scaled,
        second_inverse_deviation,
        second_norm_scale,
    )
    resid_grad = out_cotangent + residual_slice
    resid_b = resid_grad.astype(bf16)
    resid_all = lax.all_gather(resid_b, "ctx", axis=0, tiled=True)
    out_w_grad = jnp.dot(attn_local.T, resid_all, preferred_element_type=f32)
    attn_val_grad = jnp.dot(resid_all, out_local.T, preferred_element_type=f32).reshape(
        seq_len, local_heads, HEAD_DIM
    )
    delta = jnp.sum(
        attn_val_grad * attn_local.reshape(seq_len, local_heads, HEAD_DIM).astype(f32), axis=-1
    )
    attn_grad_b = attn_val_grad.astype(bf16)

    def backward_block(carry, inputs):
        key_grad, value_grad = carry
        query_blk, pos_blk, lse_blk, grad_blk, delta_blk = inputs
        scores = (
            jnp.einsum("rhd,nhd->hrn", query_blk, keys_b, preferred_element_type=f32) * score_scale
        )
        visible = all_pos[None, None, :] <= pos_blk[None, :, None]
        scores = jnp.where(visible, scores, neg_big)
        probs = jnp.where(visible, jnp.exp(scores - lse_blk[..., None]), 0.0)
        value_grad = value_grad + jnp.einsum(
            "hrn,rhd->nhd", probs.astype(bf16), grad_blk, preferred_element_type=f32
        )
        prob_grad = jnp.einsum("rhd,nhd->hrn", grad_blk, values_b, preferred_element_type=f32)
        score_grad = (probs * (prob_grad - delta_blk.T[:, :, None])).astype(bf16)
        query_grad_blk = (
            jnp.einsum("hrn,nhd->rhd", score_grad, keys_b, preferred_element_type=f32) * score_scale
        )
        key_grad = (
            key_grad
            + jnp.einsum("hrn,rhd->nhd", score_grad, query_blk, preferred_element_type=f32)
            * score_scale
        )
        return ((key_grad, value_grad), query_grad_blk)

    zero_kv = jnp.zeros((seq_len, local_heads, HEAD_DIM), f32)
    (key_grad, value_grad), query_grads = lax.scan(
        backward_block,
        (zero_kv, zero_kv),
        (
            query_blocks,
            pos_blocks,
            lse_blocks,
            attn_grad_b.reshape(block_count, query_block, local_heads, HEAD_DIM),
            delta.reshape(block_count, query_block, local_heads),
        ),
    )
    query_grad = query_grads.reshape(seq_len, local_heads, HEAD_DIM)
    grad_parts = jnp.stack(
        [
            unrotate(query_grad, cos_all, sin_all).reshape(seq_len, width_local),
            unrotate(key_grad, cos_all, sin_all).reshape(seq_len, width_local),
            value_grad.reshape(seq_len, width_local),
        ],
        axis=1,
    )
    shift_part = jnp.sum(grad_parts, axis=0)
    shift_grad = lax.dynamic_update_slice_in_dim(jnp.zeros((3, D), f32), shift_part, head_first, 1)
    grad_parts_b = grad_parts.astype(bf16)
    qkv_w_grad = jnp.einsum("td,tkc->kdc", rows_all, grad_parts_b, preferred_element_type=f32)
    first_normalized_gradient = lax.psum_scatter(
        jnp.einsum("tkc,kdc->td", grad_parts_b, qkv_local, preferred_element_type=f32).astype(
            jnp.bfloat16
        ),
        "ctx",
        scatter_dimension=0,
        tiled=True,
    ).astype(jnp.float32)
    qkv_grads, out_grads = shard_pair(qkv_w_grad, out_w_grad)
    input_slice, first_norm_scale_gradient, first_norm_bias_gradient = layer_norm_backward(
        first_normalized_gradient, first_centered_scaled, first_inverse_deviation, first_norm_scale
    )
    input_grad = resid_grad + input_slice
    small = lax.psum(
        (
            first_norm_scale_gradient,
            first_norm_bias_gradient,
            shift_grad,
            second_norm_scale_gradient,
            second_norm_bias_gradient,
        ),
        ("dp", "ctx"),
    )
    return (
        block_output,
        input_grad,
        small[0],
        small[1],
        qkv_grads,
        small[2],
        out_grads,
        small[3],
        small[4],
        gateup_grads,
        down_grads,
    )


def solution(mesh):
    return jax.shard_map(
        per_device,
        mesh=mesh,
        in_specs=(
            P(("dp", "ctx"), None),
            P(("dp", "ctx"), None),
            P("dp", None),
            P(),
            P(),
            P(None, "dp", "ctx"),
            P(),
            P("ctx", "dp"),
            P(),
            P(),
            P(None, "dp", "ctx"),
            P("ctx", "dp"),
        ),
        out_specs=(
            P(("dp", "ctx"), None),
            P(("dp", "ctx"), None),
            P(),
            P(),
            P(None, "dp", "ctx"),
            P(),
            P("ctx", "dp"),
            P(),
            P(),
            P(None, "dp", "ctx"),
            P("ctx", "dp"),
        ),
        check_vma=False,
    )
```

profile of v0, /device:TPU:0, one launch (start us, length us, event | category | flops | bytes accessed | tf_op | source)
XLA Modules:
  0.0 943.5 jit_solution(9635432900892559740)
XLA Ops:
  16.7 59.0 %all-gather.11.cloned.1.call-done = bf16[3,2048,256]{2,1,0:T(8,128)(2,1)} async-done(((bf16[3,512,256]{2,1,0:T(8,128)(2,1)}), bf16[3,2048,256]{2,1,0:T(8,128)(2,1)}) %all-gather.11.cloned.1.call-update) | async-done | bytes 3145744 | tf_op jit(solution)/shard_map/all_gather | solution.py:88
  75.8 37.8 %all-gather.9.cloned.1.call-done = bf16[1024,2048]{1,0:T(8,128)(2,1)} async-done(((bf16[128,2048]{1,0:T(8,128)(2,1)}), bf16[1024,2048]{1,0:T(8,128)(2,1)}) %all-gather.9.cloned.1.call-update) | async-done | bytes 4194320 | tf_op jit(solution)/shard_map/all_gather | solution.py:139
  113.5 3.9 convolution_add_fusion.1
  121.1 15.3 %while.27 = (s32[]{:T(128)}, bf16[2,512,4,64]{1,3,2,0:T(8,128)(2,1)S(1)}, f32[2,4,512]{2,1,0:T(4,128)S(1)}, s32[1024]{0:T(1024)S(1)}, s32[2,512]{1,0:T(2,128)S(1...) while((s32[]{:T(128)}, ...), condition=%wide.region_6.7_spmd, body=%wide.region_3.6_spmd.sunk | while | flops 564918272 | bytes 28911732 | solution.py:174
  123.2 2.9 fusion.168
  126.1 2.6 fusion.169
  130.9 2.9 fusion.168
  133.8 2.6 fusion.169
  137.1 6.1 all-gather.13.cloned.1.call-done
  143.1 4.6 convolution_convert_fusion.1
  148.4 50.0 %reduce-scatter.9.cloned.1.call-done = bf16[128,2048]{1,0:T(8,128)(2,1)} async-done(((bf16[1024,2048]{1,0:T(8,128)(2,1)}), bf16[128,2048]{1,0:T(8,128)(2,1)}) %reduce-scatter.9.cloned.1.call-update) | async-done | bytes 524304 | tf_op jit(solution)/shard_map/reduce_scatter | solution.py:176
  205.2 101.3 %all-gather.17.cloned.1.call-done = bf16[2,2048,704]{1,2,0:T(8,128)(2,1)} async-done(((bf16[2,512,704]{1,2,0:T(8,128)(2,1)}), bf16[2,2048,704]{1,2,0:T(8,128)(2,1)}) %all-gather.17.cloned.1.call-update) | async-done | bytes 5767184 | tf_op jit(solution)/shard_map/all_gather | solution.py:88
  306.6 37.2 %all-gather.15.cloned.1.call-done = bf16[1024,2048]{1,0:T(8,128)(2,1)} async-done(((bf16[128,2048]{1,0:T(8,128)(2,1)}), bf16[1024,2048]{1,0:T(8,128)(2,1)}) %all-gather.15.cloned.1.call-update) | async-done | bytes 4194320 | tf_op jit(solution)/shard_map/all_gather | solution.py:186
  343.8 8.0 fusion.71
  351.7 4.7 fusion.70
  356.5 48.0 %all-gather.19.cloned.1.call-done = bf16[704,2048]{1,0:T(8,128)(2,1)} async-done(((bf16[704,512]{1,0:T(8,128)(2,1)}), bf16[704,2048]{1,0:T(8,128)(2,1)}) %all-gather.19.cloned.1.call-update) | async-done | bytes 2883600 | tf_op jit(solution)/shard_map/all_gather | solution.py:89
  404.5 37.8 %all-gather.21.cloned.1.call-done = bf16[1024,2048]{1,0:T(8,128)(2,1)} async-done(((bf16[128,2048]{1,0:T(8,128)(2,1)}), bf16[1024,2048]{1,0:T(8,128)(2,1)}) %all-gather.21.cloned.1.call-update) | async-done | bytes 4194320 | tf_op jit(solution)/shard_map/all_gather | solution.py:140
  442.3 10.0 %multiply_convert_fusion.1 = (bf16[1024,704]{0,1:T(8,128)(2,1)S(1)}, bf16[1024,704]{0,1:T(8,128)(2,1)S(1)}, bf16[1024,704]{0,1:T(8,128)(2,1)}) fusion(f32[1024,704]{0,1:T(8,128)} %fusion.70, f32[1024,704]{0,1:T(8,128)} %fusion.71, bf16[1024,2048]{1,0:T(8,128)(2,1)} %all-gather.21.cloned.1.call-done, bf16[704,2048]{1,0:T(8,128)(2,1)} %all-gather.19.cloned.1.call-done), kind=kOutput, calls=%fused_computation.71 | convolution fusion | flops 2964324352 | bytes 17170432 | tf_op jit(solution)/shard_map/dot_general | solution.py:194
  452.3 6.4 fusion.69
  458.7 17.2 %add_convert_fusion = bf16[1024,2048]{1,0:T(8,128)(2,1)} fusion(f32[1024,2048]{1,0:T(8,128)S(1)} %fusion.69, bf16[1024,704]{0,1:T(8,128)(2,1)S(1)} %get-tuple-element.288, bf16[2,2048,704]{1,2,0:T(8,128)(2,1)} %all-gather.17.cloned.1.call-done), kind=kOutput, calls=%fused_computation.55 | convolution fusion | flops 2956984320 | bytes 16908288 | tf_op jit(solution)/shard_map/dot_general | solution.py:197
  475.9 7.7 convolution_convert_fusion
  483.7 43.5 %reduce-scatter.13.cloned.1.call-done = bf16[128,2048]{1,0:T(8,128)(2,1)} async-done(((bf16[1024,2048]{1,0:T(8,128)(2,1)}), bf16[128,2048]{1,0:T(8,128)(2,1)}) %reduce-scatter.13.cloned.1.call-update) | async-done | bytes 524304 | tf_op jit(solution)/shard_map/reduce_scatter | solution.py:204
  528.8 52.8 %reduce-scatter.11.cloned.1.call-done = bf16[128,2048]{1,0:T(8,128)(2,1)} async-done(((bf16[1024,2048]{1,0:T(8,128)(2,1)}), bf16[128,2048]{1,0:T(8,128)(2,1)}) %reduce-scatter.11.cloned.1.call-update) | async-done | bytes 524304 | tf_op jit(solution)/shard_map/reduce_scatter | solution.py:201
  581.6 3.2 fusion.113
  584.9 7.4 convolution_convert_fusion.2
  592.4 10.5 %convert_bitcast_fusion = bf16[2,2048,704]{1,2,0:T(8,128)(2,1)} fusion(bf16[1024,2048]{1,0:T(8,128)(2,1)} %all-gather.15.cloned.1.call-done, bf16[1,1024,704]{1,2,0:T(8,128)(2,1)S(1)} %bitcast.211, bf16[1,1024,704]{1,2,0:T(8,128)(2,1)} %bitcast.212), kind=kOutput, calls=%fused_computation.56 | convolution fusion | flops 5909905408 | bytes 12845056 | tf_op jit(solution)/shard_map/td,ktf->kdf/dot_general | solution.py:210
  605.2 16.4 %all-gather.23.cloned.1.call-done = bf16[1024,2048]{1,0:T(8,128)(2,1)} async-done(((bf16[128,2048]{1,0:T(8,128)(2,1)}), bf16[1024,2048]{1,0:T(8,128)(2,1)}) %all-gather.23.cloned.1.call-update) | async-done | bytes 4194320 | tf_op jit(solution)/shard_map/all_gather | solution.py:222
  621.6 4.9 fusion.116
  632.4 4.4 convolution_convert_fusion.3
  637.1 46.0 %while.28 = (s32[]{:T(128)}, f32[1024,4,64]{0,2,1:T(8,128)S(1)}, f32[1024,4,64]{0,2,1:T(8,128)}, f32[2,512,4,64]{1,0,3,2:T(2,128)}, bf16[2,512,4,64]{1,3,2,0:T(8...) while((s32[]{:T(128)}, f32[1024,4,64]{0,2,1:T(8,128)S(1)}, ...), condition=%wide.region_16.17_spmd.clone, body=%wide.region_15.16_spmd.clone.sunk | while | flops 1369309184 | bytes 53020908 | solution.py:257
  638.9 3.7 fusion.182
  642.6 3.6 multiply_convert_fusion.5
  649.2 10.4 %dynamic_update_slice.25 = f32[2,512,4,64]{1,0,3,2:T(2,128)} dynamic-update-slice(f32[2,512,4,64]{1,0,3,2:T(2,128)} %get-tuple-element.486, f32[1,512,4,64]{1,0,3,2:T(1,128)S(1)} %copy.80, s32[]{:T(128)S(6)} %copy.99, s32[]{:T(128)} %constant.100.clone.1..sunk, s32[]{:T(128)} %constant.100.clone.1..sunk, s32[]{:T(128)} %constant.100.clone.1..sunk) | dynamic-update-slice | bytes 1048580 | tf_op jit(solution)/shard_map/while/body/jit(dynamic_update_index_in_dim)/dynamic_update_slice | solution.py:257
  661.3 4.8 fusion.182
  666.1 3.6 multiply_convert_fusion.5
  672.7 10.4 %dynamic_update_slice.25 = f32[2,512,4,64]{1,0,3,2:T(2,128)} dynamic-update-slice(f32[2,512,4,64]{1,0,3,2:T(2,128)} %get-tuple-element.486, f32[1,512,4,64]{1,0,3,2:T(1,128)S(1)} %copy.80, s32[]{:T(128)S(6)} %copy.99, s32[]{:T(128)} %constant.100.clone.1..sunk, s32[]{:T(128)} %constant.100.clone.1..sunk, s32[]{:T(128)} %constant.100.clone.1..sunk) | dynamic-update-slice | bytes 1048580 | tf_op jit(solution)/shard_map/while/body/jit(dynamic_update_index_in_dim)/dynamic_update_slice | solution.py:257
  685.2 2.5 copy.53
  694.2 2.6 copy.52
  696.8 7.7 bitcast_convert_fusion
  704.8 7.6 fusion.63
  714.9 70.0 %reduce-scatter.21.cloned.1.call-done = bf16[2,512,704]{1,2,0:T(8,128)(2,1)} async-done(((bf16[2,2048,704]{1,2,0:T(8,128)(2,1)}), bf16[2,512,704]{1,2,0:T(8,128)(2,1)}) %reduce-scatter.21.cloned.1.call-update) | async-done | bytes 1441808 | tf_op jit(solution)/shard_map/reduce_scatter | solution.py:95
  785.0 3.3 convert_element_type.177
  790.2 24.8 %reduce-scatter.19.cloned.1.call-done = bf16[256,512]{1,0:T(8,128)(2,1)} async-done(((bf16[256,2048]{1,0:T(8,128)(2,1)}), bf16[256,512]{1,0:T(8,128)(2,1)}) %reduce-scatter.19.cloned.1.call-update) | async-done | bytes 262160 | tf_op jit(solution)/shard_map/reduce_scatter | solution.py:98
  816.8 51.1 %reduce-scatter.15.cloned.1.call-done = bf16[128,2048]{1,0:T(8,128)(2,1)} async-done(((bf16[1024,2048]{1,0:T(8,128)(2,1)}), bf16[128,2048]{1,0:T(8,128)(2,1)}) %reduce-scatter.15.cloned.1.call-update) | async-done | bytes 524304 | tf_op jit(solution)/shard_map/reduce_scatter | solution.py:281
  869.4 44.9 %all-reduce = (f32[2048]{0:T(1024)}, f32[2048]{0:T(1024)}, f32[3,2048]{1,0:T(4,128)}, f32[2048]{0:T(1024)}, f32[2048]{0:T(1024)}) all-reduce(f32[2048]{0:T(1024)S(1)} %get-tuple-element.233, f32[2048]{0:T(1024)S(1)} %get-tuple-element.238, ...), channel_id=1, replica_groups=mesh['dp'=4,'ctx'=8] {'dp','ctx'}, use_global_device_ids=true, to_apply=%region_21.22 | all-reduce | flops 14336 | bytes 114688 | tf_op jit(solution)/shard_map/psum | solution.py:294
  914.3 17.2 %reduce-scatter.17.cloned.1.call-done = bf16[3,512,256]{1,2,0:T(8,128)(2,1)} async-done(((bf16[3,2048,256]{1,2,0:T(8,128)(2,1)}), bf16[3,512,256]{1,2,0:T(8,128)(2,1)}) %reduce-scatter.17.cloned.1.call-update) | async-done | bytes 786448 | tf_op jit(solution)/shard_map/reduce_scatter | solution.py:95
  931.5 2.5 copy.55
  934.0 2.5 fusion.89
  (183 shorter events, 61.1 us)
Async XLA Ops:
  7.2 68.6 %all-gather.11.cloned.1.call-start = ((), (), s32[]{:S(2)}) async-start(), calls=%async_computation.9 | async-start | bytes 3932160 | tf_op jit(solution)/shard_map/all_gather | solution.py:88
  7.9 105.6 %all-gather.9.cloned.1.call-start = ((), (), s32[]{:S(2)}) async-start(), calls=%async_computation.8 | async-start | bytes 4718592 | tf_op jit(solution)/shard_map/all_gather | solution.py:139
  8.6 108.8 %copy-start.13 = (f32[2048]{0:T(1024)}, f32[2048]{0:T(1024)S(1)}, u32[]{:S(2)}) copy-start(f32[2048]{0:T(1024)S(1)} %convert_element_type.141) | copy-start | bytes 24580
  10.5 106.9 %copy-start.15 = (f32[128]{0:T(128)}, f32[128]{0:T(128)S(1)}, u32[]{:S(2)}) copy-start(f32[128]{0:T(128)S(1)} %broadcast_multiply_fusion.6) | copy-start | bytes 1540
  11.9 105.6 %copy-start.17 = (f32[128]{0:T(128)}, f32[128]{0:T(128)S(1)}, u32[]{:S(2)}) copy-start(f32[128]{0:T(128)S(1)} %add_rsqrt_fusion.1) | copy-start | bytes 1540
  14.2 129.0 %all-gather.13.cloned.1.call-start = ((), (), s32[]{:S(2)}) async-start(), calls=%async_computation.10 | async-start | bytes 1310720 | tf_op jit(solution)/shard_map/all_gather | solution.py:89
  14.9 183.6 %reduce-scatter.9.cloned.1.call-start = ((), (), s32[]{:S(2)}) async-start(), calls=%async_computation.11 | async-start | bytes 4718592 | tf_op jit(solution)/shard_map/reduce_scatter | solution.py:176
  16.7 102.9 %copy-start.11 = (f32[1024,8]{0,1:T(8,128)}, f32[1024,8]{0,1:T(8,128)S(1)}, u32[]{:S(2)}) copy-start(f32[1024,8]{0,1:T(8,128)S(1)} %get-tuple-element.304) | copy-start | bytes 98308
  16.7 102.9 %copy-start.12 = (f32[1024,8]{0,1:T(8,128)}, f32[1024,8]{0,1:T(8,128)S(1)}, u32[]{:S(2)}) copy-start(f32[1024,8]{0,1:T(8,128)S(1)} %get-tuple-element.305) | copy-start | bytes 98308
  113.5 4.0 copy-start.22
  113.5 4.7 copy-start.24
  136.4 6.7 copy-start.28
  136.4 11.3 %copy-start.8 = (bf16[2,512,4,64]{1,3,2,0:T(8,128)(2,1)}, bf16[2,512,4,64]{1,3,2,0:T(8,128)(2,1)S(1)}, u32[]{:S(2)}) copy-start(bf16[2,512,4,64]{1,3,2,0:T(8,128)(2,1)S(1)} %get-tuple-element.118) | copy-start | bytes 1572868
  137.1 6.1 copy-start.6
  147.7 0.7 copy-start.19
  147.7 0.7 copy-start.20
  147.7 50.7 %copy-start = (bf16[128,2048]{1,0:T(8,128)(2,1)S(1)}, bf16[128,2048]{1,0:T(8,128)(2,1)}, u32[]{:S(2)}) copy-start(bf16[128,2048]{1,0:T(8,128)(2,1)} %param.16) | copy-start | bytes 1572868
  147.8 56.3 %copy-start.2 = (f32[128,2048]{1,0:T(8,128)S(1)}, f32[128,2048]{1,0:T(8,128)}, u32[]{:S(2)}) copy-start(f32[128,2048]{1,0:T(8,128)} %param.17) | copy-start | bytes 3145732
  147.8 158.8 %all-gather.17.cloned.1.call-start = ((), (), s32[]{:S(2)}) async-start(), calls=%async_computation.13 | async-start | bytes 7208960 | tf_op jit(solution)/shard_map/all_gather | solution.py:88
  148.4 195.4 %all-gather.15.cloned.1.call-start = ((), (), s32[]{:S(2)}) async-start(), calls=%async_computation.12 | async-start | bytes 4718592 | tf_op jit(solution)/shard_map/all_gather | solution.py:186
  203.2 201.3 %all-gather.19.cloned.1.call-start = ((), (), s32[]{:S(2)}) async-start(), calls=%async_computation.14 | async-start | bytes 3604480 | tf_op jit(solution)/shard_map/all_gather | solution.py:89
  204.0 238.3 %all-gather.21.cloned.1.call-start = ((), (), s32[]{:S(2)}) async-start(), calls=%async_computation.16 | async-start | bytes 4718592 | tf_op jit(solution)/shard_map/all_gather | solution.py:140
  204.9 322.2 %reduce-scatter.13.cloned.1.call-start = ((), (), s32[]{:S(2)}) async-start(), calls=%async_computation.17 | async-start | bytes 4718592 | tf_op jit(solution)/shard_map/reduce_scatter | solution.py:204
  343.8 8.0 copy-start.21
  343.8 8.0 copy-start.23
  452.3 6.4 copy-start.27
  452.3 6.4 copy-start.25
  475.9 105.7 %reduce-scatter.11.cloned.1.call-start = ((), (), s32[]{:S(2)}) async-start(), calls=%async_computation.15 | async-start | bytes 4718592 | tf_op jit(solution)/shard_map/reduce_scatter | solution.py:201
  483.6 43.6 %copy-start.1 = (bf16[128,2048]{1,0:T(8,128)(2,1)S(1)}, bf16[128,2048]{1,0:T(8,128)(2,1)}, u32[]{:S(2)}) copy-start(bf16[128,2048]{1,0:T(8,128)(2,1)} %reduce-scatter.9.cloned.1.call-done) | copy-start | bytes 1572868
  483.6 137.9 %all-gather.23.cloned.1.call-start = ((), (), s32[]{:S(2)}) async-start(), calls=%async_computation.18 | async-start | bytes 4718592 | tf_op jit(solution)/shard_map/all_gather | solution.py:222
  584.8 7.6 copy-start.26
  584.8 127.7 %reduce-scatter.23.cloned.1.call-start = ((), (), s32[]{:S(2)}) async-start(), calls=%async_computation.23 | async-start | bytes 3604480 | tf_op jit(solution)/shard_map/reduce_scatter | solution.py:98
  592.3 192.7 %reduce-scatter.21.cloned.1.call-start = ((), (), s32[]{:S(2)}) async-start(), calls=%async_computation.22 | async-start | bytes 7208960 | tf_op jit(solution)/shard_map/reduce_scatter | solution.py:95
  602.9 1.0 copy-start.9
  603.0 212.0 %reduce-scatter.19.cloned.1.call-start = ((), (), s32[]{:S(2)}) async-start(), calls=%async_computation.21 | async-start | bytes 1310720 | tf_op jit(solution)/shard_map/reduce_scatter | solution.py:98
  605.2 27.2 %copy-start.7 = (bf16[32,8,2,512]{3,1,2,0:T(8,128)(2,1)S(1)}, bf16[32,8,2,512]{3,1,2,0:T(8,128)(2,1)}, u32[]{:S(2)}) copy-start(bf16[32,8,2,512]{3,1,2,0:T(8,128)(2,1)} %copy-done.6) | copy-start | bytes 1572868
  636.8 231.0 %reduce-scatter.15.cloned.1.call-start = ((), (), s32[]{:S(2)}) async-start(), calls=%async_computation.19 | async-start | bytes 4718592 | tf_op jit(solution)/shard_map/reduce_scatter | solution.py:281
  637.5 1.3 copy-start.10
  638.8 3.8 copy-start.29
  660.0 1.3 copy-start.10
  661.3 4.8 copy-start.29
  689.5 7.3 copy-start.4
  692.1 12.7 %copy-start.5 = (f32[1024,1,256]{2,0,1:T(8,128)}, f32[1024,1,256]{2,0,1:T(8,128)S(1)}, u32[]{:S(2)}) copy-start(f32[1024,1,256]{2,0,1:T(8,128)S(1)} %copy.51) | copy-start | bytes 3145732
  704.5 226.9 %reduce-scatter.17.cloned.1.call-start = ((), (), s32[]{:S(2)}) async-start(), calls=%async_computation.20 | async-start | bytes 3932160 | tf_op jit(solution)/shard_map/reduce_scatter | solution.py:95
  714.9 152.9 %copy-start.14 = (f32[2048]{0:T(1024)S(1)}, f32[2048]{0:T(1024)}, u32[]{:S(2)}) copy-start(f32[2048]{0:T(1024)} %copy-done.13) | copy-start | bytes 24580
  714.9 152.9 %copy-start.16 = (f32[128]{0:T(128)S(1)}, f32[128]{0:T(128)}, u32[]{:S(2)}) copy-start(f32[128]{0:T(128)} %copy-done.15) | copy-start | bytes 1540
  714.9 152.9 %copy-start.18 = (f32[128]{0:T(128)S(1)}, f32[128]{0:T(128)}, u32[]{:S(2)}) copy-start(f32[128]{0:T(128)} %copy-done.17) | copy-start | bytes 1540
  788.3 145.7 %copy-start.3 = (f32[128,2048]{1,0:T(8,128)S(1)}, f32[128,2048]{1,0:T(8,128)}, u32[]{:S(2)}) copy-start(f32[128,2048]{1,0:T(8,128)} %get-tuple-element.285) | copy-start | bytes 3145732
Sparse Core Ops, SparseCore 0:
  9.6 66.1 all-gather.10
  78.2 35.2 all-gather.8
  115.1 27.9 all-gather.12
  147.9 50.5 reduce-scatter.8
  199.9 106.6 all-gather.16
  308.9 34.8 all-gather.14
  345.4 59.0 all-gather.18
  407.0 35.2 all-gather.20
  476.0 51.1 reduce-scatter.12
  530.4 51.1 reduce-scatter.10
  584.9 36.5 all-gather.22
  624.3 56.3 reduce-scatter.22
  682.9 102.0 reduce-scatter.20
  787.1 27.7 reduce-scatter.18
  818.2 49.6 reduce-scatter.14
  870.0 61.3 reduce-scatter.16
where the time goes:
time: 955 us; the launch traced here: 943 us
  waiting for transfers between devices  656 us (69%)
  matrix products  140 us (15%)
  other arithmetic  45.7 us (5%)
  blocking collectives  44.9 us (5%)
  local copies, waits for them, and re-layouts  41.2 us (4%)
  between operations  14.9 us (2%)
    all_gather x2, waiting for transfers between devices, gather_pair(): lax.all_gather(first, 'dp', axis=1, tiled=True)  160 us
    reduce_scatter x2, waiting for transfers between devices, shard_pair(): lax.psum_scatter(first.astype(jnp.bfloat16), 'dp', scatter_dimension=1, t...  87.2 us
    all_gather x2, waiting for transfers between devices, gather_pair(): lax.all_gather(second, 'dp', axis=1, tiled=True)  54.1 us
    reduce_scatter x1, waiting for transfers between devices, per_device(): lax.psum_scatter(down_term.astype(jnp.bfloat16), 'ctx', scatter_dimension...  52.8 us
    reduce_scatter x1, waiting for transfers between devices, per_device(): lax.psum_scatter(jnp.einsum('tkc,kdc->td', grad_parts_b, qkv_local, prefe...  51.1 us
    reduce_scatter x1, waiting for transfers between devices, per_device(): lax.psum_scatter(jnp.dot(attn_local, out_local, preferred_element_type=f3...  50 us
    psum x1, blocking collectives, per_device(): lax.psum((first_norm_scale_gradient, first_norm_bias_gradient, shift_grad...  44.9 us
    reduce_scatter x1, waiting for transfers between devices, per_device(): lax.psum_scatter(normed_two_term.astype(jnp.bfloat16), 'ctx', scatter_dim...  43.5 us
  transfers between devices with their start and end apart: 16, of which 15 were waited for; matrix products, arithmetic and copies ran while one was open for 19% of the time, Pallas kernels for 0%

commit v1 on v0

--- a/solution.py
+++ b/solution.py
@@ -1,9 +1,17 @@
+import functools
 import math
 
 import jax
 import jax.numpy as jnp
 from jax import lax
+from jax.experimental import pallas as pl
+from jax.experimental.pallas import tpu as pltpu
 from jax.sharding import PartitionSpec as P
+
+MESH = pl.DeviceIdType.MESH
+VMEM = pl.BlockSpec(memory_space=pltpu.VMEM)
+ANY = pl.BlockSpec(memory_space=pl.ANY)
+DMA = pltpu.SemaphoreType.DMA
 
 D = 2048
 HEADS = 32
@@ -16,25 +24,615 @@
 neg_big = -1e30
 
 
-def apply_layer_norm(values, gain_vec, bias_vec):
-    mean_val = jnp.mean(values, axis=-1, keepdims=True)
-    centred = values - mean_val
-    variance = jnp.mean(centred * centred, axis=-1, keepdims=True)
-    rscale = lax.rsqrt(variance + eps_norm)
-    normed = centred * rscale
-    return (normed * gain_vec + bias_vec, normed, rscale)
-
-
-def layer_norm_backward(grad_out, normed, rscale, gain_vec):
-    gain_grad = jnp.sum(grad_out * normed, axis=0)
-    bias_grad = jnp.sum(grad_out, axis=0)
-    scaled = grad_out * gain_vec
-    grad_in = rscale * (
+class Place:
+    def __init__(self):
+        self.ndp = lax.axis_size("dp")
+        self.nctx = lax.axis_size("ctx")
+        self.nchip = self.nctx // 2
+        self.z = lax.axis_index("dp")
+        self.c = lax.axis_index("ctx")
+        self.p = lax.div(self.c, 2)
+        self.k = lax.rem(self.c, 2)
+
+    def chip(self, offset):
+        return lax.rem(self.p + offset, self.nchip)
+
+    def at(self, c):
+        return {"dp": self.z, "ctx": c}
+
+    def partner(self):
+        return self.at(2 * self.p + 1 - self.k)
+
+    def same_core(self, q):
+        return self.at(2 * q + self.k)
+
+
+def greet(place, along_ctx=True, along_dp=False, all_ctx=False):
+    barrier = pltpu.get_barrier_semaphore()
+    peers = []
+    if all_ctx:
+        peers += [place.at(lax.rem(place.c + i, place.nctx)) for i in range(1, place.nctx)]
+    elif along_ctx:
+        peers += [place.partner()] + [place.same_core(place.chip(i)) for i in range(1, place.nchip)]
+    if along_dp:
+        peers += [{"dp": lax.rem(place.z + i, place.ndp), "ctx": place.c} for i in range(1, place.ndp)]
+    for peer in peers:
+        pl.semaphore_signal(barrier, inc=1, device_id=peer, device_id_type=MESH)
+    pl.semaphore_wait(barrier, len(peers))
+
+
+def push(src, dst, send, recv, device):
+    return pltpu.make_async_remote_copy(
+        src_ref=src, dst_ref=dst, send_sem=send, recv_sem=recv, device_id=device, device_id_type=MESH
+    )
+
+
+class RowGather:
+    def __init__(self, place, block, whole, send, recv, local):
+        self.place, self.block, self.whole = place, block, whole
+        self.send, self.recv, self.local = send, recv, local
+        self.rows = block.shape[0]
+
+    def slot(self, c):
+        return self.whole.at[pl.ds(pl.multiple_of(c * self.rows, self.rows), self.rows)]
+
+    def direct(self, i):
+        place = self.place
+        q = place.chip(i)
+        return push(self.block, self.slot(place.c), self.send.at[i], self.recv.at[place.c], place.same_core(q))
+
+    def own(self):
+        place = self.place
+        return push(self.block, self.slot(place.c), self.send.at[0], self.recv.at[place.c], place.partner())
+
+    def passed(self, i):
+        place = self.place
+        c = 2 * place.chip(i) + place.k
+        return push(
+            self.slot(c), self.slot(c), self.send.at[place.nchip + i - 1], self.recv.at[c], place.partner()
+        )
+
+    def arrival(self, c):
+        return push(self.block, self.slot(c), self.send.at[0], self.recv.at[c], self.place.partner())
+
+    def keep(self):
+        return pltpu.make_async_copy(self.block, self.slot(self.place.c), self.local)
+
+    def start(self):
+        for i in range(1, self.place.nchip):
+            self.direct(i).start()
+        self.own().start()
+        self.keep().start()
+
+    def forward(self):
+        place = self.place
+        for i in range(1, place.nchip):
+            self.arrival(2 * place.chip(i) + place.k).wait_recv()
+            self.passed(i).start()
+
+    def finish(self):
+        place = self.place
+        for i in range(place.nchip):
+            self.arrival(2 * place.chip(i) + 1 - place.k).wait_recv()
+        self.own().wait_send()
+        for i in range(1, place.nchip):
+            self.direct(i).wait_send()
+            self.passed(i).wait_send()
+        self.keep().wait()
+
+
+def gather_sems(nctx):
+    return [DMA((nctx,)), DMA((nctx,)), DMA]
+
+
+class DepthGather:
+    def __init__(self, place, piece, whole, where, send, recv, local):
+        self.place, self.piece, self.whole, self.where = place, piece, whole, where
+        self.send, self.recv, self.local = send, recv, local
+        self.line = place.ndp == 4
+        self.middle = jnp.logical_or(place.z == 1, place.z == 2)
+        self.far = 6 - 3 * place.z
+
+    def copy(self, src, z_src, z_dst, sem):
+        return push(
+            src, self.where(self.whole, z_src), self.send.at[sem], self.recv.at[z_src], {"dp": z_dst, "ctx": self.place.c}
+        )
+
+    def directs(self):
+        z, n = self.place.z, self.place.ndp
+        if not self.line:
+            return [(None, self.copy(self.piece, z, lax.rem(z + i, n), i - 1)) for i in range(1, n)]
+        out = []
+        for sem, step in enumerate((2, -2, 1, -1)):
+            d = z + step
+            ok = jnp.logical_and(d >= 0, d < 4)
+            out.append((ok, self.copy(self.piece, z, jnp.clip(d, 0, 3), sem)))
+        return out
+
+    def keep(self):
+        return pltpu.make_async_copy(self.piece, self.where(self.whole, self.place.z), self.local)
+
+    def start(self):
+        for ok, copy in self.directs():
+            if ok is None:
+                copy.start()
+            else:
+                pl.when(ok)(copy.start)
+        self.keep().start()
+
+    def passed(self):
+        far = jnp.clip(self.far, 0, 3)
+        return self.copy(self.where(self.whole, far), far, jnp.clip(3 * (self.place.z - 1), 0, 3), 4)
+
+    def forward(self):
+        if self.line:
+
+            @pl.when(self.middle)
+            def _():
+                far = jnp.clip(self.far, 0, 3)
+                self.copy(self.piece, far, far, 4).wait_recv()
+                self.passed().start()
+
+    def finish(self):
+        z, n = self.place.z, self.place.ndp
+        for i in range(1, n):
+            src = lax.rem(z + i, n)
+            wait = self.copy(self.piece, src, src, 0).wait_recv
+            if self.line:
+                pl.when(jnp.logical_not(jnp.logical_and(self.middle, src == self.far)))(wait)
+            else:
+                wait()
+        for ok, copy in self.directs():
+            if ok is None:
+                copy.wait_send()
+            else:
+                pl.when(ok)(copy.wait_send)
+        if self.line:
+            pl.when(self.middle)(self.passed().wait_send)
+        self.keep().wait()
+
+
+def depth_sems(ndp):
+    return [DMA((ndp + 1,)), DMA((ndp,)), DMA]
+
+
+STEP = 16
+
+
+def row_loop(rows, body):
+    def step(i, carry):
+        body(pl.ds(pl.multiple_of(i * STEP, STEP), STEP))
+        return carry
+
+    lax.fori_loop(0, rows // STEP, step, 0)
+
+
+def normal(values):
+    centred = values - jnp.mean(values, axis=-1, keepdims=True)
+    rscale = lax.rsqrt(jnp.mean(centred * centred, axis=-1, keepdims=True) + eps_norm)
+    return centred * rscale, rscale
+
+
+def normal_back(grad_out, normed, rscale, gain):
+    scaled = grad_out * gain
+    return rscale * (
         scaled
         - jnp.mean(scaled, axis=-1, keepdims=True)
         - normed * jnp.mean(scaled * normed, axis=-1, keepdims=True)
     )
-    return (grad_in, gain_grad, bias_grad)
+
+
+def gather_kernel(
+    x_ref, cot_ref, gain_ref, bias_ref, qkv_ref, out_ref,
+    rows_all, cot_all, qkv_all, out_all,
+    row_block, cot_block, *sems
+):
+    place = Place()
+    greet(place, along_dp=True)
+    depth = qkv_ref.shape[1]
+    width = out_ref.shape[1]
+
+    def qkv_at(ref, z):
+        return ref.at[:, pl.ds(pl.multiple_of(z * depth, depth), depth), :]
+
+    def out_at(ref, z):
+        return ref.at[:, pl.ds(pl.multiple_of(z * width, width), width)]
+
+    qkv = DepthGather(place, qkv_ref, qkv_all, qkv_at, *sems[0:3])
+    out = DepthGather(place, out_ref, out_all, out_at, *sems[3:6])
+    rows = RowGather(place, row_block, rows_all, *sems[6:9])
+    cots = RowGather(place, cot_block, cot_all, *sems[9:12])
+    qkv.start()
+    out.start()
+    gain, bias = gain_ref[...].astype(jnp.float32), bias_ref[...].astype(jnp.float32)
+
+    def norm(at):
+        normed, _ = normal(x_ref[at, :].astype(jnp.float32))
+        row_block[at, :] = (normed * gain + bias).astype(jnp.bfloat16)
+        cot_block[at, :] = cot_ref[at, :].astype(jnp.bfloat16)
+
+    row_loop(x_ref.shape[0], norm)
+    rows.start()
+    cots.start()
+    rows.forward()
+    cots.forward()
+    qkv.forward()
+    out.forward()
+    rows.finish()
+    cots.finish()
+    qkv.finish()
+    out.finish()
+
+
+def gather_inputs(x, cot, gain, bias, qkv, out):
+    ndp, nctx = lax.axis_size("dp"), lax.axis_size("ctx")
+    rows, d = x.shape
+    bf16 = jnp.bfloat16
+    return pl.pallas_call(
+        gather_kernel,
+        out_shape=(
+            jax.ShapeDtypeStruct((rows * nctx, d), bf16),
+            jax.ShapeDtypeStruct((rows * nctx, d), bf16),
+            jax.ShapeDtypeStruct((qkv.shape[0], qkv.shape[1] * ndp, qkv.shape[2]), bf16),
+            jax.ShapeDtypeStruct((out.shape[0], out.shape[1] * ndp), bf16),
+        ),
+        in_specs=[VMEM] * 6,
+        out_specs=(ANY,) * 4,
+        scratch_shapes=[pltpu.VMEM((rows, d), bf16), pltpu.VMEM((rows, d), bf16)]
+        + depth_sems(ndp) * 2
+        + gather_sems(nctx) * 2,
+        compiler_params=pltpu.CompilerParams(collective_id=0, has_side_effects=True),
+        cost_estimate=pl.CostEstimate(flops=0, bytes_accessed=200_000_000, transcendentals=0),
+        name="gather_inputs",
+    )(x, cot, gain[None, :], bias[None, :], qkv, out)
+
+
+class SumScatter:
+    TILE = 512
+
+    def __init__(self, place, rows, product, mine, to_pair, from_pair, to_chip, from_chip, sems):
+        self.place, self.rows, self.product = place, rows, product
+        self.mine, self.to_pair, self.from_pair = mine, to_pair, from_pair
+        self.to_chip, self.from_chip = to_chip, from_chip
+        self.pair_send, self.pair_recv, self.chip_send, self.chip_recv = sems
+
+    def pair(self, i):
+        return push(
+            self.to_pair.at[i], self.from_pair.at[i], self.pair_send.at[i], self.pair_recv.at[i], self.place.partner()
+        )
+
+    def chips(self, i):
+        return push(
+            self.to_chip.at[i],
+            self.from_chip.at[i],
+            self.chip_send.at[i],
+            self.chip_recv.at[i],
+            self.place.same_core(self.place.chip(i + 1)),
+        )
+
+    def run(self):
+        place, rows, tile = self.place, self.rows, self.TILE
+        nchip = place.nchip
+        width = self.mine.shape[-1]
+
+        def hand_on(i):
+            self.pair(i).wait_recv()
+
+            def add(at):
+                both = self.mine[i, at, :] + self.from_pair[i, at, :].astype(jnp.float32)
+                self.to_chip[i, at, :] = both.astype(jnp.bfloat16)
+
+            row_loop(rows, add)
+            self.chips(i).start()
+
+        def step(i, carry):
+            q = lax.rem(place.p + 1 + i, nchip)
+            first = pl.multiple_of(q * 2 * rows, 2 * rows)
+
+            def columns(j, inner):
+                cols = pl.ds(pl.multiple_of(j * tile, tile), tile)
+                part = self.product(pl.ds(first, 2 * rows), cols)
+
+                @pl.when(place.k == 0)
+                def _():
+                    self.mine[i, :, cols] = part[:rows]
+                    self.to_pair[i, :, cols] = part[rows:].astype(jnp.bfloat16)
+
+                @pl.when(place.k == 1)
+                def _():
+                    self.mine[i, :, cols] = part[rows:]
+                    self.to_pair[i, :, cols] = part[:rows].astype(jnp.bfloat16)
+
+                return inner
+
+            lax.fori_loop(0, width // tile, columns, 0)
+            self.pair(i).start()
+            pl.when(i > 0)(lambda: hand_on(i - 1))
+            return carry
+
+        lax.fori_loop(0, nchip, step, 0)
+        self.pair(nchip - 1).wait_recv()
+        for i in range(nchip - 1):
+            self.chips(i).wait_recv()
+
+    def total(self, at):
+        last = self.place.nchip - 1
+        value = self.mine[last, at, :] + self.from_pair[last, at, :].astype(jnp.float32)
+        for i in range(last):
+            value = value + self.from_chip[i, at, :].astype(jnp.float32)
+        return value
+
+    def finish(self):
+        for i in range(self.place.nchip):
+            self.pair(i).wait_send()
+        for i in range(self.place.nchip - 1):
+            self.chips(i).wait_send()
+
+
+def scatter_scratch(nctx, rows, d):
+    n = nctx // 2
+    bf16 = jnp.bfloat16
+    return [
+        pltpu.VMEM((n, rows, d), jnp.float32),
+        pltpu.VMEM((n, rows, d), bf16),
+        pltpu.VMEM((n, rows, d), bf16),
+        pltpu.VMEM((n - 1, rows, d), bf16),
+        pltpu.VMEM((n - 1, rows, d), bf16),
+        DMA((n,)),
+        DMA((n,)),
+        DMA((n - 1,)),
+        DMA((n - 1,)),
+    ]
+
+
+def dot_nn(a, b):
+    return jnp.dot(a, b, preferred_element_type=jnp.float32)
+
+
+def dot_nt(a, b):
+    return lax.dot_general(a, b, (((1,), (1,)), ((), ())), preferred_element_type=jnp.float32)
+
+
+def attn_out_kernel(attn_ref, w_ref, x_ref, gain_ref, bias_ref, resid_ref, normed_all, block, *scratch):
+    place = Place()
+    greet(place)
+    scatter = SumScatter(
+        place,
+        x_ref.shape[0],
+        lambda rows, cols: dot_nn(attn_ref[rows, :], w_ref[:, cols]),
+        *scratch[:5],
+        scratch[5:9],
+    )
+    scatter.run()
+    gain, bias = gain_ref[...].astype(jnp.float32), bias_ref[...].astype(jnp.float32)
+
+    def norm(at):
+        resid = x_ref[at, :].astype(jnp.float32) + scatter.total(at)
+        resid_ref[at, :] = resid
+        normed, _ = normal(resid)
+        block[at, :] = (normed * gain + bias).astype(jnp.bfloat16)
+
+    row_loop(x_ref.shape[0], norm)
+    rows = RowGather(place, block, normed_all, *scratch[9:12])
+    rows.start()
+    rows.forward()
+    rows.finish()
+    scatter.finish()
+
+
+def attn_out(attn, w, x, gain, bias):
+    nctx = lax.axis_size("ctx")
+    rows, d = x.shape
+    return pl.pallas_call(
+        attn_out_kernel,
+        out_shape=(
+            jax.ShapeDtypeStruct((rows, d), jnp.float32),
+            jax.ShapeDtypeStruct((rows * nctx, d), jnp.bfloat16),
+        ),
+        in_specs=[VMEM] * 5,
+        out_specs=(VMEM, ANY),
+        scratch_shapes=[pltpu.VMEM((rows, d), jnp.bfloat16)]
+        + scatter_scratch(nctx, rows, d)
+        + gather_sems(nctx),
+        compiler_params=pltpu.CompilerParams(collective_id=1, has_side_effects=True),
+        cost_estimate=pl.CostEstimate(flops=0, bytes_accessed=150_000_000, transcendentals=0),
+        name="attn_out",
+    )(attn, w, x, gain[None, :], bias[None, :])
+
+
+def mlp_back_kernel(
+    gate_ref, up_ref, w_ref, resid_ref, cot_ref, gain_ref, grad_ref, vec_ref, grad_all, block, *scratch
+):
+    place = Place()
+    greet(place)
+    scatter = SumScatter(
+        place,
+        resid_ref.shape[0],
+        lambda rows, cols: dot_nt(gate_ref[rows, :], w_ref[0, cols, :]) + dot_nt(up_ref[rows, :], w_ref[1, cols, :]),
+        *scratch[:5],
+        scratch[5:9],
+    )
+    scatter.run()
+    gain = gain_ref[...].astype(jnp.float32)
+    vec_ref[...] = jnp.zeros_like(vec_ref)
+
+    def back(at):
+        grad = scatter.total(at)
+        normed, rscale = normal(resid_ref[at, :])
+        vec_ref[0:1, :] += jnp.sum(grad * normed, axis=0, keepdims=True)
+        vec_ref[1:2, :] += jnp.sum(grad, axis=0, keepdims=True)
+        out = cot_ref[at, :] + normal_back(grad, normed, rscale, gain)
+        grad_ref[at, :] = out
+        block[at, :] = out.astype(jnp.bfloat16)
+
+    row_loop(resid_ref.shape[0], back)
+    rows = RowGather(place, block, grad_all, *scratch[9:12])
+    rows.start()
+    rows.forward()
+    rows.finish()
+    scatter.finish()
+
+
+def mlp_back(gate_grad, up_grad, w, resid, cot, gain):
+    nctx = lax.axis_size("ctx")
+    rows, d = resid.shape
+    return pl.pallas_call(
+        mlp_back_kernel,
+        out_shape=(
+            jax.ShapeDtypeStruct((rows, d), jnp.float32),
+            jax.ShapeDtypeStruct((2, d), jnp.float32),
+            jax.ShapeDtypeStruct((rows * nctx, d), jnp.bfloat16),
+        ),
+        in_specs=[VMEM] * 6,
+        out_specs=(VMEM, VMEM, ANY),
+        scratch_shapes=[pltpu.VMEM((rows, d), jnp.bfloat16)]
+        + scatter_scratch(nctx, rows, d)
+        + gather_sems(nctx),
+        compiler_params=pltpu.CompilerParams(collective_id=2, has_side_effects=True),
+        cost_estimate=pl.CostEstimate(flops=0, bytes_accessed=150_000_000, transcendentals=0),
+        name="mlp_back",
+    )(gate_grad, up_grad, w, resid, cot, gain[None, :])
+
+
+def attn_back_kernel(parts_ref, w_ref, x_ref, grad_ref, gain_ref, out_ref, vec_ref, *scratch):
+    place = Place()
+    greet(place)
+
+    def product(rows, cols):
+        part = dot_nt(parts_ref[0, rows, :], w_ref[0, cols, :])
+        part = part + dot_nt(parts_ref[1, rows, :], w_ref[1, cols, :])
+        return part + dot_nt(parts_ref[2, rows, :], w_ref[2, cols, :])
+
+    scatter = SumScatter(place, x_ref.shape[0], product, *scratch[:5], scratch[5:9])
+    scatter.run()
+    gain = gain_ref[...].astype(jnp.float32)
+    vec_ref[...] = jnp.zeros_like(vec_ref)
+
+    def back(at):
+        grad = scatter.total(at)
+        normed, rscale = normal(x_ref[at, :].astype(jnp.float32))
+        vec_ref[0:1, :] += jnp.sum(grad * normed, axis=0, keepdims=True)
+        vec_ref[1:2, :] += jnp.sum(grad, axis=0, keepdims=True)
+        out_ref[at, :] = grad_ref[at, :] + normal_back(grad, normed, rscale, gain)
+
+    row_loop(x_ref.shape[0], back)
+    scatter.finish()
+
+
+def attn_back(parts, w, x, grad, gain):
+    nctx = lax.axis_size("ctx")
+    rows, d = x.shape
+    return pl.pallas_call(
+        attn_back_kernel,
+        out_shape=(
+            jax.ShapeDtypeStruct((rows, d), jnp.float32),
+            jax.ShapeDtypeStruct((2, d), jnp.float32),
+        ),
+        in_specs=[VMEM] * 5,
+        out_specs=(VMEM, VMEM),
+        scratch_shapes=scatter_scratch(nctx, rows, d),
+        compiler_params=pltpu.CompilerParams(collective_id=3, has_side_effects=True),
+        cost_estimate=pl.CostEstimate(flops=0, bytes_accessed=100_000_000, transcendentals=0),
+        name="attn_back",
+    )(parts, w, x, grad, gain[None, :])
+
+
+def down_kernel(hidden_ref, w_ref, resid_ref, out_ref, *scratch):
+    place = Place()
+    greet(place)
+    scatter = SumScatter(
+        place,
+        resid_ref.shape[0],
+        lambda rows, cols: dot_nn(hidden_ref[rows, :], w_ref[:, cols]),
+        *scratch[:5],
+        scratch[5:9],
+    )
+    scatter.run()
+
+    def add(at):
+        out_ref[at, :] = (resid_ref[at, :] + scatter.total(at)).astype(jnp.bfloat16)
+
+    row_loop(resid_ref.shape[0], add)
+    scatter.finish()
+
+
+def down(hidden, w, resid):
+    nctx = lax.axis_size("ctx")
+    rows, d = resid.shape
+    return pl.pallas_call(
+        down_kernel,
+        out_shape=jax.ShapeDtypeStruct((rows, d), jnp.bfloat16),
+        in_specs=[VMEM] * 3,
+        out_specs=VMEM,
+        scratch_shapes=scatter_scratch(nctx, rows, d),
+        compiler_params=pltpu.CompilerParams(collective_id=4, has_side_effects=True),
+        cost_estimate=pl.CostEstimate(flops=0, bytes_accessed=100_000_000, transcendentals=0),
+        name="down_sum",
+    )(hidden, w, resid)
+
+
+def vectors_kernel(v_ref, out_ref, from_ctx, from_dp, plane, ctx_send, ctx_recv, dp_send, dp_recv):
+    place = Place()
+    greet(place, all_ctx=True, along_dp=True)
+    nctx, ndp, c, z = place.nctx, place.ndp, place.c, place.z
+
+    def across(i):
+        return push(
+            v_ref, from_ctx.at[c], ctx_send.at[i - 1], ctx_recv.at[c], place.at(lax.rem(c + i, nctx))
+        )
+
+    def along(i):
+        return push(
+            plane, from_dp.at[z], dp_send.at[i - 1], dp_recv.at[z], {"dp": lax.rem(z + i, ndp), "ctx": c}
+        )
+
+    for i in range(1, nctx):
+        across(i).start()
+    from_ctx[c] = v_ref[...]
+    for i in range(1, nctx):
+        s = lax.rem(c + i, nctx)
+        push(v_ref, from_ctx.at[s], ctx_send.at[0], ctx_recv.at[s], place.at(s)).wait_recv()
+    value = from_ctx[0]
+    for i in range(1, nctx):
+        value = value + from_ctx[i]
+    plane[...] = value
+    for i in range(1, ndp):
+        along(i).start()
+    from_dp[z] = value
+    for i in range(1, ndp):
+        s = lax.rem(z + i, ndp)
+        push(plane, from_dp.at[s], dp_send.at[0], dp_recv.at[s], {"dp": s, "ctx": c}).wait_recv()
+    value = from_dp[0]
+    for i in range(1, ndp):
+        value = value + from_dp[i]
+    out_ref[...] = value
+    for i in range(1, nctx):
+        across(i).wait_send()
+    for i in range(1, ndp):
+        along(i).wait_send()
+
+
+def sum_vectors(v):
+    ndp, nctx = lax.axis_size("dp"), lax.axis_size("ctx")
+    f32 = jnp.float32
+    return pl.pallas_call(
+        vectors_kernel,
+        out_shape=jax.ShapeDtypeStruct(v.shape, f32),
+        in_specs=[VMEM],
+        out_specs=VMEM,
+        scratch_shapes=[
+            pltpu.VMEM((nctx,) + v.shape, f32),
+            pltpu.VMEM((ndp,) + v.shape, f32),
+            pltpu.VMEM(v.shape, f32),
+            DMA((nctx - 1,)),
+            DMA((nctx,)),
+            DMA((ndp - 1,)),
+            DMA((ndp,)),
+        ],
+        compiler_params=pltpu.CompilerParams(collective_id=5, has_side_effects=True),
+        cost_estimate=pl.CostEstimate(flops=0, bytes_accessed=30_000_000, transcendentals=0),
+        name="sum_vectors",
+    )(v)
 
 
 def rope_tables(positions):
@@ -124,23 +722,12 @@
     half_group = tok_rows // 2
     group_order = group_perm[0]
     score_scale = 1.0 / math.sqrt(HEAD_DIM)
-    first_norm_scale = attn_norm_gain.astype(f32)
-    first_norm_bias = attn_norm_bias.astype(f32)
-    second_norm_scale = mlp_norm_gain.astype(f32)
-    second_norm_bias = mlp_norm_bias.astype(f32)
     qkv_shift = qkv_bias.astype(f32)
-    inputs_wide_float = block_input.astype(f32)
-    first_normalized_rows, first_centered_scaled, first_inverse_deviation = apply_layer_norm(
-        inputs_wide_float, first_norm_scale, first_norm_bias
-    )
-    normed_one_b = first_normalized_rows.astype(bf16)
-    cot_b = out_cotangent.astype(bf16)
-    rows_all, cot_all = (
-        lax.all_gather(normed_one_b, "ctx", axis=0, tiled=True),
-        lax.all_gather(cot_b, "ctx", axis=0, tiled=True),
-    )
-    attn_pair = gather_pair(qkv_weight, out_weight)
-    qkv_local, out_local = (attn_pair[0], attn_pair[1])
+    rows_all, cot_all, qkv_local, out_local = gather_inputs(
+        block_input, out_cotangent, attn_norm_gain, attn_norm_bias, qkv_weight, out_weight
+    )
+    gateup_weight, down_weight, rows_all = lax.optimization_barrier((gateup_weight, down_weight, rows_all))
+    gateup_local, down_local = gather_pair(gateup_weight, down_weight)
     all_pos = group_positions(group_order, seq_len, half_group)
     cos_all, sin_all = rope_tables(all_pos)
     local_heads = HEADS // cycle_size
@@ -173,53 +760,22 @@
 
     attn_blocks, lse_blocks = lax.map(forward_block, (query_blocks, pos_blocks))
     attn_local = attn_blocks.reshape(seq_len, width_local)
-    residual_stream = inputs_wide_float + lax.psum_scatter(
-        jnp.dot(attn_local, out_local, preferred_element_type=f32).astype(jnp.bfloat16),
-        "ctx",
-        scatter_dimension=0,
-        tiled=True,
-    ).astype(jnp.float32)
-    second_normalized_rows, second_centered_scaled, second_inverse_deviation = apply_layer_norm(
-        residual_stream, second_norm_scale, second_norm_bias
-    )
-    normed_two_b = second_normalized_rows.astype(bf16)
-    mlp_all = lax.all_gather(normed_two_b, "ctx", axis=0, tiled=True)
-    mlp_pair = gather_pair(gateup_weight, down_weight)
-    gateup_local, down_local = (mlp_pair[0], mlp_pair[1])
+    residual_stream, mlp_all = attn_out(attn_local, out_local, block_input, mlp_norm_gain, mlp_norm_bias)
     gate_val = jnp.dot(mlp_all, gateup_local[0], preferred_element_type=f32)
     up_val = jnp.dot(mlp_all, gateup_local[1], preferred_element_type=f32)
     sigma = jax.nn.sigmoid(gate_val)
     hidden_b = (gate_val * sigma * up_val).astype(bf16)
-    down_term = jnp.dot(hidden_b, down_local, preferred_element_type=f32)
     hidden_grad = jnp.dot(cot_all, down_local.T, preferred_element_type=f32)
     gate_grad = (hidden_grad * up_val * sigma * (1.0 + gate_val * (1.0 - sigma))).astype(bf16)
     up_grad = (hidden_grad * gate_val * sigma).astype(bf16)
-    normed_two_term = jnp.dot(gate_grad, gateup_local[0].T, preferred_element_type=f32) + jnp.dot(
-        up_grad, gateup_local[1].T, preferred_element_type=f32
-    )
-    down_sum, second_normalized_gradient = (
-        lax.psum_scatter(
-            down_term.astype(jnp.bfloat16), "ctx", scatter_dimension=0, tiled=True
-        ).astype(jnp.float32),
-        lax.psum_scatter(
-            normed_two_term.astype(jnp.bfloat16), "ctx", scatter_dimension=0, tiled=True
-        ).astype(jnp.float32),
-    )
-    block_output = (residual_stream + down_sum).astype(bf16)
     down_w_grad = jnp.dot(hidden_b.T, cot_all, preferred_element_type=f32)
     gateup_w_grad = jnp.einsum(
         "td,ktf->kdf", mlp_all, jnp.stack([gate_grad, up_grad]), preferred_element_type=f32
     )
     gateup_grads, down_grads = shard_pair(gateup_w_grad, down_w_grad)
-    residual_slice, second_norm_scale_gradient, second_norm_bias_gradient = layer_norm_backward(
-        second_normalized_gradient,
-        second_centered_scaled,
-        second_inverse_deviation,
-        second_norm_scale,
-    )
-    resid_grad = out_cotangent + residual_slice
-    resid_b = resid_grad.astype(bf16)
-    resid_all = lax.all_gather(resid_b, "ctx", axis=0, tiled=True)
+    resid_grad, second_vectors, resid_all = mlp_back(
+        gate_grad, up_grad, gateup_local, residual_stream, out_cotangent, mlp_norm_gain
+    )
     out_w_grad = jnp.dot(attn_local.T, resid_all, preferred_element_type=f32)
     attn_val_grad = jnp.dot(resid_all, out_local.T, preferred_element_type=f32).reshape(
         seq_len, local_heads, HEAD_DIM
@@ -272,34 +828,18 @@
             unrotate(key_grad, cos_all, sin_all).reshape(seq_len, width_local),
             value_grad.reshape(seq_len, width_local),
         ],
-        axis=1,
-    )
-    shift_part = jnp.sum(grad_parts, axis=0)
+        axis=0,
+    )
+    shift_part = jnp.sum(grad_parts, axis=1)
     shift_grad = lax.dynamic_update_slice_in_dim(jnp.zeros((3, D), f32), shift_part, head_first, 1)
     grad_parts_b = grad_parts.astype(bf16)
-    qkv_w_grad = jnp.einsum("td,tkc->kdc", rows_all, grad_parts_b, preferred_element_type=f32)
-    first_normalized_gradient = lax.psum_scatter(
-        jnp.einsum("tkc,kdc->td", grad_parts_b, qkv_local, preferred_element_type=f32).astype(
-            jnp.bfloat16
-        ),
-        "ctx",
-        scatter_dimension=0,
-        tiled=True,
-    ).astype(jnp.float32)
+    qkv_w_grad = jnp.einsum("td,ktc->kdc", rows_all, grad_parts_b, preferred_element_type=f32)
     qkv_grads, out_grads = shard_pair(qkv_w_grad, out_w_grad)
-    input_slice, first_norm_scale_gradient, first_norm_bias_gradient = layer_norm_backward(
-        first_normalized_gradient, first_centered_scaled, first_inverse_deviation, first_norm_scale
-    )
-    input_grad = resid_grad + input_slice
-    small = lax.psum(
-        (
-            first_norm_scale_gradient,
-            first_norm_bias_gradient,
-            shift_grad,
-            second_norm_scale_gradient,
-            second_norm_bias_gradient,
-        ),
-        ("dp", "ctx"),
+    input_grad, first_vectors = attn_back(grad_parts_b, qkv_local, block_input, resid_grad, attn_norm_gain)
+    hidden_late, first_vectors = lax.optimization_barrier((hidden_b, first_vectors))
+    block_output = down(hidden_late, down_local, residual_stream)
+    small = sum_vectors(
+        jnp.concatenate([first_vectors, second_vectors, shift_grad, jnp.zeros((1, D), f32)], axis=0)
     )
     return (
         block_output,
@@ -307,10 +847,10 @@
         small[0],
         small[1],
         qkv_grads,
+        small[4:7],
+        out_grads,
         small[2],
-        out_grads,
         small[3],
-        small[4],
         gateup_grads,
         down_grads,
     )

time: 955 us -> 632 us (0.66)
  waiting for transfers between devices: 656 us -> 127 us
  Pallas kernels: 0 us -> 309 us
  blocking collectives: 44.9 us -> 0 us
  matrix products: 140 us -> 95.9 us
  other arithmetic: 45.7 us -> 20.1 us
  local copies, waits for them, and re-layouts: 41.2 us -> 53.2 us
    pallas_call x0 -> x6, Pallas kernels: none -> 309 us  [the longest x1 84.9 us: gather_inputs(): pl.pallas_call(gather_kernel, out_shape=(jax.ShapeDtypeStruct((rows * nct...]
    reduce_scatter x4 -> x0, waiting for transfers between devices: 197 us -> none  [the longest x1 52.8 us: per_device(): lax.psum_scatter(down_term.astype(jnp.bfloat16), 'ctx', scatter_dimension...]
    all_gather x2 -> x1, waiting for transfers between devices: 160 us -> 20.8 us  [gather_pair(): lax.all_gather(first, 'dp', axis=1, tiled=True)]
    all_gather x4 -> x0, waiting for transfers between devices: 129 us -> none  [the longest x1 37.8 us: per_device(): lax.all_gather(normed_one_b, 'ctx', axis=0, tiled=True)]
    dot_general x6 -> x1, matrix products: 51.2 us -> 4.88 us  [per_device(): jnp.einsum('td,ktc->kdc', rows_all, grad_parts_b, preferred_element_type=...]
    psum x1 -> x0, blocking collectives: 44.9 us -> none  [per_device(): lax.psum((first_norm_scale_gradient, first_norm_bias_gradient, shift_grad...]
    reduce_scatter x2, waiting for transfers between devices: 87.2 us -> 60.4 us  [shard_pair(): lax.psum_scatter(first.astype(jnp.bfloat16), 'dp', scatter_dimension=1, t...]
    reduce_scatter x2, waiting for transfers between devices: 24.8 us -> 0.01 us  [shard_pair(): lax.psum_scatter(second.astype(jnp.bfloat16), 'dp', scatter_dimension=1,...]
  transfers between devices with their start and end apart: 16 -> 6, of which waited for: 15 -> 3; matrix products, arithmetic and copies ran while one was open for 19% -> 22% of each run, Pallas kernels for 0% -> 25%
where the time goes in v1:
time: 632 us; the launch traced here: 621 us
  Pallas kernels  309 us (49%)
  waiting for transfers between devices  127 us (20%)
  matrix products  95.9 us (15%)
  local copies, waits for them, and re-layouts  53.2 us (8%)
  other arithmetic  20.1 us (3%)
  between operations  14.8 us (2%)
    pallas_call x1, Pallas kernels, gather_inputs(): pl.pallas_call(gather_kernel, out_shape=(jax.ShapeDtypeStruct((rows * nct...  84.9 us
    pallas_call x1, Pallas kernels, mlp_back(): pl.pallas_call(mlp_back_kernel, out_shape=(jax.ShapeDtypeStruct((rows, d)...  69.1 us
    pallas_call x1, Pallas kernels, attn_out(): pl.pallas_call(attn_out_kernel, out_shape=(jax.ShapeDtypeStruct((rows, d)...  63.2 us
    reduce_scatter x2, waiting for transfers between devices, shard_pair(): lax.psum_scatter(first.astype(jnp.bfloat16), 'dp', scatter_dimension=1, t...  60.4 us
    all_gather x1, waiting for transfers between devices, gather_pair(): lax.all_gather(second, 'dp', axis=1, tiled=True)  45.5 us
    pallas_call x1, Pallas kernels, attn_back(): pl.pallas_call(attn_back_kernel, out_shape=(jax.ShapeDtypeStruct((rows, d...  36.6 us
    pallas_call x1, Pallas kernels, down(): pl.pallas_call(down_kernel, out_shape=jax.ShapeDtypeStruct((rows, d), jnp...  34.8 us
    dynamic_update_slice x4, local copies, waits for them, and re-layouts, per_device(): lax.scan(backward_block, (zero_kv, zero_kv), (query_blocks, pos_blocks, l...  21.9 us
  transfers between devices with their start and end apart: 6, of which 3 were waited for; matrix products, arithmetic and copies ran while one was open for 22% of the time, Pallas kernels for 25%

profile of v1, /device:TPU:0, one launch (start us, length us, event | category | flops | bytes accessed | tf_op | source)
XLA Modules:
  0.0 621.3 jit_solution(7716652781912942833)
XLA Ops:
  9.8 84.9 %gather_inputs.1 = (bf16[1024,2048]{1,0:T(8,128)(2,1)}, bf16[1024,2048]{1,0:T(8,128)(2,1)}, bf16[3,2048,256]{2,1,0:T(8,128)(2,1)}, bf16[256,2048]{1,0:T(8,128)(2,1)}) custom-call(bf16[128,2048]{1,0:T(8,128)(2,1)} %x_ref.5, f32[128,2048]{1,0:T(8,128)} %cot_ref.3, bf16[1,2048]{1,0:T(2,128)(2,1)} %broadcast_in_dim.107.gain_ref, ...), custom_call_target="tpu_custom_call" | custom-call | bytes 200000000 | tf_op jit(solution)/shard_map/gather_inputs/pallas_call | solution.py:271
  94.7 2.7 copy.71
  99.2 4.4 fusion.73
  107.2 16.8 %while.27 = (s32[]{:T(128)}, bf16[2,512,4,64]{1,3,2,0:T(8,128)(2,1)}, f32[2,4,512]{2,1,0:T(4,128)S(1)}, s32[1024]{0:T(1024)S(1)}, s32[2,512]{1,0:T(2,128)S(1)}, ...) while((s32[]{:T(128)}, ...), condition=%wide.region_4.5_spmd, body=%wide.region_1.4_spmd.sunk | while | flops 564918272 | bytes 35203272 | solution.py:761
  107.6 1.7 fusion.139
  109.3 2.9 fusion.140
  112.2 2.6 fusion.141
  116.0 1.7 fusion.139
  117.7 2.9 fusion.140
  120.6 2.6 fusion.141
  125.2 1.6 copy.69
  127.9 63.2 %attn_out.1 = (f32[128,2048]{1,0:T(8,128)}, bf16[1024,2048]{1,0:T(8,128)(2,1)}) custom-call(bf16[1024,256]{1,0:T(8,128)(2,1)} %copy.70.attn_ref, bf16[256,2048]{1,0:T(8,128)(2,1)} %get-tuple-element.138.w_ref, bf16[128,2048]{1,0:T(8,128)(2,1)} %x_ref.5, bf16[1,2048]{1,0:T(2,128)(2,1)} %broadcast_in_dim.109.gain_ref, bf16[1,2048]{1,0:T(2,128)(2,1)} %broadcast_in_dim.110.bias_ref), custom_call_target="tpu_custom_call" | custom-call | bytes 150000000 | tf_op jit(solution)/shard_map/attn_out/pallas_call | solution.py:426
  191.1 20.8 %all-gather.3.cloned.1.call-done.w_ref = bf16[2,2048,704]{2,1,0:T(8,128)(2,1)} async-done(((bf16[2,512,704]{2,1,0:T(8,128)(2,1)}), bf16[2,2048,704]{2,1,0:T(8,128)(2,1)}) %all-gather.3.cloned.1.call-update) | async-done | bytes 5767184 | tf_op jit(solution)/shard_map/all_gather | solution.py:686
  211.9 8.4 %fusion.63 = f32[1024,704]{1,0:T(8,128)} fusion(bf16[1024,2048]{1,0:T(8,128)(2,1)} %get-tuple-element.139, bf16[2,2048,704]{2,1,0:T(8,128)(2,1)} %all-gather.3.cloned.1.call-done.w_ref), kind=kOutput, calls=%fused_computation.61 | convolution fusion | flops 2952790016 | bytes 10223616 | tf_op jit(solution)/shard_map/dot_general | solution.py:765
  220.2 5.0 fusion.64
  225.3 45.5 %all-gather.5.cloned.1.call-done.w_ref = bf16[704,2048]{1,0:T(8,128)(2,1)} async-done(((bf16[704,512]{1,0:T(8,128)(2,1)}), bf16[704,2048]{1,0:T(8,128)(2,1)}) %all-gather.5.cloned.1.call-update) | async-done | bytes 2883600 | tf_op jit(solution)/shard_map/all_gather | solution.py:687
  270.8 11.5 %multiply_convert_fusion.1 = (bf16[1024,704]{1,0:T(8,128)(2,1)}, bf16[1024,704]{1,0:T(8,128)(2,1)}, bf16[1024,704]{1,0:T(8,128)(2,1)}) fusion(f32[1024,704]{1,0:T(8,128)} %fusion.64, f32[1024,704]{1,0:T(8,128)} %fusion.63, bf16[1024,2048]{1,0:T(8,128)(2,1)} %get-tuple-element.142, bf16[704,2048]{1,0:T(8,128)(2,1)} %all-gather.5.cloned.1.call-done.w_ref), kind=kOutput, calls=%fused_computation.68 | convolution fusion | flops 2964324352 | bytes 17170432 | tf_op jit(solution)/shard_map/dot_general | solution.py:768
  282.3 69.1 %mlp_back.1 = (f32[128,2048]{1,0:T(8,128)}, f32[2,2048]{1,0:T(2,128)}, bf16[1024,2048]{1,0:T(8,128)(2,1)}) custom-call(bf16[1024,704]{1,0:T(8,128)(2,1)} %get-tuple-element.306.gate_ref, bf16[1024,704]{1,0:T(8,128)(2,1)} %get-tuple-element.305.up_ref, bf16[2,2048,704]{2,1,0:T(8,128)(2,1)} %all-gather.3.cloned.1.call-done.w_ref, ...), custom_call_target="tpu_custom_call" | custom-call | bytes 150000000 | tf_op jit(solution)/shard_map/mlp_back/pallas_call | solution.py:479
  351.4 4.5 convolution_convert_fusion.1
  356.2 4.9 fusion.94
  361.2 2.2 convert_element_type.94
  363.4 1.9 copy.81
  365.3 7.5 %convolution_convert_fusion = bf16[704,2048]{1,0:T(8,128)(2,1)} fusion(bf16[1024,704]{1,0:T(8,128)(2,1)} %get-tuple-element.151.hidden_ref, bf16[1024,2048]{1,0:T(8,128)(2,1)} %get-tuple-element.142), kind=kOutput, calls=%fused_computation.59 | convolution fusion | flops 2954231808 | bytes 8519680 | tf_op jit(solution)/shard_map/dot_general | solution.py:771
  373.0 1.4 multiply_reduce_fusion
  374.4 46.0 %while.28 = (s32[]{:T(128)}, f32[1024,4,64]{0,2,1:T(8,128)S(1)}, f32[1024,4,64]{0,2,1:T(8,128)}, f32[2,512,4,64]{1,0,3,2:T(2,128)}, bf16[2,512,4,64]{1,3,2,0:T(8...) while((s32[]{:T(128)}, f32[1024,4,64]{0,2,1:T(8,128)S(1)}, ...), condition=%wide.region_7.8_spmd.clone, body=%wide.region_6.7_spmd.clone.sunk | while | flops 1369309184 | bytes 53020908 | solution.py:813
  376.2 3.7 fusion.154
  379.9 3.6 multiply_convert_fusion.5
  383.6 1.4 fusion.155
  386.5 10.4 %dynamic_update_slice.25 = f32[2,512,4,64]{1,0,3,2:T(2,128)} dynamic-update-slice(f32[2,512,4,64]{1,0,3,2:T(2,128)} %get-tuple-element.506, f32[1,512,4,64]{1,0,3,2:T(1,128)S(1)} %copy.105, s32[]{:T(128)S(6)} %copy.124, s32[]{:T(128)} %constant.91.clone.1..sunk, s32[]{:T(128)} %constant.91.clone.1..sunk, s32[]{:T(128)} %constant.91.clone.1..sunk) | dynamic-update-slice | bytes 1048580 | tf_op jit(solution)/shard_map/while/body/jit(dynamic_update_index_in_dim)/dynamic_update_slice | solution.py:813
  398.6 4.8 fusion.154
  403.4 3.6 multiply_convert_fusion.5
  407.1 1.4 fusion.155
  410.0 10.4 %dynamic_update_slice.25 = f32[2,512,4,64]{1,0,3,2:T(2,128)} dynamic-update-slice(f32[2,512,4,64]{1,0,3,2:T(2,128)} %get-tuple-element.506, f32[1,512,4,64]{1,0,3,2:T(1,128)S(1)} %copy.105, s32[]{:T(128)S(6)} %copy.124, s32[]{:T(128)} %constant.91.clone.1..sunk, s32[]{:T(128)} %constant.91.clone.1..sunk, s32[]{:T(128)} %constant.91.clone.1..sunk) | dynamic-update-slice | bytes 1048580 | tf_op jit(solution)/shard_map/while/body/jit(dynamic_update_index_in_dim)/dynamic_update_slice | solution.py:813
  420.4 2.1 reshape.236
  422.5 1.6 copy.85
  425.9 1.6 copy.84
  430.2 4.9 fusion.68
  435.4 10.6 %convert_bitcast_fusion = bf16[2,2048,704]{1,2,0:T(8,128)(2,1)} fusion(bf16[1024,2048]{1,0:T(8,128)(2,1)} %get-tuple-element.139, bf16[1,1024,704]{2,1,0:T(8,128)(2,1)} %bitcast.191, bf16[1,1024,704]{2,1,0:T(8,128)(2,1)} %bitcast.192), kind=kOutput, calls=%fused_computation.54 | convolution fusion | flops 5909905408 | bytes 12845056 | tf_op jit(solution)/shard_map/td,ktf->kdf/dot_general | solution.py:772
  446.1 36.6 %attn_back.1 = (f32[128,2048]{1,0:T(8,128)}, f32[2,2048]{1,0:T(2,128)}) custom-call(bf16[3,1024,256]{2,1,0:T(8,128)(2,1)} %copy-done.1, bf16[3,2048,256]{2,1,0:T(8,128)(2,1)} %get-tuple-element.136.w_ref, bf16[128,2048]{1,0:T(8,128)(2,1)} %x_ref.5, f32[128,2048]{1,0:T(8,128)} %get-tuple-element.149.grad_ref, bf16[1,2048]{1,0:T(2,128)(2,1)} %broadcast_in_dim.107.gain_ref), custom_call_target="tpu_custom_call" | custom-call | bytes 100000000 | tf_op jit(solution)/shard_map/attn_back/pallas_call | solution.py:525
  482.6 34.8 %down_sum.1 = bf16[128,2048]{1,0:T(8,128)(2,1)} custom-call(bf16[1024,704]{1,0:T(8,128)(2,1)} %get-tuple-element.151.hidden_ref, bf16[704,2048]{1,0:T(8,128)(2,1)} %all-gather.5.cloned.1.call-done.w_ref, f32[128,2048]{1,0:T(8,128)} %get-tuple-element.144.resid_ref), custom_call_target="tpu_custom_call" | custom-call | bytes 100000000 | tf_op jit(solution)/shard_map/down_sum/pallas_call | solution.py:562
  518.4 20.4 %sum_vectors.1 = f32[8,2048]{1,0:T(8,128)} custom-call(f32[8,2048]{1,0:T(8,128)} %maximum_maximum_fusion.v_ref), custom_call_target="tpu_custom_call" | custom-call | bytes 30000000 | tf_op jit(solution)/shard_map/sum_vectors/pallas_call | solution.py:618
  538.8 1.5 slice.99
  540.2 1.6 fusion.92
  541.9 1.8 convert_element_type.102
  543.7 2.5 convert_element_type.107
  546.1 2.6 copy.88
  548.8 60.4 %reduce-scatter.9.cloned.1.call-done = bf16[2,512,704]{1,2,0:T(8,128)(2,1)} async-done(((bf16[2,2048,704]{1,2,0:T(8,128)(2,1)}), bf16[2,512,704]{1,2,0:T(8,128)(2,1)}) %reduce-scatter.9.cloned.1.call-update) | async-done | bytes 1441808 | tf_op jit(solution)/shard_map/reduce_scatter | solution.py:693
  609.1 3.3 convert_element_type.105
  (135 shorter events, 26.8 us)
Async XLA Ops:
  7.2 91.8 %copy-start.17 = (s32[1,16]{1,0:T(1,128)S(1)}, s32[1,16]{1,0:T(1,128)}, u32[]{:S(2)}) copy-start(s32[1,16]{1,0:T(1,128)} %param.18) | copy-start | bytes 196
  7.2 204.7 %all-gather.3.cloned.1.call-start = ((), (), s32[]{:S(2)}) async-start(), calls=%async_computation.4 | async-start | bytes 7864320 | tf_op jit(solution)/shard_map/all_gather | solution.py:686
  94.7 4.4 copy-start.2
  97.5 173.3 %all-gather.5.cloned.1.call-start = ((), (), s32[]{:S(2)}) async-start(), calls=%async_computation.5 | async-start | bytes 3604480 | tf_op jit(solution)/shard_map/all_gather | solution.py:687
  98.2 443.6 %reduce-scatter.7.cloned.1.call-start = ((), (), s32[]{:S(2)}) async-start(), calls=%async_computation.7 | async-start | bytes 1310720 | tf_op jit(solution)/shard_map/reduce_scatter | solution.py:696
  99.2 4.4 copy-start.18
  106.5 0.6 copy-start.9
  106.5 0.6 copy-start.11
  107.2 16.8 %copy-start.15 = (bf16[2048]{0:T(1024)(128)(2,1)S(1)}, bf16[2048]{0:T(1024)(128)(2,1)}, u32[]{:S(2)}) copy-start(bf16[2048]{0:T(1024)(128)(2,1)} %param.24) | copy-start | bytes 12292
  107.2 17.4 %copy-start.16 = (bf16[2048]{0:T(1024)(128)(2,1)S(1)}, bf16[2048]{0:T(1024)(128)(2,1)}, u32[]{:S(2)}) copy-start(bf16[2048]{0:T(1024)(128)(2,1)} %param.25) | copy-start | bytes 12292
  109.3 2.9 copy-start.3
  109.3 2.9 copy-start.21
  114.8 0.8 copy-start.4
  117.7 2.9 copy-start.3
  117.7 2.9 copy-start.21
  123.2 0.8 copy-start.4
  211.9 8.4 %copy-start = (bf16[2,2048,704]{2,1,0:T(8,128)(2,1)S(1)}, bf16[2,2048,704]{2,1,0:T(8,128)(2,1)}, u32[]{:S(2)}) copy-start(bf16[2,2048,704]{2,1,0:T(8,128)(2,1)} %all-gather.3.cloned.1.call-done.w_ref) | copy-start | bytes 17301508
  211.9 8.4 %copy-start.20 = (bf16[1024,2048]{1,0:T(8,128)(2,1)S(1)}, bf16[1024,2048]{1,0:T(8,128)(2,1)}, u32[]{:S(2)}) copy-start(bf16[1024,2048]{1,0:T(8,128)(2,1)} %get-tuple-element.139) | copy-start | bytes 12582916
  351.4 4.6 copy-start.5
  355.9 187.7 %reduce-scatter.11.cloned.1.call-start = ((), (), s32[]{:S(2)}) async-start(), calls=%async_computation.9 | async-start | bytes 3604480 | tf_op jit(solution)/shard_map/reduce_scatter | solution.py:696
  372.8 173.4 %reduce-scatter.5.cloned.1.call-start = ((), (), s32[]{:S(2)}) async-start(), calls=%async_computation.6 | async-start | bytes 3932160 | tf_op jit(solution)/shard_map/reduce_scatter | solution.py:693
  374.9 1.3 copy-start.8
  376.2 3.7 copy-start.22
  397.3 1.3 copy-start.8
  398.6 4.8 copy-start.22
  420.4 3.9 copy-start.10
  420.4 3.9 copy-start.12
  427.5 2.8 copy-start.19
  427.8 1.2 copy-start.1
  435.1 174.0 %reduce-scatter.9.cloned.1.call-start = ((), (), s32[]{:S(2)}) async-start(), calls=%async_computation.8 | async-start | bytes 7208960 | tf_op jit(solution)/shard_map/reduce_scatter | solution.py:693
  482.6 35.0 %copy-start.13 = (f32[2,2048]{1,0:T(2,128)S(1)}, f32[2,2048]{1,0:T(2,128)}, u32[]{:S(2)}) copy-start(f32[2,2048]{1,0:T(2,128)} %get-tuple-element.154) | copy-start | bytes 49156
  482.6 35.0 %copy-start.14 = (f32[2,2048]{1,0:T(2,128)S(1)}, f32[2,2048]{1,0:T(2,128)}, u32[]{:S(2)}) copy-start(f32[2,2048]{1,0:T(2,128)} %get-tuple-element.153) | copy-start | bytes 49156
  543.7 68.8 %copy-start.6 = (bf16[128,2048]{1,0:T(8,128)(2,1)S(1)}, bf16[128,2048]{1,0:T(8,128)(2,1)}, u32[]{:S(2)}) copy-start(bf16[128,2048]{1,0:T(8,128)(2,1)} %down_sum.1) | copy-start | bytes 1572868
  546.1 67.2 %copy-start.7 = (f32[128,2048]{1,0:T(8,128)S(1)}, f32[128,2048]{1,0:T(8,128)}, u32[]{:S(2)}) copy-start(f32[128,2048]{1,0:T(8,128)} %get-tuple-element.543) | copy-start | bytes 3145732
Sparse Core Ops, SparseCore 0:
  97.6 114.2 all-gather.2
  213.4 57.2 all-gather.4
  356.0 24.5 reduce-scatter.6
  383.3 54.8 reduce-scatter.10
  440.4 60.1 reduce-scatter.4
  502.7 106.3 reduce-scatter.8

commit v2 on v1

--- a/solution.py
+++ b/solution.py
@@ -255,8 +255,8 @@
     rows.start()
     cots.start()
     rows.forward()
+    qkv.forward()
     cots.forward()
-    qkv.forward()
     out.forward()
     rows.finish()
     cots.finish()
@@ -635,42 +635,185 @@
     )(v)
 
 
+HALF = ROT // 2
+PAIR = 256
+
+
+def tiles(count, body):
+    def step(i, carry):
+        body(i)
+        return carry
+
+    lax.fori_loop(0, count, step, 0)
+
+
+def span(i, size):
+    return pl.ds(pl.multiple_of(i * size, size), size)
+
+
+def turn(columns, cosine, sine, heads):
+    out = []
+    for h in range(heads):
+        at = h * HEAD_DIM
+        a, b = columns[at : at + HALF], columns[at + HALF : at + ROT]
+        out += [a * cosine - b * sine, b * cosine + a * sine, columns[at + ROT : at + HEAD_DIM]]
+    return jnp.concatenate(out, axis=0)
+
+
+def attend(rows_ref, w_ref, shift_ref, cos_ref, sin_ref, pos_col, pos_row, q_t, k_t, v_t, attn_t, lse, k_n, bias, attn):
+    seq = rows_ref.shape[0]
+    width = w_ref.shape[2]
+    heads = width // HEAD_DIM
+    bf16 = jnp.bfloat16
+
+    def project(t):
+        at = span(t, PAIR)
+        cosine, sine = cos_ref[:, at], sin_ref[:, at]
+        for i, ref in enumerate((q_t, k_t, v_t)):
+            raw = (dot_nn(rows_ref[at, :], w_ref[i]) + shift_ref[i : i + 1, :]).T
+            if i < 2:
+                raw = turn(raw, cosine, sine, heads)
+            raw = raw.astype(bf16)
+            if i == 0:
+                raw = raw * jnp.asarray(1.0 / math.sqrt(HEAD_DIM), bf16)
+            ref[:, at] = raw
+
+    tiles(seq // PAIR, project)
+    for h in range(heads):
+        k_n[h] = k_t[h * HEAD_DIM : (h + 1) * HEAD_DIM, :].T
+
+    def queries(t):
+        at = span(t, PAIR)
+        bias[...] = jnp.where(pos_col[...] <= pos_row[:, at], 0.0, neg_big)
+
+        for h in range(heads):
+            feats = slice(h * HEAD_DIM, (h + 1) * HEAD_DIM)
+            scores = dot_nn(k_n[h], q_t[feats, at]) + bias[...]
+            peak = jnp.max(scores, axis=0, keepdims=True)
+            probs = jnp.exp(scores - peak)
+            total = jnp.sum(probs, axis=0, keepdims=True)
+            out = dot_nn(v_t[feats, :], probs.astype(bf16)) / total
+            attn_t[feats, at] = out.astype(bf16)
+            lse[h : h + 1, at] = peak + jnp.log(total)
+        attn[at, :] = attn_t[:, at].T
+
+    tiles(seq // PAIR, queries)
+
+
+def attend_kernel(rows_ref, w_ref, shift_ref, cos_ref, sin_ref, pos_col, pos_row, *rest):
+    attend(rows_ref, w_ref, shift_ref, cos_ref, sin_ref, pos_col, pos_row, *rest[:5], rest[6], rest[7], rest[5])
+
+
+def attention(rows_all, w, shift, cosine, sine, pos_col, pos_row):
+    seq, width = rows_all.shape[0], w.shape[2]
+    bf16 = jnp.bfloat16
+    heads = width // HEAD_DIM
+    return pl.pallas_call(
+        attend_kernel,
+        out_shape=tuple(jax.ShapeDtypeStruct((width, seq), bf16) for _ in range(4))
+        + (jax.ShapeDtypeStruct((8, seq), jnp.float32), jax.ShapeDtypeStruct((seq, width), bf16)),
+        in_specs=[VMEM] * 7,
+        out_specs=(VMEM,) * 6,
+        scratch_shapes=[pltpu.VMEM((heads, seq, HEAD_DIM), bf16), pltpu.VMEM((seq, PAIR), jnp.float32)],
+        cost_estimate=pl.CostEstimate(flops=0, bytes_accessed=40_000_000, transcendentals=0),
+        name="attention",
+    )(rows_all, w, shift, cosine, sine, pos_col, pos_row)
+
+
+def attend_back_kernel(
+    grad_ref, w_ref, rows_ref, cos_ref, sin_ref, pos_col, pos_row, q_t, k_t, v_t, attn_t, lse,
+    parts_ref, sums_ref, w_grads, g_t, delta, q_grad, kv_grad, bias, flat
+):
+    seq, d = grad_ref.shape
+    width = w_ref.shape[0]
+    heads = width // HEAD_DIM
+    bf16, f32 = jnp.bfloat16, jnp.float32
+
+    def first(t):
+        at = span(t, PAIR)
+        grad = dot_nt(w_ref[...], grad_ref[at, :])
+        both = grad * attn_t[:, at].astype(f32)
+        for h in range(heads):
+            delta[h : h + 1, at] = jnp.sum(both[h * HEAD_DIM : (h + 1) * HEAD_DIM], axis=0, keepdims=True)
+        g_t[:, at] = grad.astype(bf16)
+
+    tiles(seq // PAIR, first)
+    q_grad[...] = jnp.zeros_like(q_grad)
+
+    def keys(t):
+        at = span(t, PAIR)
+        bias[...] = jnp.where(pos_col[at, :] <= pos_row[...], 0.0, neg_big)
+        for h in range(heads):
+            feats = slice(h * HEAD_DIM, (h + 1) * HEAD_DIM)
+            keys_t = k_t[feats, at]
+            probs = jnp.exp(dot_nn(keys_t.T, q_t[feats, :]) + bias[...] - lse[h : h + 1, :])
+            kv_grad[1, feats, at] = dot_nt(g_t[feats, :], probs.astype(bf16))
+            back = dot_nn(v_t[feats, at].T, g_t[feats, :])
+            scores = (probs * (back - delta[h : h + 1, :])).astype(bf16)
+            kv_grad[0, feats, at] = dot_nt(q_t[feats, :], scores)
+            q_grad[feats, :] += dot_nn(keys_t, scores)
+
+    tiles(seq // PAIR, keys)
+    sums_ref[...] = jnp.zeros_like(sums_ref)
+
+    def part(t):
+        at = span(t, PAIR)
+        cosine, sine = cos_ref[:, at], sin_ref[:, at]
+        for i in range(3):
+            if i == 0:
+                grad = turn(q_grad[:, at] * (1.0 / math.sqrt(HEAD_DIM)), cosine, -sine, heads)
+            elif i == 1:
+                grad = turn(kv_grad[0, :, at], cosine, -sine, heads)
+            else:
+                grad = kv_grad[1, :, at]
+            natural = grad.T
+            sums_ref[i : i + 1, :] += jnp.sum(natural, axis=0, keepdims=True)
+            parts_ref[i, at, :] = natural.astype(bf16)
+            flat[i, :, at] = grad.astype(bf16)
+
+    tiles(seq // PAIR, part)
+
+    def weights(j):
+        cols = span(j, 2 * PAIR)
+        rows = rows_ref[:, cols]
+        for i in range(3):
+            w_grads[i, cols, :] = dot_nn(flat[i], rows).T.astype(bf16)
+        w_grads[3, cols, :] = dot_nn(attn_t[...], grad_ref[:, cols]).T.astype(bf16)
+
+    tiles(d // (2 * PAIR), weights)
+
+
+def attention_back(grad_all, w, rows_all, cosine, sine, pos_col, pos_row, q_t, k_t, v_t, attn_t, lse):
+    seq, d = rows_all.shape
+    width = w.shape[0]
+    bf16, f32 = jnp.bfloat16, jnp.float32
+    return pl.pallas_call(
+        attend_back_kernel,
+        out_shape=(
+            jax.ShapeDtypeStruct((3, seq, width), bf16),
+            jax.ShapeDtypeStruct((3, width), f32),
+            jax.ShapeDtypeStruct((4, d, width), bf16),
+        ),
+        in_specs=[VMEM] * 12,
+        out_specs=(VMEM,) * 3,
+        scratch_shapes=[
+            pltpu.VMEM((width, seq), bf16),
+            pltpu.VMEM((8, seq), f32),
+            pltpu.VMEM((width, seq), f32),
+            pltpu.VMEM((2, width, seq), f32),
+            pltpu.VMEM((PAIR, seq), f32),
+            pltpu.VMEM((3, width, seq), bf16),
+        ],
+        cost_estimate=pl.CostEstimate(flops=0, bytes_accessed=120_000_000, transcendentals=0),
+        name="attention_back",
+    )(grad_all, w, rows_all, cosine, sine, pos_col, pos_row, q_t, k_t, v_t, attn_t, lse)
+
+
 def rope_tables(positions):
-    half_rot = ROT // 2
-    exponent = jnp.arange(half_rot, dtype=jnp.float32) * (2.0 / ROT)
+    exponent = jnp.arange(HALF, dtype=jnp.float32) * (2.0 / ROT)
     inverse = jnp.exp(-exponent * math.log(rope_base))
-    angle_val = positions.astype(jnp.float32)[:, None] * inverse[None, :]
-    return (jnp.cos(angle_val)[:, None, :], jnp.sin(angle_val)[:, None, :])
-
-
-def rotate(tensor, cosine, sine_val):
-    half_rot = ROT // 2
-    first_half = tensor[..., :half_rot]
-    second = tensor[..., half_rot:ROT]
-    remainder = tensor[..., ROT:]
-    return jnp.concatenate(
-        [
-            first_half * cosine - second * sine_val,
-            second * cosine + first_half * sine_val,
-            remainder,
-        ],
-        axis=-1,
-    )
-
-
-def unrotate(tensor, cosine, sine_val):
-    half_rot = ROT // 2
-    first_half = tensor[..., :half_rot]
-    second = tensor[..., half_rot:ROT]
-    remainder = tensor[..., ROT:]
-    return jnp.concatenate(
-        [
-            first_half * cosine + second * sine_val,
-            second * cosine - first_half * sine_val,
-            remainder,
-        ],
-        axis=-1,
-    )
+    angle_val = inverse[:, None] * positions.astype(jnp.float32)[None, :]
+    return (jnp.cos(angle_val), jnp.sin(angle_val))
 
 
 def group_positions(group_order, count, half_group):
@@ -681,22 +824,8 @@
     return group_start * half_group + row_ids % half_group
 
 
-def gather_pair(first, second):
-    return (
-        lax.all_gather(first, "dp", axis=1, tiled=True),
-        lax.all_gather(second, "dp", axis=1, tiled=True),
-    )
-
-
-def shard_pair(first, second):
-    return (
-        lax.psum_scatter(first.astype(jnp.bfloat16), "dp", scatter_dimension=1, tiled=True).astype(
-            jnp.float32
-        ),
-        lax.psum_scatter(second.astype(jnp.bfloat16), "dp", scatter_dimension=1, tiled=True).astype(
-            jnp.float32
-        ),
-    )
+def shard(grad):
+    return lax.psum_scatter(grad, "dp", scatter_dimension=1, tiled=True)
 
 
 def per_device(
@@ -721,122 +850,50 @@
     seq_len = tok_rows * cycle_size
     half_group = tok_rows // 2
     group_order = group_perm[0]
-    score_scale = 1.0 / math.sqrt(HEAD_DIM)
     qkv_shift = qkv_bias.astype(f32)
     rows_all, cot_all, qkv_local, out_local = gather_inputs(
         block_input, out_cotangent, attn_norm_gain, attn_norm_bias, qkv_weight, out_weight
     )
-    gateup_weight, down_weight, rows_all = lax.optimization_barrier((gateup_weight, down_weight, rows_all))
-    gateup_local, down_local = gather_pair(gateup_weight, down_weight)
+    down_local = lax.all_gather(down_weight, "dp", axis=1, tiled=True)
+    gateup_local = lax.all_gather(gateup_weight, "dp", axis=1, tiled=True)
     all_pos = group_positions(group_order, seq_len, half_group)
     cos_all, sin_all = rope_tables(all_pos)
-    local_heads = HEADS // cycle_size
-    width_local = local_heads * HEAD_DIM
+    pos_f = all_pos.astype(f32)
+    pos_col, pos_row = pos_f[:, None], pos_f[None, :]
+    width_local = qkv_weight.shape[2]
     head_first = cycle_index * width_local
     shift_local = lax.dynamic_slice_in_dim(qkv_shift, head_first, width_local, 1)
-    query_raw = jnp.dot(rows_all, qkv_local[0], preferred_element_type=f32) + shift_local[0]
-    key_raw = jnp.dot(rows_all, qkv_local[1], preferred_element_type=f32) + shift_local[1]
-    value_raw = jnp.dot(rows_all, qkv_local[2], preferred_element_type=f32) + shift_local[2]
-    query = rotate(query_raw.reshape(seq_len, local_heads, HEAD_DIM), cos_all, sin_all).astype(bf16)
-    keys_b = rotate(key_raw.reshape(seq_len, local_heads, HEAD_DIM), cos_all, sin_all).astype(bf16)
-    values_b = value_raw.reshape(seq_len, local_heads, HEAD_DIM).astype(bf16)
-    query_block = min(512, seq_len)
-    block_count = seq_len // query_block
-    query_blocks = query.reshape(block_count, query_block, local_heads, HEAD_DIM)
-    pos_blocks = all_pos.reshape(block_count, query_block)
-
-    def forward_block(inputs):
-        query_blk, pos_blk = inputs
-        scores = (
-            jnp.einsum("rhd,nhd->hrn", query_blk, keys_b, preferred_element_type=f32) * score_scale
-        )
-        visible = all_pos[None, None, :] <= pos_blk[None, :, None]
-        scores = jnp.where(visible, scores, neg_big)
-        peak = jnp.max(scores, axis=-1)
-        probs = jnp.where(visible, jnp.exp(scores - peak[..., None]), 0.0)
-        total = jnp.sum(probs, axis=-1)
-        accum = jnp.einsum("hrn,nhd->rhd", probs.astype(bf16), values_b, preferred_element_type=f32)
-        return ((accum / total.T[:, :, None]).astype(bf16), peak + jnp.log(total))
-
-    attn_blocks, lse_blocks = lax.map(forward_block, (query_blocks, pos_blocks))
-    attn_local = attn_blocks.reshape(seq_len, width_local)
+    q_t, k_t, v_t, attn_t, lse, attn_local = attention(
+        rows_all, qkv_local, shift_local, cos_all, sin_all, pos_col, pos_row
+    )
+    attn_local, down_local = lax.optimization_barrier((attn_local, down_local))
     residual_stream, mlp_all = attn_out(attn_local, out_local, block_input, mlp_norm_gain, mlp_norm_bias)
     gate_val = jnp.dot(mlp_all, gateup_local[0], preferred_element_type=f32)
     up_val = jnp.dot(mlp_all, gateup_local[1], preferred_element_type=f32)
     sigma = jax.nn.sigmoid(gate_val)
     hidden_b = (gate_val * sigma * up_val).astype(bf16)
+    down_w_grad = jnp.dot(hidden_b.T, cot_all, preferred_element_type=f32).astype(bf16)
+    down_local, down_w_grad = lax.optimization_barrier((down_local, down_w_grad))
+    down_grads = shard(down_w_grad)
     hidden_grad = jnp.dot(cot_all, down_local.T, preferred_element_type=f32)
     gate_grad = (hidden_grad * up_val * sigma * (1.0 + gate_val * (1.0 - sigma))).astype(bf16)
     up_grad = (hidden_grad * gate_val * sigma).astype(bf16)
-    down_w_grad = jnp.dot(hidden_b.T, cot_all, preferred_element_type=f32)
     gateup_w_grad = jnp.einsum(
         "td,ktf->kdf", mlp_all, jnp.stack([gate_grad, up_grad]), preferred_element_type=f32
-    )
-    gateup_grads, down_grads = shard_pair(gateup_w_grad, down_w_grad)
+    ).astype(bf16)
+    gate_grad, up_grad, gateup_w_grad = lax.optimization_barrier((gate_grad, up_grad, gateup_w_grad))
+    gateup_grads = shard(gateup_w_grad)
     resid_grad, second_vectors, resid_all = mlp_back(
         gate_grad, up_grad, gateup_local, residual_stream, out_cotangent, mlp_norm_gain
     )
-    out_w_grad = jnp.dot(attn_local.T, resid_all, preferred_element_type=f32)
-    attn_val_grad = jnp.dot(resid_all, out_local.T, preferred_element_type=f32).reshape(
-        seq_len, local_heads, HEAD_DIM
-    )
-    delta = jnp.sum(
-        attn_val_grad * attn_local.reshape(seq_len, local_heads, HEAD_DIM).astype(f32), axis=-1
-    )
-    attn_grad_b = attn_val_grad.astype(bf16)
-
-    def backward_block(carry, inputs):
-        key_grad, value_grad = carry
-        query_blk, pos_blk, lse_blk, grad_blk, delta_blk = inputs
-        scores = (
-            jnp.einsum("rhd,nhd->hrn", query_blk, keys_b, preferred_element_type=f32) * score_scale
-        )
-        visible = all_pos[None, None, :] <= pos_blk[None, :, None]
-        scores = jnp.where(visible, scores, neg_big)
-        probs = jnp.where(visible, jnp.exp(scores - lse_blk[..., None]), 0.0)
-        value_grad = value_grad + jnp.einsum(
-            "hrn,rhd->nhd", probs.astype(bf16), grad_blk, preferred_element_type=f32
-        )
-        prob_grad = jnp.einsum("rhd,nhd->hrn", grad_blk, values_b, preferred_element_type=f32)
-        score_grad = (probs * (prob_grad - delta_blk.T[:, :, None])).astype(bf16)
-        query_grad_blk = (
-            jnp.einsum("hrn,nhd->rhd", score_grad, keys_b, preferred_element_type=f32) * score_scale
-        )
-        key_grad = (
-            key_grad
-            + jnp.einsum("hrn,rhd->nhd", score_grad, query_blk, preferred_element_type=f32)
-            * score_scale
-        )
-        return ((key_grad, value_grad), query_grad_blk)
-
-    zero_kv = jnp.zeros((seq_len, local_heads, HEAD_DIM), f32)
-    (key_grad, value_grad), query_grads = lax.scan(
-        backward_block,
-        (zero_kv, zero_kv),
-        (
-            query_blocks,
-            pos_blocks,
-            lse_blocks,
-            attn_grad_b.reshape(block_count, query_block, local_heads, HEAD_DIM),
-            delta.reshape(block_count, query_block, local_heads),
-        ),
-    )
-    query_grad = query_grads.reshape(seq_len, local_heads, HEAD_DIM)
-    grad_parts = jnp.stack(
-        [
-            unrotate(query_grad, cos_all, sin_all).reshape(seq_len, width_local),
-            unrotate(key_grad, cos_all, sin_all).reshape(seq_len, width_local),
-            value_grad.reshape(seq_len, width_local),
-        ],
-        axis=0,
-    )
-    shift_part = jnp.sum(grad_parts, axis=1)
+    resid_all, down_grads = lax.optimization_barrier((resid_all, down_grads))
+    grad_parts_b, shift_part, attn_grads = attention_back(
+        resid_all, out_local, rows_all, cos_all, sin_all, pos_col, pos_row, q_t, k_t, v_t, attn_t, lse
+    )
     shift_grad = lax.dynamic_update_slice_in_dim(jnp.zeros((3, D), f32), shift_part, head_first, 1)
-    grad_parts_b = grad_parts.astype(bf16)
-    qkv_w_grad = jnp.einsum("td,ktc->kdc", rows_all, grad_parts_b, preferred_element_type=f32)
-    qkv_grads, out_grads = shard_pair(qkv_w_grad, out_w_grad)
+    attn_grads = shard(attn_grads).astype(f32)
     input_grad, first_vectors = attn_back(grad_parts_b, qkv_local, block_input, resid_grad, attn_norm_gain)
-    hidden_late, first_vectors = lax.optimization_barrier((hidden_b, first_vectors))
+    hidden_late, first_vectors, gateup_grads = lax.optimization_barrier((hidden_b, first_vectors, gateup_grads))
     block_output = down(hidden_late, down_local, residual_stream)
     small = sum_vectors(
         jnp.concatenate([first_vectors, second_vectors, shift_grad, jnp.zeros((1, D), f32)], axis=0)
@@ -846,13 +903,13 @@
         input_grad,
         small[0],
         small[1],
-        qkv_grads,
+        attn_grads[:3],
         small[4:7],
-        out_grads,
+        attn_grads[3].T,
         small[2],
         small[3],
-        gateup_grads,
-        down_grads,
+        gateup_grads.astype(f32),
+        down_grads.astype(f32),
     )
 
 

time: 632 us -> 519 us (0.82); the launches traced: 621 us -> 519 us
  Pallas kernels: 309 us -> 403 us
  waiting for transfers between devices: 127 us -> 43.5 us
  matrix products: 95.9 us -> 33.2 us
  local copies, waits for them, and re-layouts: 53.2 us -> 14.4 us
  other arithmetic: 20.1 us -> 10.5 us
    all_gather x2, waiting for transfers between devices: 66.3 us -> 6.91 us  [the longest x1 6.91 us: per_device(): gateup_local = lax.all_gather(gateup_weight, 'dp', axis=1, tiled=True)]
    dot_general x21 -> x1, matrix products: 60.4 us -> 4.5 us  [per_device(): jnp.dot(hidden_b.T, cot_all, preferred_element_type=f32).astype(bf16)]
    pallas_call x0 -> x2, Pallas kernels: none -> 46.8 us  [the longest x1 26.5 us: attention_back(): pl.pallas_call(attend_back_kernel, out_shape=(jax.ShapeDtypeStruct((3, se...]
    pallas_call x1, Pallas kernels: 84.9 us -> 130 us  [gather_inputs(): pl.pallas_call(gather_kernel, out_shape=(jax.ShapeDtypeStruct((rows * nct...]
    reduce_scatter x4 -> x3, waiting for transfers between devices: 60.4 us -> 35.9 us  [shard(): return lax.psum_scatter(grad, 'dp', scatter_dimension=1, tiled=True)]
    dynamic_update_slice x4 -> x0, local copies, waits for them, and re-layouts: 21.9 us -> none  [per_device(): lax.scan(backward_block, (zero_kv, zero_kv), (query_blocks, pos_blocks, l...]
    reduce_sum x4 -> x0, other arithmetic: 7.48 us -> none  [the longest x2 5.82 us: forward_block(): total = jnp.sum(probs, axis=-1)]
  transfers between devices with their start and end apart: 6 -> 5, of which waited for: 3 -> 3; matrix products, arithmetic and copies ran while one was open for 22% -> 6% of each run, Pallas kernels for 25% -> 78%
where the time goes in v2:
time: 519 us
  Pallas kernels  403 us (78%)
  waiting for transfers between devices  43.5 us (8%)
  matrix products  33.2 us (6%)
  local copies, waits for them, and re-layouts  14.4 us (3%)
  between operations  14.1 us (3%)
  other arithmetic  10.5 us (2%)
    pallas_call x1, Pallas kernels, gather_inputs(): pl.pallas_call(gather_kernel, out_shape=(jax.ShapeDtypeStruct((rows * nct...  130 us
    pallas_call x1, Pallas kernels, mlp_back(): pl.pallas_call(mlp_back_kernel, out_shape=(jax.ShapeDtypeStruct((rows, d)...  68.7 us
    pallas_call x1, Pallas kernels, attn_out(): pl.pallas_call(attn_out_kernel, out_shape=(jax.ShapeDtypeStruct((rows, d)...  63.6 us
    pallas_call x1, Pallas kernels, attn_back(): pl.pallas_call(attn_back_kernel, out_shape=(jax.ShapeDtypeStruct((rows, d...  36.5 us
    reduce_scatter x3, waiting for transfers between devices, shard(): return lax.psum_scatter(grad, 'dp', scatter_dimension=1, tiled=True)  35.9 us
    pallas_call x1, Pallas kernels, down(): pl.pallas_call(down_kernel, out_shape=jax.ShapeDtypeStruct((rows, d), jnp...  33.8 us
    pallas_call x1, Pallas kernels, attention_back(): pl.pallas_call(attend_back_kernel, out_shape=(jax.ShapeDtypeStruct((3, se...  26.5 us
    pallas_call x1, Pallas kernels, sum_vectors(): pl.pallas_call(vectors_kernel, out_shape=jax.ShapeDtypeStruct(v.shape, f3...  23.3 us
  transfers between devices with their start and end apart: 5, of which 3 were waited for; matrix products, arithmetic and copies ran while one was open for 6% of the time, Pallas kernels for 78%

profile of v2, /device:TPU:0, one launch (start us, length us, event | category | flops | bytes accessed | tf_op | source)
XLA Modules:
  0.0 518.9 jit_solution(6714752345454183967)
XLA Ops:
  7.2 0.0 all-gather.3.cloned.1.call-start
  7.3 0.7 all-gather.3.cloned.1.call-update
  8.0 0.0 all-gather.5.cloned.1.call-start
  8.0 2.6 copy.47
  10.6 0.0 reduce-scatter.4.cloned.1.call-start
  10.7 0.6 broadcast_in_dim.40.gain_ref
  11.3 0.6 broadcast_in_dim.41.bias_ref
  11.9 0.1 select_reduce_fusion
  12.0 0.2 copy.46
  12.2 0.6 broadcast_in_dim.45.gain_ref
  12.8 0.6 broadcast_in_dim.46.bias_ref
  13.4 129.9 %gather_inputs.1 = (bf16[1024,2048]{1,0:T(8,128)(2,1)}, bf16[1024,2048]{1,0:T(8,128)(2,1)}, bf16[3,2048,256]{2,1,0:T(8,128)(2,1)}, bf16[256,2048]{1,0:T(8,128)(2,1)}) custom-call(bf16[128,2048]{1,0:T(8,128)(2,1)} %x_ref.5, f32[128,2048]{1,0:T(8,128)} %cot_ref.3, bf16[1,2048]{1,0:T(2,128)(2,1)} %broadcast_in_dim.40.gain_ref, ...), custom_call_target="tpu_custom_call" | custom-call | bytes 200000000 | tf_op jit(solution)/shard_map/gather_inputs/pallas_call | solution.py:271
  143.3 1.3 dynamic-slice_convert_fusion.shift_ref
  144.6 0.6 fusion.21.pos_row
  145.2 0.8 multiply_sine_fusion
  146.0 0.9 fusion.7.pos_col
  146.9 20.3 %attention.1 = (bf16[256,1024]{1,0:T(8,128)(2,1)}, bf16[256,1024]{1,0:T(8,128)(2,1)}, bf16[256,1024]{1,0:T(8,128)(2,1)}, bf16[256,1024]{1,0:T(8,128)(2,1)}, f32[...) custom-call(bf16[1024,2048]{1,0:T(8,128)(2,1)} %get-tuple-element.43.rows_ref, bf16[3,2048,256]{2,1,0:T(8,128)(2,1)} %get-tuple-element.44.w_ref, ...), custom_call_target="tpu_custom_call" | custom-call | bytes 40000000 | tf_op jit(solution)/shard_map/attention/pallas_call | solution.py:711
  167.2 63.6 %attn_out.1 = (f32[128,2048]{1,0:T(8,128)}, bf16[1024,2048]{1,0:T(8,128)(2,1)}) custom-call(bf16[1024,256]{1,0:T(8,128)(2,1)} %get-tuple-element.46.attn_ref, bf16[256,2048]{1,0:T(8,128)(2,1)} %get-tuple-element.47.w_ref, bf16[128,2048]{1,0:T(8,128)(2,1)} %x_ref.5, bf16[1,2048]{1,0:T(2,128)(2,1)} %broadcast_in_dim.45.gain_ref, ...), custom_call_target="tpu_custom_call" | custom-call | bytes 150000000 | tf_op jit(solution)/shard_map/attn_out/pallas_call | solution.py:426
  230.8 6.9 %all-gather.5.cloned.1.call-done.w_ref = bf16[2,2048,704]{2,1,0:T(8,128)(2,1)} async-done(((bf16[2,512,704]{2,1,0:T(8,128)(2,1)}), bf16[2,2048,704]{2,1,0:T(8,128)(2,1)}) %all-gather.5.cloned.1.call-update) | async-done | bytes 5767184 | tf_op jit(solution)/shard_map/all_gather | solution.py:858
  237.7 6.6 %fusion.2 = f32[1024,704]{1,0:T(8,128)S(1)} fusion(bf16[1024,2048]{1,0:T(8,128)(2,1)} %get-tuple-element.48, bf16[2,2048,704]{2,1,0:T(8,128)(2,1)} %all-gather.5.cloned.1.call-done.w_ref), kind=kOutput, calls=%fused_computation.6 | convolution fusion | flops 2952790016 | bytes 10223616 | tf_op jit(solution)/shard_map/dot_general | solution.py:871
  244.3 5.3 %multiply_convert_fusion.2 = (bf16[1024,704]{1,0:T(8,128)(2,1)S(1)}, f32[1024,704]{1,0:T(8,128)}) fusion(f32[1024,704]{1,0:T(8,128)S(1)} %fusion.2, bf16[1024,2048]{1,0:T(8,128)(2,1)S(1)} %copy-done.19, bf16[2,2048,704]{2,1,0:T(8,128)(2,1)S(1)} %copy-done.1), kind=kOutput, calls=%fused_computation.12 | convolution fusion | flops 2957115392 | bytes 14811136 | tf_op jit(solution)/shard_map/dot_general | solution.py:872
  249.6 1.1 copy-done.6
  250.8 4.5 convolution_convert_fusion
  255.3 0.2 reduce-scatter.6.cloned.1.call-start
  255.6 8.3 %multiply_convert_fusion = (bf16[1024,704]{1,0:T(8,128)(2,1)S(1)}, bf16[1024,704]{1,0:T(8,128)(2,1)S(1)}) fusion(f32[1024,704]{1,0:T(8,128)} %copy-done.21, f32[1024,704]{1,0:T(8,128)} %get-tuple-element.119, bf16[1024,2048]{1,0:T(8,128)(2,1)} %get-tuple-element.49, bf16[704,2048]{1,0:T(8,128)(2,1)S(1)} %copy-done.2), kind=kOutput, calls=%fused_computation.10 | convolution fusion | flops 2962161664 | bytes 15728640 | tf_op jit(solution)/shard_map/dot_general | solution.py:878
  263.9 1.1 copy-done.4
  265.0 0.5 copy-done.5
  265.6 8.5 %convert_bitcast_fusion = bf16[2,2048,704]{1,2,0:T(8,128)(2,1)} fusion(bf16[1024,2048]{1,0:T(8,128)(2,1)S(1)} %copy-done.20, bf16[1,1024,704]{2,1,0:T(8,128)(2,1)S(1)} %bitcast.33, bf16[1,1024,704]{2,1,0:T(8,128)(2,1)S(1)} %bitcast.34), kind=kOutput, calls=%fused_computation | convolution fusion | flops 5909905408 | bytes 12845056 | tf_op jit(solution)/shard_map/td,ktf->kdf/dot_general | solution.py:881
  274.0 0.3 reduce-scatter.8.cloned.1.call-start
  274.3 68.7 %mlp_back.1 = (f32[128,2048]{1,0:T(8,128)}, f32[2,2048]{1,0:T(2,128)}, bf16[1024,2048]{1,0:T(8,128)(2,1)}) custom-call(bf16[1024,704]{1,0:T(8,128)(2,1)} %copy-done.5, bf16[1024,704]{1,0:T(8,128)(2,1)} %copy-done.4, bf16[2,2048,704]{2,1,0:T(8,128)(2,1)} %all-gather.5.cloned.1.call-done.w_ref, f32[128,2048]{1,0:T(8,128)} %get-tuple-element.54.resid_ref, ...), custom_call_target="tpu_custom_call" | custom-call | bytes 150000000 | tf_op jit(solution)/shard_map/mlp_back/pallas_call | solution.py:479
  343.0 0.0 reduce-scatter.4.cloned.1.call-done
  343.1 26.5 %attention_back.1 = (bf16[3,1024,256]{2,1,0:T(8,128)(2,1)}, f32[3,256]{1,0:T(4,128)}, bf16[4,2048,256]{2,1,0:T(8,128)(2,1)}) custom-call(bf16[1024,2048]{1,0:T(8,128)(2,1)} %get-tuple-element.57.grad_ref, bf16[256,2048]{1,0:T(8,128)(2,1)} %get-tuple-element.47.w_ref, bf16[1024,2048]{1,0:T(8,128)(2,1)} %get-tuple-element.43.rows_ref, ...), custom_call_target="tpu_custom_call" | custom-call | bytes 120000000 | tf_op jit(solution)/shard_map/attention_back/pallas_call | solution.py:790
  369.6 0.1 pad.3.clone
  369.7 36.5 %attn_back.1 = (f32[128,2048]{1,0:T(8,128)}, f32[2,2048]{1,0:T(2,128)}) custom-call(bf16[3,1024,256]{2,1,0:T(8,128)(2,1)} %get-tuple-element.63.parts_ref, bf16[3,2048,256]{2,1,0:T(8,128)(2,1)} %get-tuple-element.44.w_ref, bf16[128,2048]{1,0:T(8,128)(2,1)} %x_ref.5, f32[128,2048]{1,0:T(8,128)} %get-tuple-element.64.grad_ref, ...), custom_call_target="tpu_custom_call" | custom-call | bytes 100000000 | tf_op jit(solution)/shard_map/attn_back/pallas_call | solution.py:525
  406.2 1.3 convert_element_type.65
  407.6 15.5 %reduce-scatter.6.cloned.1.call-done = bf16[2,512,704]{1,2,0:T(8,128)(2,1)} async-done(((bf16[2,2048,704]{1,2,0:T(8,128)(2,1)}), bf16[2,512,704]{1,2,0:T(8,128)(2,1)}) %reduce-scatter.6.cloned.1.call-update) | async-done | bytes 1441808 | tf_op jit(solution)/shard_map/reduce_scatter | solution.py:828
  423.1 3.3 convert_element_type.64
  426.5 0.7 maximum_maximum_fusion.v_ref
  427.2 23.3 %sum_vectors.1 = f32[8,2048]{1,0:T(8,128)} custom-call(f32[8,2048]{1,0:T(8,128)} %maximum_maximum_fusion.v_ref), custom_call_target="tpu_custom_call" | custom-call | bytes 30000000 | tf_op jit(solution)/shard_map/sum_vectors/pallas_call | solution.py:618
  450.5 1.5 slice.32
  452.0 33.8 %down_sum.1 = bf16[128,2048]{1,0:T(8,128)(2,1)} custom-call(bf16[1024,704]{1,0:T(8,128)(2,1)} %copy-done.6, bf16[704,2048]{1,0:T(8,128)(2,1)} %all-gather.3.cloned.1.call-done.w_ref, f32[128,2048]{1,0:T(8,128)} %get-tuple-element.54.resid_ref), custom_call_target="tpu_custom_call" | custom-call | bytes 100000000 | tf_op jit(solution)/shard_map/down_sum/pallas_call | solution.py:562
  485.8 0.6 fusion.23
  486.5 20.3 %reduce-scatter.8.cloned.1.call-done = bf16[4,512,256]{2,1,0:T(8,128)(2,1)} async-done(((bf16[4,2048,256]{2,1,0:T(8,128)(2,1)}), bf16[4,512,256]{2,1,0:T(8,128)(2,1)}) %reduce-scatter.8.cloned.1.call-update) | async-done | bytes 1048592 | tf_op jit(solution)/shard_map/reduce_scatter | solution.py:828
  506.8 1.5 convert_element_type.63
  508.3 1.0 copy.57
  509.3 1.3 slice.38
  510.6 0.8 copy.65
  511.4 1.0 copy.66
  (52 shorter events, 0.2 us)
Async XLA Ops:
  7.2 3.5 copy-start.12
  7.2 4.1 copy-start.13
  7.2 4.7 copy-start.17
  7.2 5.0 copy-start.14
  7.2 5.6 %copy-start.15 = (bf16[2048]{0:T(1024)(128)(2,1)S(1)}, bf16[2048]{0:T(1024)(128)(2,1)}, u32[]{:S(2)}) copy-start(bf16[2048]{0:T(1024)(128)(2,1)} %param.21) | copy-start | bytes 12292
  7.2 160.0 %all-gather.3.cloned.1.call-start = ((), (), s32[]{:S(2)}) async-start(), calls=%async_computation.3 | async-start | bytes 3604480 | tf_op jit(solution)/shard_map/all_gather | solution.py:857
  8.0 229.7 %all-gather.5.cloned.1.call-start = ((), (), s32[]{:S(2)}) async-start(), calls=%async_computation.4 | async-start | bytes 7864320 | tf_op jit(solution)/shard_map/all_gather | solution.py:858
  10.6 332.5 %reduce-scatter.4.cloned.1.call-start = ((), (), s32[]{:S(2)}) async-start(), calls=%async_computation.5 | async-start | bytes 3604480 | tf_op jit(solution)/shard_map/reduce_scatter | solution.py:828
  237.7 6.6 %copy-start.1 = (bf16[2,2048,704]{2,1,0:T(8,128)(2,1)S(1)}, bf16[2,2048,704]{2,1,0:T(8,128)(2,1)}, u32[]{:S(2)}) copy-start(bf16[2,2048,704]{2,1,0:T(8,128)(2,1)} %all-gather.5.cloned.1.call-done.w_ref) | copy-start | bytes 17301508
  237.7 6.6 %copy-start.19 = (bf16[1024,2048]{1,0:T(8,128)(2,1)S(1)}, bf16[1024,2048]{1,0:T(8,128)(2,1)}, u32[]{:S(2)}) copy-start(bf16[1024,2048]{1,0:T(8,128)(2,1)} %get-tuple-element.48) | copy-start | bytes 12582916
  244.3 5.3 %copy-start.21 = (f32[1024,704]{1,0:T(8,128)}, f32[1024,704]{1,0:T(8,128)S(1)}, u32[]{:S(2)}) copy-start(f32[1024,704]{1,0:T(8,128)S(1)} %fusion.2) | copy-start | bytes 8650756
  244.3 6.5 %copy-start.18 = (bf16[1024,2048]{1,0:T(8,128)(2,1)S(1)}, bf16[1024,2048]{1,0:T(8,128)(2,1)}, u32[]{:S(2)}) copy-start(bf16[1024,2048]{1,0:T(8,128)(2,1)} %get-tuple-element.49) | copy-start | bytes 12582916
  249.6 1.1 copy-start.6
  250.8 4.8 copy-start.2
  255.3 167.8 %reduce-scatter.6.cloned.1.call-start = ((), (), s32[]{:S(2)}) async-start(), calls=%async_computation.6 | async-start | bytes 7208960 | tf_op jit(solution)/shard_map/reduce_scatter | solution.py:828
  255.5 10.0 %copy-start.20 = (bf16[1024,2048]{1,0:T(8,128)(2,1)S(1)}, bf16[1024,2048]{1,0:T(8,128)(2,1)}, u32[]{:S(2)}) copy-start(bf16[1024,2048]{1,0:T(8,128)(2,1)} %get-tuple-element.48) | copy-start | bytes 12582916
  263.9 1.1 copy-start.4
  263.9 1.7 copy-start.5
  274.0 232.7 %reduce-scatter.8.cloned.1.call-start = ((), (), s32[]{:S(2)}) async-start(), calls=%async_computation.7 | async-start | bytes 5242880 | tf_op jit(solution)/shard_map/reduce_scatter | solution.py:828
  369.7 36.5 %copy-start.8 = (bf16[704,512]{1,0:T(8,128)(2,1)S(1)}, bf16[704,512]{1,0:T(8,128)(2,1)}, u32[]{:S(2)}) copy-start(bf16[704,512]{1,0:T(8,128)(2,1)} %reduce-scatter.4.cloned.1.call-done) | copy-start | bytes 2162692
  369.7 37.9 %copy-start.16 = (f32[3,256]{1,0:T(4,128)S(1)}, f32[3,256]{1,0:T(4,128)}, u32[]{:S(2)}) copy-start(f32[3,256]{1,0:T(4,128)} %get-tuple-element.71) | copy-start | bytes 9220
  406.2 20.2 %copy-start.10 = (f32[2,2048]{1,0:T(2,128)S(1)}, f32[2,2048]{1,0:T(2,128)}, u32[]{:S(2)}) copy-start(f32[2,2048]{1,0:T(2,128)} %get-tuple-element.70) | copy-start | bytes 49156
  406.2 20.2 %copy-start.11 = (f32[2,2048]{1,0:T(2,128)S(1)}, f32[2,2048]{1,0:T(2,128)}, u32[]{:S(2)}) copy-start(f32[2,2048]{1,0:T(2,128)} %get-tuple-element.69) | copy-start | bytes 49156
  450.5 35.4 %copy-start.9 = (f32[8,2048]{1,0:T(8,128)S(1)}, f32[8,2048]{1,0:T(8,128)}, u32[]{:S(2)}) copy-start(f32[8,2048]{1,0:T(8,128)} %sum_vectors.1) | copy-start | bytes 196612
  506.8 2.6 copy-start
  508.3 2.3 copy-start.3
  508.3 3.1 copy-start.7
Sparse Core Ops, SparseCore 0:
  9.6 105.8 all-gather.2
  117.6 120.0 all-gather.4
  255.4 63.4 reduce-scatter.3
  321.1 102.0 reduce-scatter.5
  425.2 81.4 reduce-scatter.7

commit v3 on v2

--- a/solution.py
+++ b/solution.py
@@ -222,71 +222,6 @@
     )
 
 
-def gather_kernel(
-    x_ref, cot_ref, gain_ref, bias_ref, qkv_ref, out_ref,
-    rows_all, cot_all, qkv_all, out_all,
-    row_block, cot_block, *sems
-):
-    place = Place()
-    greet(place, along_dp=True)
-    depth = qkv_ref.shape[1]
-    width = out_ref.shape[1]
-
-    def qkv_at(ref, z):
-        return ref.at[:, pl.ds(pl.multiple_of(z * depth, depth), depth), :]
-
-    def out_at(ref, z):
-        return ref.at[:, pl.ds(pl.multiple_of(z * width, width), width)]
-
-    qkv = DepthGather(place, qkv_ref, qkv_all, qkv_at, *sems[0:3])
-    out = DepthGather(place, out_ref, out_all, out_at, *sems[3:6])
-    rows = RowGather(place, row_block, rows_all, *sems[6:9])
-    cots = RowGather(place, cot_block, cot_all, *sems[9:12])
-    qkv.start()
-    out.start()
-    gain, bias = gain_ref[...].astype(jnp.float32), bias_ref[...].astype(jnp.float32)
-
-    def norm(at):
-        normed, _ = normal(x_ref[at, :].astype(jnp.float32))
-        row_block[at, :] = (normed * gain + bias).astype(jnp.bfloat16)
-        cot_block[at, :] = cot_ref[at, :].astype(jnp.bfloat16)
-
-    row_loop(x_ref.shape[0], norm)
-    rows.start()
-    cots.start()
-    rows.forward()
-    qkv.forward()
-    cots.forward()
-    out.forward()
-    rows.finish()
-    cots.finish()
-    qkv.finish()
-    out.finish()
-
-
-def gather_inputs(x, cot, gain, bias, qkv, out):
-    ndp, nctx = lax.axis_size("dp"), lax.axis_size("ctx")
-    rows, d = x.shape
-    bf16 = jnp.bfloat16
-    return pl.pallas_call(
-        gather_kernel,
-        out_shape=(
-            jax.ShapeDtypeStruct((rows * nctx, d), bf16),
-            jax.ShapeDtypeStruct((rows * nctx, d), bf16),
-            jax.ShapeDtypeStruct((qkv.shape[0], qkv.shape[1] * ndp, qkv.shape[2]), bf16),
-            jax.ShapeDtypeStruct((out.shape[0], out.shape[1] * ndp), bf16),
-        ),
-        in_specs=[VMEM] * 6,
-        out_specs=(ANY,) * 4,
-        scratch_shapes=[pltpu.VMEM((rows, d), bf16), pltpu.VMEM((rows, d), bf16)]
-        + depth_sems(ndp) * 2
-        + gather_sems(nctx) * 2,
-        compiler_params=pltpu.CompilerParams(collective_id=0, has_side_effects=True),
-        cost_estimate=pl.CostEstimate(flops=0, bytes_accessed=200_000_000, transcendentals=0),
-        name="gather_inputs",
-    )(x, cot, gain[None, :], bias[None, :], qkv, out)
-
-
 class SumScatter:
     TILE = 512
 
@@ -298,7 +233,7 @@
 
     def pair(self, i):
         return push(
-            self.to_pair.at[i], self.from_pair.at[i], self.pair_send.at[i], self.pair_recv.at[i], self.place.partner()
+            self.to_pair.at[lax.rem(i, 2)], self.from_pair.at[i], self.pair_send.at[i], self.pair_recv.at[i], self.place.partner()
         )
 
     def chips(self, i):
@@ -319,7 +254,7 @@
             self.pair(i).wait_recv()
 
             def add(at):
-                both = self.mine[i, at, :] + self.from_pair[i, at, :].astype(jnp.float32)
+                both = self.mine[lax.rem(i, 2), at, :] + self.from_pair[i, at, :].astype(jnp.float32)
                 self.to_chip[i, at, :] = both.astype(jnp.bfloat16)
 
             row_loop(rows, add)
@@ -328,6 +263,8 @@
         def step(i, carry):
             q = lax.rem(place.p + 1 + i, nchip)
             first = pl.multiple_of(q * 2 * rows, 2 * rows)
+            slot = lax.rem(i, 2)
+            pl.when(i >= 2)(lambda: self.pair(i - 2).wait_send())
 
             def columns(j, inner):
                 cols = pl.ds(pl.multiple_of(j * tile, tile), tile)
@@ -335,13 +272,13 @@
 
                 @pl.when(place.k == 0)
                 def _():
-                    self.mine[i, :, cols] = part[:rows]
-                    self.to_pair[i, :, cols] = part[rows:].astype(jnp.bfloat16)
+                    self.mine[slot, :, cols] = part[:rows]
+                    self.to_pair[slot, :, cols] = part[rows:].astype(jnp.bfloat16)
 
                 @pl.when(place.k == 1)
                 def _():
-                    self.mine[i, :, cols] = part[rows:]
-                    self.to_pair[i, :, cols] = part[:rows].astype(jnp.bfloat16)
+                    self.mine[slot, :, cols] = part[rows:]
+                    self.to_pair[slot, :, cols] = part[:rows].astype(jnp.bfloat16)
 
                 return inner
 
@@ -357,13 +294,13 @@
 
     def total(self, at):
         last = self.place.nchip - 1
-        value = self.mine[last, at, :] + self.from_pair[last, at, :].astype(jnp.float32)
+        value = self.mine[last % 2, at, :] + self.from_pair[last, at, :].astype(jnp.float32)
         for i in range(last):
             value = value + self.from_chip[i, at, :].astype(jnp.float32)
         return value
 
     def finish(self):
-        for i in range(self.place.nchip):
+        for i in range(max(self.place.nchip - 2, 0), self.place.nchip):
             self.pair(i).wait_send()
         for i in range(self.place.nchip - 1):
             self.chips(i).wait_send()
@@ -373,8 +310,8 @@
     n = nctx // 2
     bf16 = jnp.bfloat16
     return [
-        pltpu.VMEM((n, rows, d), jnp.float32),
-        pltpu.VMEM((n, rows, d), bf16),
+        pltpu.VMEM((2, rows, d), jnp.float32),
+        pltpu.VMEM((2, rows, d), bf16),
         pltpu.VMEM((n, rows, d), bf16),
         pltpu.VMEM((n - 1, rows, d), bf16),
         pltpu.VMEM((n - 1, rows, d), bf16),
@@ -391,53 +328,6 @@
 
 def dot_nt(a, b):
     return lax.dot_general(a, b, (((1,), (1,)), ((), ())), preferred_element_type=jnp.float32)
-
-
-def attn_out_kernel(attn_ref, w_ref, x_ref, gain_ref, bias_ref, resid_ref, normed_all, block, *scratch):
-    place = Place()
-    greet(place)
-    scatter = SumScatter(
-        place,
-        x_ref.shape[0],
-        lambda rows, cols: dot_nn(attn_ref[rows, :], w_ref[:, cols]),
-        *scratch[:5],
-        scratch[5:9],
-    )
-    scatter.run()
-    gain, bias = gain_ref[...].astype(jnp.float32), bias_ref[...].astype(jnp.float32)
-
-    def norm(at):
-        resid = x_ref[at, :].astype(jnp.float32) + scatter.total(at)
-        resid_ref[at, :] = resid
-        normed, _ = normal(resid)
-        block[at, :] = (normed * gain + bias).astype(jnp.bfloat16)
-
-    row_loop(x_ref.shape[0], norm)
-    rows = RowGather(place, block, normed_all, *scratch[9:12])
-    rows.start()
-    rows.forward()
-    rows.finish()
-    scatter.finish()
-
-
-def attn_out(attn, w, x, gain, bias):
-    nctx = lax.axis_size("ctx")
-    rows, d = x.shape
-    return pl.pallas_call(
-        attn_out_kernel,
-        out_shape=(
-            jax.ShapeDtypeStruct((rows, d), jnp.float32),
-            jax.ShapeDtypeStruct((rows * nctx, d), jnp.bfloat16),
-        ),
-        in_specs=[VMEM] * 5,
-        out_specs=(VMEM, ANY),
-        scratch_shapes=[pltpu.VMEM((rows, d), jnp.bfloat16)]
-        + scatter_scratch(nctx, rows, d)
-        + gather_sems(nctx),
-        compiler_params=pltpu.CompilerParams(collective_id=1, has_side_effects=True),
-        cost_estimate=pl.CostEstimate(flops=0, bytes_accessed=150_000_000, transcendentals=0),
-        name="attn_out",
-    )(attn, w, x, gain[None, :], bias[None, :])
 
 
 def mlp_back_kernel(
@@ -700,24 +590,321 @@
     tiles(seq // PAIR, queries)
 
 
-def attend_kernel(rows_ref, w_ref, shift_ref, cos_ref, sin_ref, pos_col, pos_row, *rest):
-    attend(rows_ref, w_ref, shift_ref, cos_ref, sin_ref, pos_col, pos_row, *rest[:5], rest[6], rest[7], rest[5])
-
-
-def attention(rows_all, w, shift, cosine, sine, pos_col, pos_row):
-    seq, width = rows_all.shape[0], w.shape[2]
-    bf16 = jnp.bfloat16
+class DepthScatter:
+    def __init__(self, place, part, got, both, width, send, recv):
+        self.place, self.part, self.got, self.both, self.width = place, part, got, both, width
+        self.send, self.recv = send, recv
+        self.line = place.ndp == 4
+        z = place.z
+        self.end = jnp.logical_or(z == 0, z == 3)
+        self.middle = jnp.logical_not(self.end)
+        self.next = jnp.where(z == 3, 2, 1)
+        self.other = jnp.clip(3 - z, 1, 2)
+        self.near = jnp.clip(3 * (z - 1), 0, 3)
+
+    def block(self, z):
+        return self.part.at[:, pl.ds(pl.multiple_of(z * self.width, self.width), self.width)]
+
+    def copy(self, src, slot, sem, z):
+        return push(src, self.got.at[slot], self.send.at[sem], self.recv.at[slot], {"dp": z, "ctx": self.place.c})
+
+    def from_end(self):
+        far = 3 - self.place.z
+        return [
+            self.copy(self.block(far), 2, 0, self.next),
+            self.copy(self.block(3 - self.next), 3, 1, self.next),
+            self.copy(self.block(self.next), 0, 2, self.next),
+        ]
+
+    def from_middle(self):
+        return [
+            self.copy(self.block(self.near), 0, 0, self.near),
+            self.copy(self.both.at[0], 1, 1, 3 - self.near),
+            self.copy(self.both.at[1], 1, 2, self.other),
+        ]
+
+    def across(self):
+        z, n = self.place.z, self.place.ndp
+        return [self.copy(self.block(lax.rem(z + i, n)), i - 1, i - 1, lax.rem(z + i, n)) for i in range(1, n)]
+
+    def start(self):
+        if not self.line:
+            for copy in self.across():
+                copy.start()
+            return
+
+        @pl.when(self.end)
+        def _():
+            for copy in self.from_end():
+                copy.start()
+
+        @pl.when(self.middle)
+        def _():
+            self.from_middle()[0].start()
+
+    def hand_on(self):
+        if not self.line:
+            return
+
+        @pl.when(self.middle)
+        def _():
+            for j, owner in enumerate((3 - self.near, self.other)):
+                self.copy(self.both.at[0], 2 + j, 0, self.near).wait_recv()
+                cols = pl.ds(pl.multiple_of(owner * self.width, self.width), self.width)
+
+                def add(at, j=j, cols=cols):
+                    total = self.part[at, cols].astype(jnp.float32) + self.got[2 + j, at, :].astype(jnp.float32)
+                    self.both[j, at, :] = total.astype(jnp.bfloat16)
+
+                row_loop(self.part.shape[0], add)
+                self.from_middle()[1 + j].start()
+
+    def finish(self, out_ref):
+        count = 2 if self.line else self.place.ndp - 1
+        for slot in range(count):
+            self.copy(self.got.at[slot], slot, 0, self.next).wait_recv()
+        cols = pl.ds(pl.multiple_of(self.place.z * self.width, self.width), self.width)
+
+        def add(at):
+            value = self.part[at, cols].astype(jnp.float32)
+            for slot in range(count):
+                value = value + self.got[slot, at, :].astype(jnp.float32)
+            out_ref[at, :] = value
+
+        row_loop(self.part.shape[0], add)
+        if not self.line:
+            for copy in self.across():
+                copy.wait_send()
+            return
+
+        @pl.when(self.end)
+        def _():
+            for copy in self.from_end():
+                copy.wait_send()
+
+        @pl.when(self.middle)
+        def _():
+            for copy in self.from_middle():
+                copy.wait_send()
+
+
+def depth_scatter_scratch(ndp, rows, width):
+    slots = 4 if ndp == 4 else ndp - 1
+    return [
+        pltpu.VMEM((slots, rows, width), jnp.bfloat16),
+        pltpu.VMEM((2, rows, width), jnp.bfloat16),
+        DMA((max(slots, 3),)),
+        DMA((slots,)),
+    ]
+
+
+def forward_kernel(
+    x_ref, cot_ref, gain1_ref, bias1_ref, gain2_ref, bias2_ref, shift_ref, cos_ref, sin_ref, pos_col, pos_row,
+    qkv_ref, out_ref, gateup_ref, down_ref,
+    resid_ref, q_t, k_t, v_t, attn_t, lse, hidden_ref, gate_side, up_side, down_grads,
+    rows_out, cots_out, qkv_out, out_out, normed_out, gateup_out, down_all,
+    row_block, cot_block, rows_all, cot_all, qkv_all, out_all, gateup_all,
+    k_n, bias, attn, gate_f, hidden_t, *sems
+):
+    f32, bf16 = jnp.float32, jnp.bfloat16
+    place = Place()
+    greet(place, along_dp=True)
+    sems = list(sems)
+
+    def take(n):
+        head = sems[:n]
+        del sems[:n]
+        return head
+
+    def along_rows(size):
+        return lambda ref, z: ref.at[:, pl.ds(pl.multiple_of(z * size, size), size), :]
+
+    def along_lanes(size):
+        return lambda ref, z: ref.at[:, pl.ds(pl.multiple_of(z * size, size), size)]
+
+    depth, width = qkv_ref.shape[1], out_ref.shape[1]
+
+    def half(i):
+        return lambda ref, z: ref.at[i, pl.ds(pl.multiple_of(z * depth, depth), depth), :]
+
+    qkv = DepthGather(place, qkv_ref, qkv_all, along_rows(depth), *take(3))
+    out = DepthGather(place, out_ref, out_all, along_lanes(width), *take(3))
+    gate = DepthGather(place, gateup_ref.at[0], gateup_all, half(0), *take(3))
+    up = DepthGather(place, gateup_ref.at[1], gateup_all, half(1), *take(3))
+    down = DepthGather(place, down_ref, down_all, along_lanes(width), *take(3))
+    rows = RowGather(place, row_block, rows_all, *take(3))
+    cots = RowGather(place, cot_block, cot_all, *take(3))
+    normeds = RowGather(place, row_block, rows_all, *take(3))
+    scatter_refs = take(9)
+    got, both, dsend, drecv = take(4)
+    (save_sem,) = take(1)
+    seq = rows_all.shape[0]
+
+    def save(i, src, dst):
+        return pltpu.make_async_copy(src, dst, save_sem.at[i])
+
+    saves = [
+        save(0, rows_all, rows_out),
+        save(1, cot_all, cots_out),
+        save(2, qkv_all, qkv_out),
+        save(3, out_all, out_out),
+        save(4, rows_all, normed_out),
+        save(5, gateup_all, gateup_out),
+    ]
+
+    qkv.start()
+    out.start()
+    gain, shift = gain1_ref[...].astype(f32), bias1_ref[...].astype(f32)
+
+    def norm1(at):
+        normed, _ = normal(x_ref[at, :].astype(f32))
+        row_block[at, :] = (normed * gain + shift).astype(bf16)
+        cot_block[at, :] = cot_ref[at, :].astype(bf16)
+
+    row_loop(x_ref.shape[0], norm1)
+    rows.start()
+    cots.start()
+    rows.forward()
+    qkv.forward()
+    cots.forward()
+    out.forward()
+    gate.start()
+    up.start()
+    rows.finish()
+    saves[0].start()
+    cots.finish()
+    saves[1].start()
+    qkv.finish()
+    saves[2].start()
+    attend(rows_all, qkv_all, shift_ref, cos_ref, sin_ref, pos_col, pos_row, q_t, k_t, v_t, attn_t, lse, k_n, bias, attn)
+    out.finish()
+    saves[3].start()
+    saves[0].wait()
+    scatter = SumScatter(
+        place,
+        x_ref.shape[0],
+        lambda at, cols: dot_nn(attn[at, :], out_all[:, cols]),
+        *scatter_refs[:5],
+        scatter_refs[5:9],
+    )
+    scatter.run()
+    gain2, shift2 = gain2_ref[...].astype(f32), bias2_ref[...].astype(f32)
+
+    def norm2(at):
+        resid = x_ref[at, :].astype(f32) + scatter.total(at)
+        resid_ref[at, :] = resid
+        normed, _ = normal(resid)
+        row_block[at, :] = (normed * gain2 + shift2).astype(bf16)
+
+    row_loop(x_ref.shape[0], norm2)
+    normeds.start()
+    gate.forward()
+    normeds.forward()
+    up.forward()
+    down.start()
+    normeds.finish()
+    saves[4].start()
+    scatter.finish()
+    gate.finish()
+
+    def gates(t):
+        at = span(t, PAIR)
+        gate_f[at, :] = dot_nn(rows_all[at, :], gateup_all[0])
+
+    tiles(seq // PAIR, gates)
+    up.finish()
+    saves[5].start()
+
+    def ups(t):
+        at = span(t, PAIR)
+        value = dot_nn(rows_all[at, :], gateup_all[1])
+        g = gate_f[at, :]
+        sigma = jax.nn.sigmoid(g)
+        swish = g * sigma
+        hidden = (swish * value).astype(bf16)
+        hidden_ref[at, :] = hidden
+        hidden_t[:, at] = hidden.T
+        gate_side[at, :] = (value * sigma * (1.0 + g * (1.0 - sigma))).astype(bf16)
+        up_side[at, :] = swish.astype(bf16)
+
+    tiles(seq // PAIR, ups)
+    saves[4].wait()
+    part = rows_all.at[: hidden_t.shape[0]]
+
+    def weights(j):
+        cols = span(j, 2 * PAIR)
+        part[:, cols] = dot_nn(hidden_t[...], cot_all[:, cols]).astype(bf16)
+
+    tiles(cot_all.shape[1] // (2 * PAIR), weights)
+    summed = DepthScatter(place, part, got, both, width, dsend, drecv)
+    summed.start()
+    down.forward()
+    summed.hand_on()
+    summed.finish(down_grads)
+    down.finish()
+    for i in (1, 2, 3, 5):
+        saves[i].wait()
+
+
+def forward(x, cot, gain1, bias1, gain2, bias2, shift, cosine, sine, pos_col, pos_row, qkv, out, gateup, down):
+    ndp, nctx = lax.axis_size("dp"), lax.axis_size("ctx")
+    rows, d = x.shape
+    seq, width, ff = rows * nctx, qkv.shape[2], gateup.shape[2]
     heads = width // HEAD_DIM
+    bf16, f32 = jnp.bfloat16, jnp.float32
+    row = [v[None, :] for v in (gain1, bias1, gain2, bias2)]
+
+    def shaped(shape, dtype=bf16):
+        return jax.ShapeDtypeStruct(shape, dtype)
+
     return pl.pallas_call(
-        attend_kernel,
-        out_shape=tuple(jax.ShapeDtypeStruct((width, seq), bf16) for _ in range(4))
-        + (jax.ShapeDtypeStruct((8, seq), jnp.float32), jax.ShapeDtypeStruct((seq, width), bf16)),
-        in_specs=[VMEM] * 7,
-        out_specs=(VMEM,) * 6,
-        scratch_shapes=[pltpu.VMEM((heads, seq, HEAD_DIM), bf16), pltpu.VMEM((seq, PAIR), jnp.float32)],
-        cost_estimate=pl.CostEstimate(flops=0, bytes_accessed=40_000_000, transcendentals=0),
-        name="attention",
-    )(rows_all, w, shift, cosine, sine, pos_col, pos_row)
+        forward_kernel,
+        out_shape=(
+            shaped((rows, d), f32),
+            shaped((width, seq)),
+            shaped((width, seq)),
+            shaped((width, seq)),
+            shaped((width, seq)),
+            shaped((8, seq), f32),
+            shaped((seq, ff)),
+            shaped((seq, ff)),
+            shaped((seq, ff)),
+            shaped(down.shape, f32),
+            shaped((seq, d)),
+            shaped((seq, d)),
+            shaped((3, d, width)),
+            shaped((width, d)),
+            shaped((seq, d)),
+            shaped((2, d, ff)),
+            shaped((ff, d)),
+        ),
+        in_specs=[VMEM] * 15,
+        out_specs=(VMEM,) * 10 + (ANY,) * 7,
+        scratch_shapes=[
+            pltpu.VMEM((rows, d), bf16),
+            pltpu.VMEM((rows, d), bf16),
+            pltpu.VMEM((seq, d), bf16),
+            pltpu.VMEM((seq, d), bf16),
+            pltpu.VMEM((3, d, width), bf16),
+            pltpu.VMEM((width, d), bf16),
+            pltpu.VMEM((2, d, ff), bf16),
+            pltpu.VMEM((heads, seq, HEAD_DIM), bf16),
+            pltpu.VMEM((seq, PAIR), f32),
+            pltpu.VMEM((seq, width), bf16),
+            pltpu.VMEM((seq, ff), f32),
+            pltpu.VMEM((ff, seq), bf16),
+        ]
+        + depth_sems(ndp) * 5
+        + gather_sems(nctx) * 3
+        + scatter_scratch(nctx, rows, d)
+        + depth_scatter_scratch(ndp, ff, d // ndp)
+        + [DMA((6,))],
+        compiler_params=pltpu.CompilerParams(
+            collective_id=0, has_side_effects=True, vmem_limit_bytes=67_000_000
+        ),
+        cost_estimate=pl.CostEstimate(flops=0, bytes_accessed=700_000_000, transcendentals=0),
+        name="forward",
+    )(x, cot, *row, shift, cosine, sine, pos_col, pos_row, qkv, out, gateup, down)
 
 
 def attend_back_kernel(
@@ -851,11 +1038,6 @@
     half_group = tok_rows // 2
     group_order = group_perm[0]
     qkv_shift = qkv_bias.astype(f32)
-    rows_all, cot_all, qkv_local, out_local = gather_inputs(
-        block_input, out_cotangent, attn_norm_gain, attn_norm_bias, qkv_weight, out_weight
-    )
-    down_local = lax.all_gather(down_weight, "dp", axis=1, tiled=True)
-    gateup_local = lax.all_gather(gateup_weight, "dp", axis=1, tiled=True)
     all_pos = group_positions(group_order, seq_len, half_group)
     cos_all, sin_all = rope_tables(all_pos)
     pos_f = all_pos.astype(f32)
@@ -863,21 +1045,16 @@
     width_local = qkv_weight.shape[2]
     head_first = cycle_index * width_local
     shift_local = lax.dynamic_slice_in_dim(qkv_shift, head_first, width_local, 1)
-    q_t, k_t, v_t, attn_t, lse, attn_local = attention(
-        rows_all, qkv_local, shift_local, cos_all, sin_all, pos_col, pos_row
+    (
+        residual_stream, q_t, k_t, v_t, attn_t, lse, hidden_b, gate_side, up_side, down_grads,
+        rows_all, cot_all, qkv_local, out_local, mlp_all, gateup_local, down_local,
+    ) = forward(
+        block_input, out_cotangent, attn_norm_gain, attn_norm_bias, mlp_norm_gain, mlp_norm_bias, shift_local,
+        cos_all, sin_all, pos_col, pos_row, qkv_weight, out_weight, gateup_weight, down_weight,
     )
-    attn_local, down_local = lax.optimization_barrier((attn_local, down_local))
-    residual_stream, mlp_all = attn_out(attn_local, out_local, block_input, mlp_norm_gain, mlp_norm_bias)
-    gate_val = jnp.dot(mlp_all, gateup_local[0], preferred_element_type=f32)
-    up_val = jnp.dot(mlp_all, gateup_local[1], preferred_element_type=f32)
-    sigma = jax.nn.sigmoid(gate_val)
-    hidden_b = (gate_val * sigma * up_val).astype(bf16)
-    down_w_grad = jnp.dot(hidden_b.T, cot_all, preferred_element_type=f32).astype(bf16)
-    down_local, down_w_grad = lax.optimization_barrier((down_local, down_w_grad))
-    down_grads = shard(down_w_grad)
     hidden_grad = jnp.dot(cot_all, down_local.T, preferred_element_type=f32)
-    gate_grad = (hidden_grad * up_val * sigma * (1.0 + gate_val * (1.0 - sigma))).astype(bf16)
-    up_grad = (hidden_grad * gate_val * sigma).astype(bf16)
+    gate_grad = (hidden_grad * gate_side.astype(f32)).astype(bf16)
+    up_grad = (hidden_grad * up_side.astype(f32)).astype(bf16)
     gateup_w_grad = jnp.einsum(
         "td,ktf->kdf", mlp_all, jnp.stack([gate_grad, up_grad]), preferred_element_type=f32
     ).astype(bf16)
@@ -886,18 +1063,19 @@
     resid_grad, second_vectors, resid_all = mlp_back(
         gate_grad, up_grad, gateup_local, residual_stream, out_cotangent, mlp_norm_gain
     )
-    resid_all, down_grads = lax.optimization_barrier((resid_all, down_grads))
     grad_parts_b, shift_part, attn_grads = attention_back(
         resid_all, out_local, rows_all, cos_all, sin_all, pos_col, pos_row, q_t, k_t, v_t, attn_t, lse
     )
     shift_grad = lax.dynamic_update_slice_in_dim(jnp.zeros((3, D), f32), shift_part, head_first, 1)
-    attn_grads = shard(attn_grads).astype(f32)
+    attn_grads = shard(attn_grads)
     input_grad, first_vectors = attn_back(grad_parts_b, qkv_local, block_input, resid_grad, attn_norm_gain)
     hidden_late, first_vectors, gateup_grads = lax.optimization_barrier((hidden_b, first_vectors, gateup_grads))
     block_output = down(hidden_late, down_local, residual_stream)
     small = sum_vectors(
         jnp.concatenate([first_vectors, second_vectors, shift_grad, jnp.zeros((1, D), f32)], axis=0)
     )
+    small, block_output, attn_grads = lax.optimization_barrier((small, block_output, attn_grads))
+    attn_grads = attn_grads.astype(f32)
     return (
         block_output,
         input_grad,
@@ -909,7 +1087,7 @@
         small[2],
         small[3],
         gateup_grads.astype(f32),
-        down_grads.astype(f32),
+        down_grads,
     )
 
 

time: 519 us -> 512 us (0.987)
  Pallas kernels: 403 us -> 459 us
  waiting for transfers between devices: 43.5 us -> 0.08 us
  matrix products: 33.2 us -> 16 us
    pallas_call x3 -> x1, Pallas kernels: 214 us -> 276 us  [forward(): pl.pallas_call(forward_kernel, out_shape=(shaped((rows, d), f32), shaped(...]
    reduce_scatter x3 -> x2, waiting for transfers between devices: 35.9 us -> 0.04 us  [shard(): return lax.psum_scatter(grad, 'dp', scatter_dimension=1, tiled=True)]
    dot_general x3 -> x0, matrix products: 16.4 us -> none  [the longest x1 6.59 us: per_device(): gate_val = jnp.dot(mlp_all, gateup_local[0], preferred_element_type=f32)]
    all_gather x2 -> x0, waiting for transfers between devices: 6.91 us -> none  [the longest x1 6.91 us: per_device(): gateup_local = lax.all_gather(gateup_weight, 'dp', axis=1, tiled=True)]
    pallas_call x1, Pallas kernels: 23.3 us -> 17.3 us  [sum_vectors(): pl.pallas_call(vectors_kernel, out_shape=jax.ShapeDtypeStruct(v.shape, f3...]
  transfers between devices with their start and end apart: 5 -> 2, of which waited for: 3 -> 0; matrix products, arithmetic and copies ran while one was open for 6% -> 0% of each run, Pallas kernels for 78% -> 36%
where the time goes in v3:
time: 512 us
  Pallas kernels  459 us (90%)
  matrix products  16 us (3%)
  between operations  14.3 us (3%)
  local copies, waits for them, and re-layouts  13.2 us (3%)
  other arithmetic  8.51 us (2%)
    pallas_call x1, Pallas kernels, forward(): pl.pallas_call(forward_kernel, out_shape=(shaped((rows, d), f32), shaped(...  276 us
    pallas_call x1, Pallas kernels, mlp_back(): pl.pallas_call(mlp_back_kernel, out_shape=(jax.ShapeDtypeStruct((rows, d)...  68.7 us
    pallas_call x1, Pallas kernels, attn_back(): pl.pallas_call(attn_back_kernel, out_shape=(jax.ShapeDtypeStruct((rows, d...  36.4 us
    pallas_call x1, Pallas kernels, down(): pl.pallas_call(down_kernel, out_shape=jax.ShapeDtypeStruct((rows, d), jnp...  34.8 us
    pallas_call x1, Pallas kernels, attention_back(): pl.pallas_call(attend_back_kernel, out_shape=(jax.ShapeDtypeStruct((3, se...  26.4 us
    pallas_call x1, Pallas kernels, sum_vectors(): pl.pallas_call(vectors_kernel, out_shape=jax.ShapeDtypeStruct(v.shape, f3...  17.3 us
  transfers between devices with their start and end apart: 2, of which 0 were waited for; matrix products, arithmetic and copies ran while one was open for 0% of the time, Pallas kernels for 36%

profile of v3, /device:TPU:0, one launch (start us, length us, event | category | flops | bytes accessed | tf_op | source)
XLA Modules:
  0.0 511.7 jit_solution(2345590773113819991)
XLA Ops:
  7.2 0.0 copy-start.10
  7.2 0.0 copy-start.11
  7.2 0.0 reduce-scatter.3.cloned.1.call-start
  7.3 0.7 select_reduce_fusion
  8.0 0.2 copy.34
  8.3 0.9 fusion.5.pos_col
  9.1 0.6 fusion.19.pos_row
  9.7 1.3 broadcast_in_dim.40.gain1_ref.gain_ref
  11.0 1.3 broadcast_in_dim.42.gain2_ref.gain_ref
  12.3 2.6 copy.35.gateup_ref
  14.9 0.0 copy-done.10
  14.9 0.6 broadcast_in_dim.41.bias1_ref
  15.5 0.6 broadcast_in_dim.43.bias2_ref
  16.1 1.3 dynamic-slice_convert_fusion.shift_ref
  17.4 0.8 multiply_sine_fusion
  18.2 275.8 %forward.1 = (f32[128,2048]{1,0:T(8,128)}, bf16[256,1024]{1,0:T(8,128)(2,1)}, bf16[256,1024]{1,0:T(8,128)(2,1)}, bf16[256,1024]{1,0:T(8,128)(2,1)}, bf16[256,102...) custom-call(bf16[128,2048]{1,0:T(8,128)(2,1)} %x_ref.3, ...), custom_call_target="tpu_custom_call" | custom-call | bytes 700000000 | tf_op jit(solution)/shard_map/forward/pallas_call | solution.py:860
  294.0 7.6 %multiply_convert_fusion = (bf16[1024,704]{1,0:T(8,128)(2,1)S(1)}, bf16[1024,704]{1,0:T(8,128)(2,1)S(1)}) fusion(bf16[1024,704]{1,0:T(8,128)(2,1)} %get-tuple-element.49, bf16[1024,704]{1,0:T(8,128)(2,1)} %get-tuple-element.48, bf16[1024,2048]{1,0:T(8,128)(2,1)} %get-tuple-element.46, bf16[704,2048]{1,0:T(8,128)(2,1)} %get-tuple-element.47.w_ref), kind=kOutput, calls=%fused_computation.5 | convolution fusion | flops 2957115392 | bytes 12845056 | tf_op jit(solution)/shard_map/dot_general | solution.py:1055
  301.6 0.0 copy-start.2
  301.6 0.0 copy-start.3
  301.6 8.4 %convert_bitcast_fusion = bf16[2,2048,704]{1,2,0:T(8,128)(2,1)} fusion(bf16[1024,2048]{1,0:T(8,128)(2,1)S(1)} %copy-done.13, bf16[1,1024,704]{2,1,0:T(8,128)(2,1)S(1)} %bitcast.21, bf16[1,1024,704]{2,1,0:T(8,128)(2,1)S(1)} %bitcast.22), kind=kOutput, calls=%fused_computation | convolution fusion | flops 5909905408 | bytes 12845056 | tf_op jit(solution)/shard_map/td,ktf->kdf/dot_general | solution.py:1058
  310.0 0.0 copy-done.2
  310.0 0.0 reduce-scatter.3.cloned.1.call-update
  310.1 0.3 reduce-scatter.5.cloned.1.call-start
  310.3 68.7 %mlp_back.1 = (f32[128,2048]{1,0:T(8,128)}, f32[2,2048]{1,0:T(2,128)}, bf16[1024,2048]{1,0:T(8,128)(2,1)}) custom-call(bf16[1024,704]{1,0:T(8,128)(2,1)} %copy-done.3, bf16[1024,704]{1,0:T(8,128)(2,1)} %copy-done.2, bf16[2,2048,704]{2,1,0:T(8,128)(2,1)} %get-tuple-element.53.w_ref, f32[128,2048]{1,0:T(8,128)} %get-tuple-element.54.resid_ref, ...), custom_call_target="tpu_custom_call" | custom-call | bytes 150000000 | tf_op jit(solution)/shard_map/mlp_back/pallas_call | solution.py:369
  379.0 26.4 %attention_back.1 = (bf16[3,1024,256]{2,1,0:T(8,128)(2,1)}, f32[3,256]{1,0:T(4,128)}, bf16[4,2048,256]{2,1,0:T(8,128)(2,1)}) custom-call(bf16[1024,2048]{1,0:T(8,128)(2,1)} %get-tuple-element.55.grad_ref, bf16[256,2048]{1,0:T(8,128)(2,1)} %get-tuple-element.56.w_ref, bf16[1024,2048]{1,0:T(8,128)(2,1)} %get-tuple-element.57.rows_ref, ...), custom_call_target="tpu_custom_call" | custom-call | bytes 120000000 | tf_op jit(solution)/shard_map/attention_back/pallas_call | solution.py:977
  405.3 0.0 reduce-scatter.5.cloned.1.call-update
  405.4 0.0 copy-start.12
  405.4 36.4 %attn_back.1 = (f32[128,2048]{1,0:T(8,128)}, f32[2,2048]{1,0:T(2,128)}) custom-call(bf16[3,1024,256]{2,1,0:T(8,128)(2,1)} %get-tuple-element.63.parts_ref, bf16[3,2048,256]{2,1,0:T(8,128)(2,1)} %get-tuple-element.64.w_ref, bf16[128,2048]{1,0:T(8,128)(2,1)} %x_ref.3, f32[128,2048]{1,0:T(8,128)} %get-tuple-element.65.grad_ref, ...), custom_call_target="tpu_custom_call" | custom-call | bytes 100000000 | tf_op jit(solution)/shard_map/attn_back/pallas_call | solution.py:415
  441.8 0.1 pad.3.clone
  441.9 0.0 reduce-scatter.3.cloned.1.call-done
  442.0 34.8 %down_sum.1 = bf16[128,2048]{1,0:T(8,128)(2,1)} custom-call(bf16[1024,704]{1,0:T(8,128)(2,1)} %get-tuple-element.71.hidden_ref, bf16[704,2048]{1,0:T(8,128)(2,1)} %get-tuple-element.47.w_ref, f32[128,2048]{1,0:T(8,128)} %get-tuple-element.54.resid_ref), custom_call_target="tpu_custom_call" | custom-call | bytes 100000000 | tf_op jit(solution)/shard_map/down_sum/pallas_call | solution.py:452
  476.8 0.0 copy-done.8
  476.8 0.0 copy-done.9
  476.8 0.7 maximum_maximum_fusion.v_ref
  477.5 17.3 %sum_vectors.1 = f32[8,2048]{1,0:T(8,128)} custom-call(f32[8,2048]{1,0:T(8,128)} %maximum_maximum_fusion.v_ref), custom_call_target="tpu_custom_call" | custom-call | bytes 30000000 | tf_op jit(solution)/shard_map/sum_vectors/pallas_call | solution.py:508
  494.9 0.0 copy-start.7
  494.9 0.0 reduce-scatter.5.cloned.1.call-done
  494.9 1.5 convert_element_type.60
  496.4 0.0 copy-done
  496.4 1.3 slice.28
  497.7 0.6 fusion.21
  498.3 0.6 slice.24
  499.0 1.0 copy.39
  500.0 2.0 convert_element_type.61
  502.0 0.0 copy-done.1
  502.0 0.8 copy.46
  502.8 1.0 copy.47
  503.8 1.1 copy.48
  (22 shorter events, 0.1 us)
Async XLA Ops:
  7.2 7.7 %copy-start.10 = (bf16[2048]{0:T(1024)(128)(2,1)S(1)}, bf16[2048]{0:T(1024)(128)(2,1)}, u32[]{:S(2)}) copy-start(bf16[2048]{0:T(1024)(128)(2,1)} %param.16) | copy-start | bytes 12292
  7.2 8.3 %copy-start.11 = (bf16[2048]{0:T(1024)(128)(2,1)S(1)}, bf16[2048]{0:T(1024)(128)(2,1)}, u32[]{:S(2)}) copy-start(bf16[2048]{0:T(1024)(128)(2,1)} %param.21) | copy-start | bytes 12292
  7.2 434.7 %reduce-scatter.3.cloned.1.call-start = ((), (), s32[]{:S(2)}) async-start(), calls=%async_computation.2 | async-start | bytes 7208960 | tf_op jit(solution)/shard_map/reduce_scatter | solution.py:1015
  294.0 7.6 %copy-start.13 = (bf16[1024,2048]{1,0:T(8,128)(2,1)S(1)}, bf16[1024,2048]{1,0:T(8,128)(2,1)}, u32[]{:S(2)}) copy-start(bf16[1024,2048]{1,0:T(8,128)(2,1)} %get-tuple-element.50) | copy-start | bytes 12582916
  301.6 8.4 %copy-start.2 = (bf16[1024,704]{1,0:T(8,128)(2,1)}, bf16[1024,704]{1,0:T(8,128)(2,1)S(1)}, u32[]{:S(2)}) copy-start(bf16[1024,704]{1,0:T(8,128)(2,1)S(1)} %get-tuple-element.52.up_ref) | copy-start | bytes 4325380
  301.6 8.4 %copy-start.3 = (bf16[1024,704]{1,0:T(8,128)(2,1)}, bf16[1024,704]{1,0:T(8,128)(2,1)S(1)}, u32[]{:S(2)}) copy-start(bf16[1024,704]{1,0:T(8,128)(2,1)S(1)} %get-tuple-element.51.gate_ref) | copy-start | bytes 4325380
  310.1 184.8 %reduce-scatter.5.cloned.1.call-start = ((), (), s32[]{:S(2)}) async-start(), calls=%async_computation.3 | async-start | bytes 5242880 | tf_op jit(solution)/shard_map/reduce_scatter | solution.py:1015
  405.4 36.5 %copy-start.12 = (f32[3,256]{1,0:T(4,128)S(1)}, f32[3,256]{1,0:T(4,128)}, u32[]{:S(2)}) copy-start(f32[3,256]{1,0:T(4,128)} %get-tuple-element.70) | copy-start | bytes 9220
  441.9 34.9 %copy-start.8 = (f32[2,2048]{1,0:T(2,128)S(1)}, f32[2,2048]{1,0:T(2,128)}, u32[]{:S(2)}) copy-start(f32[2,2048]{1,0:T(2,128)} %get-tuple-element.69) | copy-start | bytes 49156
  442.0 34.9 %copy-start.9 = (f32[2,2048]{1,0:T(2,128)S(1)}, f32[2,2048]{1,0:T(2,128)}, u32[]{:S(2)}) copy-start(f32[2,2048]{1,0:T(2,128)} %get-tuple-element.68) | copy-start | bytes 49156
  494.9 2.9 copy-start.7
  494.9 1.5 copy-start
  496.4 3.6 copy-start.5
  499.0 3.0 copy-start.1
  500.0 2.8 copy-start.6
  500.0 3.8 copy-start.4
Sparse Core Ops, SparseCore 0:
  310.2 101.5 reduce-scatter.2
  414.0 77.2 reduce-scatter.4

commit v4 on v3

--- a/solution.py
+++ b/solution.py
@@ -121,17 +121,98 @@
         self.keep().wait()
 
 
+class BoxGather(RowGather):
+    def part(self, c, half):
+        size = self.rows // 2
+        return self.whole.at[pl.ds(pl.multiple_of(c * self.rows + half * size, size), size)]
+
+    def near(self, axis):
+        place = self.place
+        other = 1 - lax.rem(place.p, 2) if axis == 0 else 1 - lax.div(place.p, 2)
+        q = 2 * lax.div(place.p, 2) + other if axis == 0 else 2 * other + lax.rem(place.p, 2)
+        return 2 * q + place.k
+
+    def across(self):
+        return 2 * (3 - self.place.p) + self.place.k
+
+    def piece(self, c, half, sem, to, own=False):
+        size = self.rows // 2
+        src = self.block.at[pl.ds(half * size, size)] if own else self.part(c, half)
+        return push(src, self.part(c, half), self.send.at[sem], self.recv.at[2 * c + half], self.place.at(to))
+
+    def own(self):
+        place = self.place
+        return push(self.block, self.slot(place.c), self.send.at[0], self.recv.at[2 * place.c], place.partner())
+
+    def first(self):
+        c = self.place.c
+        return [self.piece(c, h, 1 + n, self.near(a), True) for n, (a, h) in enumerate(((0, 0), (1, 1), (0, 1), (1, 0)))]
+
+    def second(self):
+        return [self.piece(self.near(a), a, 5 + a, self.near(1 - a)) for a in (0, 1)]
+
+    def to_partner(self):
+        place = self.place
+        pair = 2 * place.p + 1 - place.k
+        return [
+            self.piece(c, h, 7 + n, pair)
+            for n, (c, h) in enumerate(
+                ((self.near(0), 0), (self.near(1), 1), (self.near(0), 1), (self.near(1), 0), (self.across(), 0), (self.across(), 1))
+            )
+        ]
+
+    def start(self):
+        for copy in self.first():
+            copy.start()
+        self.own().start()
+        self.keep().start()
+
+    def forward(self):
+        second, pair = self.second(), self.to_partner()
+        for n, copy in enumerate(pair):
+            copy.wait_recv()
+            if n < 2:
+                second[n].start()
+            copy.start()
+
+    def finish(self):
+        place = self.place
+        pair = 2 * place.p + 1 - place.k
+        self.arrival_pair().wait_recv()
+        for n in range(6):
+            c = (self.near(0), self.near(1), self.near(0), self.near(1), self.across(), self.across())[n]
+            half = (0, 1, 1, 0, 0, 1)[n]
+            twin = c + 1 - 2 * place.k
+            self.piece(twin, half, 7 + n, pair).wait_recv()
+        self.own().wait_send()
+        for copy in self.first() + self.second() + self.to_partner():
+            copy.wait_send()
+        self.keep().wait()
+
+    def arrival_pair(self):
+        c = self.place.c + 1 - 2 * self.place.k
+        return push(self.block, self.slot(c), self.send.at[0], self.recv.at[2 * c], self.place.partner())
+
+
+def row_gather(place, *args):
+    return (BoxGather if place.nchip == 4 else RowGather)(place, *args)
+
+
 def gather_sems(nctx):
-    return [DMA((nctx,)), DMA((nctx,)), DMA]
+    return [DMA((13,)), DMA((2 * nctx,)), DMA] if nctx == 8 else [DMA((nctx,)), DMA((nctx,)), DMA]
 
 
 class DepthGather:
-    def __init__(self, place, piece, whole, where, send, recv, local):
+    def __init__(self, place, piece, whole, where, send, recv, local, passing=True):
         self.place, self.piece, self.whole, self.where = place, piece, whole, where
         self.send, self.recv, self.local = send, recv, local
-        self.line = place.ndp == 4
-        self.middle = jnp.logical_or(place.z == 1, place.z == 2)
-        self.far = 6 - 3 * place.z
+        self.line = place.ndp == 4 and passing
+        z = place.z
+        self.end = jnp.logical_or(z == 0, z == 3)
+        self.middle = jnp.logical_not(self.end)
+        self.near = jnp.clip(3 * (z - 1), 0, 3)
+        self.far = 3 - self.near
+        self.other = jnp.clip(3 - z, 1, 2)
 
     def copy(self, src, z_src, z_dst, sem):
         return push(
@@ -143,9 +224,11 @@
         if not self.line:
             return [(None, self.copy(self.piece, z, lax.rem(z + i, n), i - 1)) for i in range(1, n)]
         out = []
-        for sem, step in enumerate((2, -2, 1, -1)):
+        for sem, step in enumerate((1, -1, 2, -2)):
             d = z + step
             ok = jnp.logical_and(d >= 0, d < 4)
+            if abs(step) == 2:
+                ok = jnp.logical_and(ok, self.end)
             out.append((ok, self.copy(self.piece, z, jnp.clip(d, 0, 3), sem)))
         return out
 
@@ -160,18 +243,22 @@
                 pl.when(ok)(copy.start)
         self.keep().start()
 
-    def passed(self):
-        far = jnp.clip(self.far, 0, 3)
-        return self.copy(self.where(self.whole, far), far, jnp.clip(3 * (self.place.z - 1), 0, 3), 4)
-
-    def forward(self):
+    def passed(self, src, sem):
+        return self.copy(self.where(self.whole, src), src, self.near, sem)
+
+    def forward_next(self):
+        self.forward(self.other, 4)
+
+    def forward_far(self):
+        self.forward(self.far, 5)
+
+    def forward(self, src, sem):
         if self.line:
 
             @pl.when(self.middle)
             def _():
-                far = jnp.clip(self.far, 0, 3)
-                self.copy(self.piece, far, far, 4).wait_recv()
-                self.passed().start()
+                self.copy(self.piece, src, src, sem).wait_recv()
+                self.passed(src, sem).start()
 
     def finish(self):
         z, n = self.place.z, self.place.ndp
@@ -179,7 +266,7 @@
             src = lax.rem(z + i, n)
             wait = self.copy(self.piece, src, src, 0).wait_recv
             if self.line:
-                pl.when(jnp.logical_not(jnp.logical_and(self.middle, src == self.far)))(wait)
+                pl.when(jnp.logical_or(self.end, src == self.near))(wait)
             else:
                 wait()
         for ok, copy in self.directs():
@@ -188,12 +275,17 @@
             else:
                 pl.when(ok)(copy.wait_send)
         if self.line:
-            pl.when(self.middle)(self.passed().wait_send)
+
+            @pl.when(self.middle)
+            def _():
+                self.passed(self.other, 4).wait_send()
+                self.passed(self.far, 5).wait_send()
+
         self.keep().wait()
 
 
 def depth_sems(ndp):
-    return [DMA((ndp + 1,)), DMA((ndp,)), DMA]
+    return [DMA((max(ndp, 6),)), DMA((ndp,)), DMA]
 
 
 STEP = 16
@@ -245,24 +337,32 @@
             self.place.same_core(self.place.chip(i + 1)),
         )
 
+    def chip_of(self, i):
+        return lax.rem(self.place.p + 1 + i, self.place.nchip)
+
+    def hand_on(self, i):
+        self.pair(i).wait_recv()
+
+        def add(at):
+            both = self.mine[lax.rem(i, 2), at, :] + self.from_pair[i, at, :].astype(jnp.float32)
+            self.to_chip[i, at, :] = both.astype(jnp.bfloat16)
+
+        row_loop(self.rows, add)
+        self.chips(i).start()
+
+    def last(self):
+        nchip = self.place.nchip
+        self.pair(nchip - 1).wait_recv()
+        for i in range(nchip - 1):
+            self.chips(i).wait_recv()
+
     def run(self):
         place, rows, tile = self.place, self.rows, self.TILE
         nchip = place.nchip
         width = self.mine.shape[-1]
 
-        def hand_on(i):
-            self.pair(i).wait_recv()
-
-            def add(at):
-                both = self.mine[lax.rem(i, 2), at, :] + self.from_pair[i, at, :].astype(jnp.float32)
-                self.to_chip[i, at, :] = both.astype(jnp.bfloat16)
-
-            row_loop(rows, add)
-            self.chips(i).start()
-
         def step(i, carry):
-            q = lax.rem(place.p + 1 + i, nchip)
-            first = pl.multiple_of(q * 2 * rows, 2 * rows)
+            first = pl.multiple_of(self.chip_of(i) * 2 * rows, 2 * rows)
             slot = lax.rem(i, 2)
             pl.when(i >= 2)(lambda: self.pair(i - 2).wait_send())
 
@@ -284,13 +384,11 @@
 
             lax.fori_loop(0, width // tile, columns, 0)
             self.pair(i).start()
-            pl.when(i > 0)(lambda: hand_on(i - 1))
+            pl.when(i > 0)(lambda: self.hand_on(i - 1))
             return carry
 
         lax.fori_loop(0, nchip, step, 0)
-        self.pair(nchip - 1).wait_recv()
-        for i in range(nchip - 1):
-            self.chips(i).wait_recv()
+        self.last()
 
     def total(self, at):
         last = self.place.nchip - 1
@@ -304,6 +402,87 @@
             self.pair(i).wait_send()
         for i in range(self.place.nchip - 1):
             self.chips(i).wait_send()
+
+
+class BoxScatter(SumScatter):
+    def near(self, axis):
+        p = self.place.p
+        x, y = lax.rem(p, 2), lax.div(p, 2)
+        return self.place.same_core(2 * y + 1 - x if axis == 0 else 2 * (1 - y) + x)
+
+    def half(self, src, dst, rows, sem, axis):
+        size = self.rows // 2
+        at = pl.ds(rows * size, size)
+        return push(
+            self.to_chip.at[src, at], self.from_chip.at[dst, at], self.chip_send.at[sem], self.chip_recv.at[sem], self.near(axis)
+        )
+
+    def moves(self):
+        return [
+            self.half(0, 2, 0, 0, 0),
+            self.half(0, 2, 1, 1, 1),
+            self.half(1, 0, 0, 2, 0),
+            self.half(2, 1, 1, 3, 1),
+            self.half(1, 0, 1, 4, 0),
+            self.half(2, 1, 0, 5, 1),
+        ]
+
+    def chip_of(self, i):
+        p = self.place.p
+        x, y = lax.rem(p, 2), lax.div(p, 2)
+        other_x = jnp.logical_or(i == 0, i == 1)
+        other_y = jnp.logical_or(i == 0, i == 2)
+        return 2 * jnp.where(other_y, 1 - y, y) + jnp.where(other_x, 1 - x, x)
+
+    def hand_on(self, i):
+        self.pair(i).wait_recv()
+        slot = lax.rem(i, 2)
+
+        def add(at):
+            both = self.mine[slot, at, :] + self.from_pair[i, at, :].astype(jnp.float32)
+            self.to_chip[i, at, :] = both.astype(jnp.bfloat16)
+
+        row_loop(self.rows, add)
+        moves = self.moves()
+
+        @pl.when(i == 0)
+        def _():
+            moves[0].start()
+            moves[1].start()
+
+        pl.when(i == 1)(moves[2].start)
+        pl.when(i == 2)(moves[3].start)
+
+    def last(self):
+        moves = self.moves()
+        size = self.rows // 2
+        for arrived, src, first, onward in ((1, 1, size, 4), (0, 2, 0, 5)):
+            moves[arrived].wait_recv()
+
+            def add(at, src=src, first=first):
+                at = pl.ds(pl.multiple_of(first + at.start, STEP), STEP)
+                both = self.to_chip[src, at, :].astype(jnp.float32) + self.from_chip[2, at, :].astype(jnp.float32)
+                self.to_chip[src, at, :] = both.astype(jnp.bfloat16)
+
+            row_loop(size, add)
+            moves[onward].start()
+        self.pair(3).wait_recv()
+        for n in (2, 3, 4, 5):
+            moves[n].wait_recv()
+
+    def total(self, at):
+        value = self.mine[1, at, :] + self.from_pair[3, at, :].astype(jnp.float32)
+        return value + self.from_chip[0, at, :].astype(jnp.float32) + self.from_chip[1, at, :].astype(jnp.float32)
+
+    def finish(self):
+        for i in (2, 3):
+            self.pair(i).wait_send()
+        for copy in self.moves():
+            copy.wait_send()
+
+
+def sum_scatter(place, *args):
+    return (BoxScatter if place.nchip == 4 else SumScatter)(place, *args)
 
 
 def scatter_scratch(nctx, rows, d):
@@ -317,8 +496,8 @@
         pltpu.VMEM((n - 1, rows, d), bf16),
         DMA((n,)),
         DMA((n,)),
-        DMA((n - 1,)),
-        DMA((n - 1,)),
+        DMA((6 if n == 4 else n - 1,)),
+        DMA((6 if n == 4 else n - 1,)),
     ]
 
 
@@ -335,15 +514,15 @@
 ):
     place = Place()
     greet(place)
-    scatter = SumScatter(
+    scatter = sum_scatter(
         place,
         resid_ref.shape[0],
-        lambda rows, cols: dot_nt(gate_ref[rows, :], w_ref[0, cols, :]) + dot_nt(up_ref[rows, :], w_ref[1, cols, :]),
+        lambda rows, cols: dot_nn(gate_ref[rows, :], w_ref[0, :, cols]) + dot_nn(up_ref[rows, :], w_ref[1, :, cols]),
         *scratch[:5],
         scratch[5:9],
     )
     scatter.run()
-    gain = gain_ref[...].astype(jnp.float32)
+    gain = gain_ref[...].astype(jnp.float32)[None, :]
     vec_ref[...] = jnp.zeros_like(vec_ref)
 
     def back(at):
@@ -356,7 +535,7 @@
         block[at, :] = out.astype(jnp.bfloat16)
 
     row_loop(resid_ref.shape[0], back)
-    rows = RowGather(place, block, grad_all, *scratch[9:12])
+    rows = row_gather(place, block, grad_all, *scratch[9:12])
     rows.start()
     rows.forward()
     rows.finish()
@@ -381,7 +560,7 @@
         compiler_params=pltpu.CompilerParams(collective_id=2, has_side_effects=True),
         cost_estimate=pl.CostEstimate(flops=0, bytes_accessed=150_000_000, transcendentals=0),
         name="mlp_back",
-    )(gate_grad, up_grad, w, resid, cot, gain[None, :])
+    )(gate_grad, up_grad, w, resid, cot, gain)
 
 
 def attn_back_kernel(parts_ref, w_ref, x_ref, grad_ref, gain_ref, out_ref, vec_ref, *scratch):
@@ -393,9 +572,9 @@
         part = part + dot_nt(parts_ref[1, rows, :], w_ref[1, cols, :])
         return part + dot_nt(parts_ref[2, rows, :], w_ref[2, cols, :])
 
-    scatter = SumScatter(place, x_ref.shape[0], product, *scratch[:5], scratch[5:9])
+    scatter = sum_scatter(place, x_ref.shape[0], product, *scratch[:5], scratch[5:9])
     scatter.run()
-    gain = gain_ref[...].astype(jnp.float32)
+    gain = gain_ref[...].astype(jnp.float32)[None, :]
     vec_ref[...] = jnp.zeros_like(vec_ref)
 
     def back(at):
@@ -424,13 +603,13 @@
         compiler_params=pltpu.CompilerParams(collective_id=3, has_side_effects=True),
         cost_estimate=pl.CostEstimate(flops=0, bytes_accessed=100_000_000, transcendentals=0),
         name="attn_back",
-    )(parts, w, x, grad, gain[None, :])
+    )(parts, w, x, grad, gain)
 
 
 def down_kernel(hidden_ref, w_ref, resid_ref, out_ref, *scratch):
     place = Place()
     greet(place)
-    scatter = SumScatter(
+    scatter = sum_scatter(
         place,
         resid_ref.shape[0],
         lambda rows, cols: dot_nn(hidden_ref[rows, :], w_ref[:, cols]),
@@ -618,9 +797,9 @@
 
     def from_middle(self):
         return [
-            self.copy(self.block(self.near), 0, 0, self.near),
-            self.copy(self.both.at[0], 1, 1, 3 - self.near),
-            self.copy(self.both.at[1], 1, 2, self.other),
+            self.copy(self.both.at[0], 4, 0, self.other),
+            self.copy(self.both.at[1], 1, 1, self.other),
+            self.copy(self.both.at[2], 0, 2, self.near),
         ]
 
     def across(self):
@@ -638,29 +817,24 @@
             for copy in self.from_end():
                 copy.start()
 
+    def hand_on(self, n):
+        if not self.line:
+            return
+
         @pl.when(self.middle)
         def _():
-            self.from_middle()[0].start()
-
-    def hand_on(self):
-        if not self.line:
-            return
-
-        @pl.when(self.middle)
-        def _():
-            for j, owner in enumerate((3 - self.near, self.other)):
-                self.copy(self.both.at[0], 2 + j, 0, self.near).wait_recv()
-                cols = pl.ds(pl.multiple_of(owner * self.width, self.width), self.width)
-
-                def add(at, j=j, cols=cols):
-                    total = self.part[at, cols].astype(jnp.float32) + self.got[2 + j, at, :].astype(jnp.float32)
-                    self.both[j, at, :] = total.astype(jnp.bfloat16)
-
-                row_loop(self.part.shape[0], add)
-                self.from_middle()[1 + j].start()
-
-    def finish(self, out_ref):
-        count = 2 if self.line else self.place.ndp - 1
+            owner, slot = ((3 - self.near, 2), (self.other, 3), (self.near, 4))[n]
+            self.copy(self.both.at[0], slot, 0, self.near).wait_recv()
+            cols = pl.ds(pl.multiple_of(owner * self.width, self.width), self.width)
+
+            def add(at):
+                total = self.part[at, cols].astype(jnp.float32) + self.got[slot, at, :].astype(jnp.float32)
+                self.both[n, at, :] = total.astype(jnp.bfloat16)
+
+            row_loop(self.part.shape[0], add)
+            self.from_middle()[n].start()
+
+    def collect(self, count, out_ref):
         for slot in range(count):
             self.copy(self.got.at[slot], slot, 0, self.next).wait_recv()
         cols = pl.ds(pl.multiple_of(self.place.z * self.width, self.width), self.width)
@@ -672,39 +846,60 @@
             out_ref[at, :] = value
 
         row_loop(self.part.shape[0], add)
+
+    def finish(self, out_ref):
         if not self.line:
+            self.collect(self.place.ndp - 1, out_ref)
             for copy in self.across():
                 copy.wait_send()
             return
 
         @pl.when(self.end)
         def _():
+            self.collect(1, out_ref)
             for copy in self.from_end():
                 copy.wait_send()
 
         @pl.when(self.middle)
         def _():
+            self.collect(2, out_ref)
             for copy in self.from_middle():
                 copy.wait_send()
 
 
 def depth_scatter_scratch(ndp, rows, width):
-    slots = 4 if ndp == 4 else ndp - 1
+    slots = 5 if ndp == 4 else ndp - 1
     return [
         pltpu.VMEM((slots, rows, width), jnp.bfloat16),
-        pltpu.VMEM((2, rows, width), jnp.bfloat16),
+        pltpu.VMEM((3, rows, width), jnp.bfloat16),
         DMA((max(slots, 3),)),
         DMA((slots,)),
     ]
 
 
+def tables(perm_ref, cos_ref, sin_ref, pos_col, pos_row, size):
+    seq = pos_row.shape[1]
+    lane = lax.broadcasted_iota(jnp.int32, (8, seq), 1)
+    group = lane // size
+    start = jnp.zeros((8, seq), jnp.int32)
+    for g in range(seq // size):
+        start = jnp.where(group == g, perm_ref[0, g], start)
+    pos = (start * size + lane - group * size).astype(jnp.float32)
+    pos_row[...] = pos[0:1]
+    pos_col[...] = pos.T[:, 0:1]
+    step = lax.broadcasted_iota(jnp.int32, (8, seq), 0).astype(jnp.float32)
+    angle = pos * jnp.exp(step * (-2.0 / ROT * math.log(rope_base)))
+    cos_ref[...] = jnp.cos(angle)
+    sin_ref[...] = jnp.sin(angle)
+
+
 def forward_kernel(
-    x_ref, cot_ref, gain1_ref, bias1_ref, gain2_ref, bias2_ref, shift_ref, cos_ref, sin_ref, pos_col, pos_row,
+    perm_ref, x_ref, cot_ref, gain1_ref, bias1_ref, gain2_ref, bias2_ref, shift_ref,
     qkv_ref, out_ref, gateup_ref, down_ref,
-    resid_ref, q_t, k_t, v_t, attn_t, lse, hidden_ref, gate_side, up_side, down_grads,
-    rows_out, cots_out, qkv_out, out_out, normed_out, gateup_out, down_all,
-    row_block, cot_block, rows_all, cot_all, qkv_all, out_all, gateup_all,
-    k_n, bias, attn, gate_f, hidden_t, *sems
+    resid_ref, q_t, k_t, v_t, attn_t, lse, hidden_ref, gate_side, up_side, down_grads, cos_ref, sin_ref, pos_col, pos_row,
+    rows_out, qkv_out, out_out, gateup_out, down_out, grads_out,
+    row_block, cot_block, rows_all, cot_all, qkv_all, out_all, gateup_all, down_all,
+    k_n, bias, attn, gate_f, hidden_t, up_t, part, shifts, *sems
 ):
     f32, bf16 = jnp.float32, jnp.bfloat16
     place = Place()
@@ -725,36 +920,35 @@
     depth, width = qkv_ref.shape[1], out_ref.shape[1]
 
     def half(i):
-        return lambda ref, z: ref.at[i, pl.ds(pl.multiple_of(z * depth, depth), depth), :]
+        return lambda ref, z: ref.at[i, :, pl.ds(pl.multiple_of(z * depth, depth), depth)]
 
     qkv = DepthGather(place, qkv_ref, qkv_all, along_rows(depth), *take(3))
-    out = DepthGather(place, out_ref, out_all, along_lanes(width), *take(3))
+    out = DepthGather(place, out_ref, out_all, along_lanes(width), *take(3), passing=False)
     gate = DepthGather(place, gateup_ref.at[0], gateup_all, half(0), *take(3))
     up = DepthGather(place, gateup_ref.at[1], gateup_all, half(1), *take(3))
     down = DepthGather(place, down_ref, down_all, along_lanes(width), *take(3))
-    rows = RowGather(place, row_block, rows_all, *take(3))
-    cots = RowGather(place, cot_block, cot_all, *take(3))
-    normeds = RowGather(place, row_block, rows_all, *take(3))
+    rows = row_gather(place, row_block, rows_all, *take(3))
+    cots = row_gather(place, cot_block, cot_all, *take(3))
+    normeds = row_gather(place, row_block, rows_all, *take(3))
     scatter_refs = take(9)
     got, both, dsend, drecv = take(4)
     (save_sem,) = take(1)
-    seq = rows_all.shape[0]
+    seq, d = rows_all.shape
 
     def save(i, src, dst):
         return pltpu.make_async_copy(src, dst, save_sem.at[i])
 
     saves = [
         save(0, rows_all, rows_out),
-        save(1, cot_all, cots_out),
-        save(2, qkv_all, qkv_out),
-        save(3, out_all, out_out),
-        save(4, rows_all, normed_out),
-        save(5, gateup_all, gateup_out),
+        save(1, qkv_all, qkv_out),
+        save(2, out_all, out_out),
+        save(3, gateup_all, gateup_out),
+        save(4, down_all, down_out),
+        save(5, gateup_all, grads_out),
     ]
 
     qkv.start()
-    out.start()
-    gain, shift = gain1_ref[...].astype(f32), bias1_ref[...].astype(f32)
+    gain, shift = gain1_ref[...].astype(f32)[None, :], bias1_ref[...].astype(f32)[None, :]
 
     def norm1(at):
         normed, _ = normal(x_ref[at, :].astype(f32))
@@ -764,23 +958,27 @@
     row_loop(x_ref.shape[0], norm1)
     rows.start()
     cots.start()
+    head = qkv_ref.shape[2]
+    shifts[...] = shift_ref[:, pl.ds(pl.multiple_of(place.c * head, head), head)].astype(f32)
+    tables(perm_ref, cos_ref, sin_ref, pos_col, pos_row, x_ref.shape[0] // 2)
     rows.forward()
-    qkv.forward()
+    qkv.forward_next()
     cots.forward()
-    out.forward()
+    qkv.forward_far()
+    out.start()
     gate.start()
     up.start()
     rows.finish()
     saves[0].start()
     cots.finish()
+    qkv.finish()
     saves[1].start()
-    qkv.finish()
+    attend(rows_all, qkv_all, shifts, cos_ref, sin_ref, pos_col, pos_row, q_t, k_t, v_t, attn_t, lse, k_n, bias, attn)
+    gate.forward_next()
+    out.finish()
     saves[2].start()
-    attend(rows_all, qkv_all, shift_ref, cos_ref, sin_ref, pos_col, pos_row, q_t, k_t, v_t, attn_t, lse, k_n, bias, attn)
-    out.finish()
-    saves[3].start()
     saves[0].wait()
-    scatter = SumScatter(
+    scatter = sum_scatter(
         place,
         x_ref.shape[0],
         lambda at, cols: dot_nn(attn[at, :], out_all[:, cols]),
@@ -788,7 +986,8 @@
         scatter_refs[5:9],
     )
     scatter.run()
-    gain2, shift2 = gain2_ref[...].astype(f32), bias2_ref[...].astype(f32)
+    up.forward_next()
+    gain2, shift2 = gain2_ref[...].astype(f32)[None, :], bias2_ref[...].astype(f32)[None, :]
 
     def norm2(at):
         resid = x_ref[at, :].astype(f32) + scatter.total(at)
@@ -798,26 +997,26 @@
 
     row_loop(x_ref.shape[0], norm2)
     normeds.start()
-    gate.forward()
+    gate.forward_far()
     normeds.forward()
-    up.forward()
+    up.forward_far()
     down.start()
     normeds.finish()
-    saves[4].start()
     scatter.finish()
     gate.finish()
 
     def gates(t):
         at = span(t, PAIR)
-        gate_f[at, :] = dot_nn(rows_all[at, :], gateup_all[0])
+        gate_f[at, :] = dot_nt(rows_all[at, :], gateup_all[0])
 
     tiles(seq // PAIR, gates)
+    down.forward_next()
     up.finish()
-    saves[5].start()
+    saves[3].start()
 
     def ups(t):
         at = span(t, PAIR)
-        value = dot_nn(rows_all[at, :], gateup_all[1])
+        value = dot_nt(rows_all[at, :], gateup_all[1])
         g = gate_f[at, :]
         sigma = jax.nn.sigmoid(g)
         swish = g * sigma
@@ -828,31 +1027,54 @@
         up_side[at, :] = swish.astype(bf16)
 
     tiles(seq // PAIR, ups)
-    saves[4].wait()
-    part = rows_all.at[: hidden_t.shape[0]]
-
-    def weights(j):
+
+    def down_weights(j):
         cols = span(j, 2 * PAIR)
         part[:, cols] = dot_nn(hidden_t[...], cot_all[:, cols]).astype(bf16)
 
-    tiles(cot_all.shape[1] // (2 * PAIR), weights)
+    tiles(d // (2 * PAIR), down_weights)
     summed = DepthScatter(place, part, got, both, width, dsend, drecv)
     summed.start()
-    down.forward()
-    summed.hand_on()
+    down.forward_far()
+    summed.hand_on(0)
+    summed.hand_on(1)
+    down.finish()
+    saves[4].start()
+    summed.hand_on(2)
+    saves[3].wait()
+
+    def sides(t):
+        at = span(t, PAIR)
+        grad = dot_nt(cot_all[at, :], down_all[...])
+        gate_grad = (grad * gate_side[at, :].astype(f32)).astype(bf16)
+        up_grad = (grad * up_side[at, :].astype(f32)).astype(bf16)
+        gate_side[at, :] = gate_grad
+        up_side[at, :] = up_grad
+        hidden_t[:, at] = gate_grad.T
+        up_t[:, at] = up_grad.T
+
+    tiles(seq // PAIR, sides)
+
+    def gateup_weights(j):
+        cols = span(j, 2 * PAIR)
+        normed = rows_all[:, cols]
+        gateup_all[0, :, cols] = dot_nn(hidden_t[...], normed).astype(bf16)
+        gateup_all[1, :, cols] = dot_nn(up_t[...], normed).astype(bf16)
+
+    tiles(d // (2 * PAIR), gateup_weights)
+    saves[5].start()
     summed.finish(down_grads)
-    down.finish()
-    for i in (1, 2, 3, 5):
+    for i in (1, 2, 4, 5):
         saves[i].wait()
 
 
-def forward(x, cot, gain1, bias1, gain2, bias2, shift, cosine, sine, pos_col, pos_row, qkv, out, gateup, down):
+def forward(perm, x, cot, gain1, bias1, gain2, bias2, shift, qkv, out, gateup, down):
     ndp, nctx = lax.axis_size("dp"), lax.axis_size("ctx")
     rows, d = x.shape
-    seq, width, ff = rows * nctx, qkv.shape[2], gateup.shape[2]
+    seq, width, ff = rows * nctx, qkv.shape[2], gateup.shape[1]
     heads = width // HEAD_DIM
     bf16, f32 = jnp.bfloat16, jnp.float32
-    row = [v[None, :] for v in (gain1, bias1, gain2, bias2)]
+    row = [gain1, bias1, gain2, bias2]
 
     def shaped(shape, dtype=bf16):
         return jax.ShapeDtypeStruct(shape, dtype)
@@ -870,16 +1092,19 @@
             shaped((seq, ff)),
             shaped((seq, ff)),
             shaped(down.shape, f32),
-            shaped((seq, d)),
+            shaped((8, seq), f32),
+            shaped((8, seq), f32),
+            shaped((seq, 1), f32),
+            shaped((1, seq), f32),
             shaped((seq, d)),
             shaped((3, d, width)),
             shaped((width, d)),
-            shaped((seq, d)),
-            shaped((2, d, ff)),
+            shaped((2, ff, d)),
             shaped((ff, d)),
+            shaped((2, ff, d)),
         ),
-        in_specs=[VMEM] * 15,
-        out_specs=(VMEM,) * 10 + (ANY,) * 7,
+        in_specs=[pl.BlockSpec(memory_space=pltpu.SMEM)] + [VMEM] * 7 + [ANY] * 4,
+        out_specs=(VMEM,) * 14 + (ANY,) * 6,
         scratch_shapes=[
             pltpu.VMEM((rows, d), bf16),
             pltpu.VMEM((rows, d), bf16),
@@ -887,12 +1112,16 @@
             pltpu.VMEM((seq, d), bf16),
             pltpu.VMEM((3, d, width), bf16),
             pltpu.VMEM((width, d), bf16),
-            pltpu.VMEM((2, d, ff), bf16),
+            pltpu.VMEM((2, ff, d), bf16),
+            pltpu.VMEM((ff, d), bf16),
             pltpu.VMEM((heads, seq, HEAD_DIM), bf16),
             pltpu.VMEM((seq, PAIR), f32),
             pltpu.VMEM((seq, width), bf16),
             pltpu.VMEM((seq, ff), f32),
             pltpu.VMEM((ff, seq), bf16),
+            pltpu.VMEM((ff, seq), bf16),
+            pltpu.VMEM((ff, d), bf16),
+            pltpu.VMEM((3, width), f32),
         ]
         + depth_sems(ndp) * 5
         + gather_sems(nctx) * 3
@@ -904,7 +1133,7 @@
         ),
         cost_estimate=pl.CostEstimate(flops=0, bytes_accessed=700_000_000, transcendentals=0),
         name="forward",
-    )(x, cot, *row, shift, cosine, sine, pos_col, pos_row, qkv, out, gateup, down)
+    )(perm, x, cot, *row, shift, qkv, out, gateup, down)
 
 
 def attend_back_kernel(
@@ -996,23 +1225,8 @@
     )(grad_all, w, rows_all, cosine, sine, pos_col, pos_row, q_t, k_t, v_t, attn_t, lse)
 
 
-def rope_tables(positions):
-    exponent = jnp.arange(HALF, dtype=jnp.float32) * (2.0 / ROT)
-    inverse = jnp.exp(-exponent * math.log(rope_base))
-    angle_val = inverse[:, None] * positions.astype(jnp.float32)[None, :]
-    return (jnp.cos(angle_val), jnp.sin(angle_val))
-
-
-def group_positions(group_order, count, half_group):
-    row_ids = jnp.arange(count, dtype=jnp.int32)
-    group_ids = row_ids // half_group
-    matches = group_ids[:, None] == jnp.arange(group_order.shape[0], dtype=jnp.int32)[None, :]
-    group_start = jnp.sum(jnp.where(matches, group_order[None, :], 0), axis=1)
-    return group_start * half_group + row_ids % half_group
-
-
-def shard(grad):
-    return lax.psum_scatter(grad, "dp", scatter_dimension=1, tiled=True)
+def shard(grad, dim):
+    return lax.psum_scatter(grad, "dp", scatter_dimension=dim, tiled=True)
 
 
 def per_device(
@@ -1029,45 +1243,25 @@
     gateup_weight,
     down_weight,
 ):
-    f32 = jnp.float32
-    bf16 = jnp.bfloat16
-    tok_rows = block_input.shape[0]
-    cycle_size = lax.axis_size("ctx")
-    cycle_index = lax.axis_index("ctx")
-    seq_len = tok_rows * cycle_size
-    half_group = tok_rows // 2
-    group_order = group_perm[0]
-    qkv_shift = qkv_bias.astype(f32)
-    all_pos = group_positions(group_order, seq_len, half_group)
-    cos_all, sin_all = rope_tables(all_pos)
-    pos_f = all_pos.astype(f32)
-    pos_col, pos_row = pos_f[:, None], pos_f[None, :]
     width_local = qkv_weight.shape[2]
-    head_first = cycle_index * width_local
-    shift_local = lax.dynamic_slice_in_dim(qkv_shift, head_first, width_local, 1)
     (
-        residual_stream, q_t, k_t, v_t, attn_t, lse, hidden_b, gate_side, up_side, down_grads,
-        rows_all, cot_all, qkv_local, out_local, mlp_all, gateup_local, down_local,
+        residual_stream, q_t, k_t, v_t, attn_t, lse, hidden_b, gate_grad, up_grad, down_grads, cos_all, sin_all, pos_col, pos_row,
+        rows_all, qkv_local, out_local, gateup_local, down_local, gateup_grads,
     ) = forward(
-        block_input, out_cotangent, attn_norm_gain, attn_norm_bias, mlp_norm_gain, mlp_norm_bias, shift_local,
-        cos_all, sin_all, pos_col, pos_row, qkv_weight, out_weight, gateup_weight, down_weight,
+        group_perm, block_input, out_cotangent, attn_norm_gain, attn_norm_bias, mlp_norm_gain, mlp_norm_bias, qkv_bias,
+        qkv_weight, out_weight, gateup_weight.transpose(0, 2, 1), down_weight,
     )
-    hidden_grad = jnp.dot(cot_all, down_local.T, preferred_element_type=f32)
-    gate_grad = (hidden_grad * gate_side.astype(f32)).astype(bf16)
-    up_grad = (hidden_grad * up_side.astype(f32)).astype(bf16)
-    gateup_w_grad = jnp.einsum(
-        "td,ktf->kdf", mlp_all, jnp.stack([gate_grad, up_grad]), preferred_element_type=f32
-    ).astype(bf16)
-    gate_grad, up_grad, gateup_w_grad = lax.optimization_barrier((gate_grad, up_grad, gateup_w_grad))
-    gateup_grads = shard(gateup_w_grad)
+    gateup_grads = shard(gateup_grads, 2)
     resid_grad, second_vectors, resid_all = mlp_back(
         gate_grad, up_grad, gateup_local, residual_stream, out_cotangent, mlp_norm_gain
     )
     grad_parts_b, shift_part, attn_grads = attention_back(
         resid_all, out_local, rows_all, cos_all, sin_all, pos_col, pos_row, q_t, k_t, v_t, attn_t, lse
     )
+    head_first = lax.axis_index("ctx") * width_local
+    f32 = jnp.float32
     shift_grad = lax.dynamic_update_slice_in_dim(jnp.zeros((3, D), f32), shift_part, head_first, 1)
-    attn_grads = shard(attn_grads)
+    attn_grads = shard(attn_grads, 1)
     input_grad, first_vectors = attn_back(grad_parts_b, qkv_local, block_input, resid_grad, attn_norm_gain)
     hidden_late, first_vectors, gateup_grads = lax.optimization_barrier((hidden_b, first_vectors, gateup_grads))
     block_output = down(hidden_late, down_local, residual_stream)
@@ -1086,7 +1280,7 @@
         attn_grads[3].T,
         small[2],
         small[3],
-        gateup_grads.astype(f32),
+        gateup_grads.astype(f32).transpose(0, 2, 1),
         down_grads,
     )
 

time: 512 us -> 458 us (0.89)
  Pallas kernels: 459 us -> 408 us
  waiting for transfers between devices: 0.08 us -> 23.9 us
  matrix products: 16 us -> 0 us
  local copies, waits for them, and re-layouts: 13.2 us -> 7.81 us
    pallas_call x1, Pallas kernels: 276 us -> 250 us  [forward(): pl.pallas_call(forward_kernel, out_shape=(shaped((rows, d), f32), shaped(...]
    reduce_scatter x2, waiting for transfers between devices: 0.04 us -> 23.9 us  [shard(): return lax.psum_scatter(grad, 'dp', scatter_dimension=dim, tiled=True)]
    dot_general x2 -> x0, matrix products: 16 us -> none  [the longest x1 8.39 us: per_device(): jnp.einsum('td,ktf->kdf', mlp_all, jnp.stack([gate_grad, up_grad]), prefe...]
    pallas_call x1, Pallas kernels: 68.7 us -> 52.8 us  [mlp_back(): pl.pallas_call(mlp_back_kernel, out_shape=(jax.ShapeDtypeStruct((rows, d)...]
    pallas_call x1, Pallas kernels: 34.8 us -> 28.2 us  [down(): pl.pallas_call(down_kernel, out_shape=jax.ShapeDtypeStruct((rows, d), jnp...]
    pallas_call x1, Pallas kernels: 36.4 us -> 30.9 us  [attn_back(): pl.pallas_call(attn_back_kernel, out_shape=(jax.ShapeDtypeStruct((rows, d...]
  transfers between devices with their start and end apart: 2 -> 2, of which waited for: 0 -> 1; matrix products, arithmetic and copies ran while one was open for 0% -> 0% of each run, Pallas kernels for 36% -> 35%
where the time goes in v4:
time: 458 us
  Pallas kernels  408 us (89%)
  waiting for transfers between devices  23.9 us (5%)
  between operations  14.2 us (3%)
  local copies, waits for them, and re-layouts  7.81 us (2%)
    pallas_call x1, Pallas kernels, forward(): pl.pallas_call(forward_kernel, out_shape=(shaped((rows, d), f32), shaped(...  250 us
    pallas_call x1, Pallas kernels, mlp_back(): pl.pallas_call(mlp_back_kernel, out_shape=(jax.ShapeDtypeStruct((rows, d)...  52.8 us
    pallas_call x1, Pallas kernels, attn_back(): pl.pallas_call(attn_back_kernel, out_shape=(jax.ShapeDtypeStruct((rows, d...  30.9 us
    pallas_call x1, Pallas kernels, down(): pl.pallas_call(down_kernel, out_shape=jax.ShapeDtypeStruct((rows, d), jnp...  28.2 us
    pallas_call x1, Pallas kernels, attention_back(): pl.pallas_call(attend_back_kernel, out_shape=(jax.ShapeDtypeStruct((3, se...  26.4 us
    reduce_scatter x2, waiting for transfers between devices, shard(): return lax.psum_scatter(grad, 'dp', scatter_dimension=dim, tiled=True)  23.9 us
    pallas_call x1, Pallas kernels, sum_vectors(): pl.pallas_call(vectors_kernel, out_shape=jax.ShapeDtypeStruct(v.shape, f3...  20.5 us
  transfers between devices with their start and end apart: 2, of which 1 were waited for; matrix products, arithmetic and copies ran while one was open for 0% of the time, Pallas kernels for 35%

profile of v4, /device:TPU:0, one launch (start us, length us, event | category | flops | bytes accessed | tf_op | source)
XLA Modules:
  0.0 458.1 jit_solution(4127232429345664534)
XLA Ops:
  7.2 0.0 reduce-scatter.3.cloned.1.call-start
  7.2 249.7 %forward.1 = (f32[128,2048]{1,0:T(8,128)}, bf16[256,1024]{1,0:T(8,128)(2,1)}, bf16[256,1024]{1,0:T(8,128)(2,1)}, bf16[256,1024]{1,0:T(8,128)(2,1)}, bf16[256,102...) custom-call(s32[1,16]{1,0:T(1,128)} %perm_ref.1, ...), custom_call_target="tpu_custom_call" | custom-call | bytes 700000000 | tf_op jit(solution)/shard_map/forward/pallas_call | solution.py:1082
  256.9 0.0 reduce-scatter.3.cloned.1.call-update
  256.9 0.2 reduce-scatter.5.cloned.1.call-start
  257.2 52.8 %mlp_back.1 = (f32[128,2048]{1,0:T(8,128)}, f32[2,2048]{1,0:T(2,128)}, bf16[1024,2048]{1,0:T(8,128)(2,1)}) custom-call(bf16[1024,704]{1,0:T(8,128)(2,1)} %get-tuple-element.46.gate_ref, bf16[1024,704]{1,0:T(8,128)(2,1)} %get-tuple-element.47.up_ref, bf16[2,704,2048]{2,1,0:T(8,128)(2,1)} %get-tuple-element.48.w_ref, f32[128,2048]{1,0:T(8,128)} %get-tuple-element.49.resid_ref, ...), custom_call_target="tpu_custom_call" | custom-call | bytes 150000000 | tf_op jit(solution)/shard_map/mlp_back/pallas_call | solution.py:548
  309.9 26.4 %attention_back.1 = (bf16[3,1024,256]{2,1,0:T(8,128)(2,1)}, f32[3,256]{1,0:T(4,128)}, bf16[4,2048,256]{2,1,0:T(8,128)(2,1)}) custom-call(bf16[1024,2048]{1,0:T(8,128)(2,1)} %get-tuple-element.50.grad_ref, bf16[256,2048]{1,0:T(8,128)(2,1)} %get-tuple-element.51.w_ref, bf16[1024,2048]{1,0:T(8,128)(2,1)} %get-tuple-element.52.rows_ref, ...), custom_call_target="tpu_custom_call" | custom-call | bytes 120000000 | tf_op jit(solution)/shard_map/attention_back/pallas_call | solution.py:1206
  336.4 0.0 reduce-scatter.5.cloned.1.call-update
  336.4 0.0 copy-start.7
  336.4 0.0 copy-start.6
  336.4 30.9 %attn_back.1 = (f32[128,2048]{1,0:T(8,128)}, f32[2,2048]{1,0:T(2,128)}) custom-call(bf16[3,1024,256]{2,1,0:T(8,128)(2,1)} %get-tuple-element.62.parts_ref, bf16[3,2048,256]{2,1,0:T(8,128)(2,1)} %get-tuple-element.63.w_ref, bf16[128,2048]{1,0:T(8,128)(2,1)} %x_ref.3, f32[128,2048]{1,0:T(8,128)} %get-tuple-element.64.grad_ref, bf16[2048]{0:T(1024)(128)(2,1)} %gain_ref.3), custom_call_target="tpu_custom_call" | custom-call | bytes 100000000 | tf_op jit(solution)/shard_map/attn_back/pallas_call | solution.py:594
  367.3 0.1 pad.3.clone
  367.4 0.0 copy-done.7
  367.4 0.0 reduce-scatter.3.cloned.1.call-done
  367.5 0.0 copy-done.6
  367.5 1.4 maximum_maximum_fusion.v_ref
  368.9 20.5 %sum_vectors.1 = f32[8,2048]{1,0:T(8,128)} custom-call(f32[8,2048]{1,0:T(8,128)} %maximum_maximum_fusion.v_ref), custom_call_target="tpu_custom_call" | custom-call | bytes 30000000 | tf_op jit(solution)/shard_map/sum_vectors/pallas_call | solution.py:687
  389.4 0.0 copy-start.5
  389.4 28.2 %down_sum.1 = bf16[128,2048]{1,0:T(8,128)(2,1)} custom-call(bf16[1024,704]{1,0:T(8,128)(2,1)} %get-tuple-element.70.hidden_ref, bf16[704,2048]{1,0:T(8,128)(2,1)} %get-tuple-element.71.w_ref, f32[128,2048]{1,0:T(8,128)} %get-tuple-element.49.resid_ref), custom_call_target="tpu_custom_call" | custom-call | bytes 100000000 | tf_op jit(solution)/shard_map/down_sum/pallas_call | solution.py:631
  417.6 23.8 %reduce-scatter.5.cloned.1.call-done = bf16[4,512,256]{2,1,0:T(8,128)(2,1)} async-done(((bf16[4,2048,256]{2,1,0:T(8,128)(2,1)}), bf16[4,512,256]{2,1,0:T(8,128)(2,1)}) %reduce-scatter.5.cloned.1.call-update) | async-done | bytes 1048592 | tf_op jit(solution)/shard_map/reduce_scatter | solution.py:1229
  441.4 0.0 copy-done.5
  441.4 0.0 copy-start
  441.4 0.6 slice.24
  442.0 0.6 fusion
  442.7 2.4 slice.28
  445.1 0.0 copy-done
  445.1 0.0 copy-start.3
  445.1 0.2 convert_element_type.4
  445.3 1.0 copy.23
  446.3 0.1 copy-done.3
  446.4 0.0 copy-start.1
  446.4 0.0 copy-start.4
  446.4 2.0 convert_bitcast_fusion
  448.4 0.0 copy-start.2
  448.4 0.0 copy-done.1
  448.4 0.8 copy.28
  449.2 0.0 copy-done.4
  449.2 1.0 copy.29
  450.2 0.0 copy-done.2
  450.2 1.1 copy.30
  (3 shorter events, 0.1 us)
Async XLA Ops:
  7.2 360.3 %reduce-scatter.3.cloned.1.call-start = ((), (), s32[]{:S(2)}) async-start(), calls=%async_computation.2 | async-start | bytes 7208960 | tf_op jit(solution)/shard_map/reduce_scatter | solution.py:1229
  256.9 184.5 %reduce-scatter.5.cloned.1.call-start = ((), (), s32[]{:S(2)}) async-start(), calls=%async_computation.3 | async-start | bytes 5242880 | tf_op jit(solution)/shard_map/reduce_scatter | solution.py:1229
  336.4 31.0 %copy-start.7 = (f32[3,256]{1,0:T(4,128)S(1)}, f32[3,256]{1,0:T(4,128)}, u32[]{:S(2)}) copy-start(f32[3,256]{1,0:T(4,128)} %get-tuple-element.69) | copy-start | bytes 9220
  336.4 31.1 %copy-start.6 = (f32[2,2048]{1,0:T(2,128)S(1)}, f32[2,2048]{1,0:T(2,128)}, u32[]{:S(2)}) copy-start(f32[2,2048]{1,0:T(2,128)} %get-tuple-element.68) | copy-start | bytes 49156
  389.4 52.0 %copy-start.5 = (f32[8,2048]{1,0:T(8,128)S(1)}, f32[8,2048]{1,0:T(8,128)}, u32[]{:S(2)}) copy-start(f32[8,2048]{1,0:T(8,128)} %sum_vectors.1) | copy-start | bytes 196612
  441.4 3.7 copy-start
  445.1 1.4 copy-start.3
  446.4 2.0 copy-start.1
  446.4 2.8 copy-start.4
  448.4 1.8 copy-start.2
Sparse Core Ops, SparseCore 0:
  257.0 100.4 reduce-scatter.2
  359.8 81.5 reduce-scatter.4

commit v5 on v4

--- a/solution.py
+++ b/solution.py
@@ -350,13 +350,15 @@
         row_loop(self.rows, add)
         self.chips(i).start()
 
-    def last(self):
+    def last(self, hooks):
+        for hook in hooks:
+            hook()
         nchip = self.place.nchip
         self.pair(nchip - 1).wait_recv()
         for i in range(nchip - 1):
             self.chips(i).wait_recv()
 
-    def run(self):
+    def run(self, hooks=()):
         place, rows, tile = self.place, self.rows, self.TILE
         nchip = place.nchip
         width = self.mine.shape[-1]
@@ -388,7 +390,7 @@
             return carry
 
         lax.fori_loop(0, nchip, step, 0)
-        self.last()
+        self.last(list(hooks))
 
     def total(self, at):
         last = self.place.nchip - 1
@@ -453,10 +455,12 @@
         pl.when(i == 1)(moves[2].start)
         pl.when(i == 2)(moves[3].start)
 
-    def last(self):
+    def last(self, hooks):
         moves = self.moves()
         size = self.rows // 2
         for arrived, src, first, onward in ((1, 1, size, 4), (0, 2, 0, 5)):
+            if hooks:
+                hooks.pop(0)()
             moves[arrived].wait_recv()
 
             def add(at, src=src, first=first):
@@ -509,201 +513,6 @@
     return lax.dot_general(a, b, (((1,), (1,)), ((), ())), preferred_element_type=jnp.float32)
 
 
-def mlp_back_kernel(
-    gate_ref, up_ref, w_ref, resid_ref, cot_ref, gain_ref, grad_ref, vec_ref, grad_all, block, *scratch
-):
-    place = Place()
-    greet(place)
-    scatter = sum_scatter(
-        place,
-        resid_ref.shape[0],
-        lambda rows, cols: dot_nn(gate_ref[rows, :], w_ref[0, :, cols]) + dot_nn(up_ref[rows, :], w_ref[1, :, cols]),
-        *scratch[:5],
-        scratch[5:9],
-    )
-    scatter.run()
-    gain = gain_ref[...].astype(jnp.float32)[None, :]
-    vec_ref[...] = jnp.zeros_like(vec_ref)
-
-    def back(at):
-        grad = scatter.total(at)
-        normed, rscale = normal(resid_ref[at, :])
-        vec_ref[0:1, :] += jnp.sum(grad * normed, axis=0, keepdims=True)
-        vec_ref[1:2, :] += jnp.sum(grad, axis=0, keepdims=True)
-        out = cot_ref[at, :] + normal_back(grad, normed, rscale, gain)
-        grad_ref[at, :] = out
-        block[at, :] = out.astype(jnp.bfloat16)
-
-    row_loop(resid_ref.shape[0], back)
-    rows = row_gather(place, block, grad_all, *scratch[9:12])
-    rows.start()
-    rows.forward()
-    rows.finish()
-    scatter.finish()
-
-
-def mlp_back(gate_grad, up_grad, w, resid, cot, gain):
-    nctx = lax.axis_size("ctx")
-    rows, d = resid.shape
-    return pl.pallas_call(
-        mlp_back_kernel,
-        out_shape=(
-            jax.ShapeDtypeStruct((rows, d), jnp.float32),
-            jax.ShapeDtypeStruct((2, d), jnp.float32),
-            jax.ShapeDtypeStruct((rows * nctx, d), jnp.bfloat16),
-        ),
-        in_specs=[VMEM] * 6,
-        out_specs=(VMEM, VMEM, ANY),
-        scratch_shapes=[pltpu.VMEM((rows, d), jnp.bfloat16)]
-        + scatter_scratch(nctx, rows, d)
-        + gather_sems(nctx),
-        compiler_params=pltpu.CompilerParams(collective_id=2, has_side_effects=True),
-        cost_estimate=pl.CostEstimate(flops=0, bytes_accessed=150_000_000, transcendentals=0),
-        name="mlp_back",
-    )(gate_grad, up_grad, w, resid, cot, gain)
-
-
-def attn_back_kernel(parts_ref, w_ref, x_ref, grad_ref, gain_ref, out_ref, vec_ref, *scratch):
-    place = Place()
-    greet(place)
-
-    def product(rows, cols):
-        part = dot_nt(parts_ref[0, rows, :], w_ref[0, cols, :])
-        part = part + dot_nt(parts_ref[1, rows, :], w_ref[1, cols, :])
-        return part + dot_nt(parts_ref[2, rows, :], w_ref[2, cols, :])
-
-    scatter = sum_scatter(place, x_ref.shape[0], product, *scratch[:5], scratch[5:9])
-    scatter.run()
-    gain = gain_ref[...].astype(jnp.float32)[None, :]
-    vec_ref[...] = jnp.zeros_like(vec_ref)
-
-    def back(at):
-        grad = scatter.total(at)
-        normed, rscale = normal(x_ref[at, :].astype(jnp.float32))
-        vec_ref[0:1, :] += jnp.sum(grad * normed, axis=0, keepdims=True)
-        vec_ref[1:2, :] += jnp.sum(grad, axis=0, keepdims=True)
-        out_ref[at, :] = grad_ref[at, :] + normal_back(grad, normed, rscale, gain)
-
-    row_loop(x_ref.shape[0], back)
-    scatter.finish()
-
-
-def attn_back(parts, w, x, grad, gain):
-    nctx = lax.axis_size("ctx")
-    rows, d = x.shape
-    return pl.pallas_call(
-        attn_back_kernel,
-        out_shape=(
-            jax.ShapeDtypeStruct((rows, d), jnp.float32),
-            jax.ShapeDtypeStruct((2, d), jnp.float32),
-        ),
-        in_specs=[VMEM] * 5,
-        out_specs=(VMEM, VMEM),
-        scratch_shapes=scatter_scratch(nctx, rows, d),
-        compiler_params=pltpu.CompilerParams(collective_id=3, has_side_effects=True),
-        cost_estimate=pl.CostEstimate(flops=0, bytes_accessed=100_000_000, transcendentals=0),
-        name="attn_back",
-    )(parts, w, x, grad, gain)
-
-
-def down_kernel(hidden_ref, w_ref, resid_ref, out_ref, *scratch):
-    place = Place()
-    greet(place)
-    scatter = sum_scatter(
-        place,
-        resid_ref.shape[0],
-        lambda rows, cols: dot_nn(hidden_ref[rows, :], w_ref[:, cols]),
-        *scratch[:5],
-        scratch[5:9],
-    )
-    scatter.run()
-
-    def add(at):
-        out_ref[at, :] = (resid_ref[at, :] + scatter.total(at)).astype(jnp.bfloat16)
-
-    row_loop(resid_ref.shape[0], add)
-    scatter.finish()
-
-
-def down(hidden, w, resid):
-    nctx = lax.axis_size("ctx")
-    rows, d = resid.shape
-    return pl.pallas_call(
-        down_kernel,
-        out_shape=jax.ShapeDtypeStruct((rows, d), jnp.bfloat16),
-        in_specs=[VMEM] * 3,
-        out_specs=VMEM,
-        scratch_shapes=scatter_scratch(nctx, rows, d),
-        compiler_params=pltpu.CompilerParams(collective_id=4, has_side_effects=True),
-        cost_estimate=pl.CostEstimate(flops=0, bytes_accessed=100_000_000, transcendentals=0),
-        name="down_sum",
-    )(hidden, w, resid)
-
-
-def vectors_kernel(v_ref, out_ref, from_ctx, from_dp, plane, ctx_send, ctx_recv, dp_send, dp_recv):
-    place = Place()
-    greet(place, all_ctx=True, along_dp=True)
-    nctx, ndp, c, z = place.nctx, place.ndp, place.c, place.z
-
-    def across(i):
-        return push(
-            v_ref, from_ctx.at[c], ctx_send.at[i - 1], ctx_recv.at[c], place.at(lax.rem(c + i, nctx))
-        )
-
-    def along(i):
-        return push(
-            plane, from_dp.at[z], dp_send.at[i - 1], dp_recv.at[z], {"dp": lax.rem(z + i, ndp), "ctx": c}
-        )
-
-    for i in range(1, nctx):
-        across(i).start()
-    from_ctx[c] = v_ref[...]
-    for i in range(1, nctx):
-        s = lax.rem(c + i, nctx)
-        push(v_ref, from_ctx.at[s], ctx_send.at[0], ctx_recv.at[s], place.at(s)).wait_recv()
-    value = from_ctx[0]
-    for i in range(1, nctx):
-        value = value + from_ctx[i]
-    plane[...] = value
-    for i in range(1, ndp):
-        along(i).start()
-    from_dp[z] = value
-    for i in range(1, ndp):
-        s = lax.rem(z + i, ndp)
-        push(plane, from_dp.at[s], dp_send.at[0], dp_recv.at[s], {"dp": s, "ctx": c}).wait_recv()
-    value = from_dp[0]
-    for i in range(1, ndp):
-        value = value + from_dp[i]
-    out_ref[...] = value
-    for i in range(1, nctx):
-        across(i).wait_send()
-    for i in range(1, ndp):
-        along(i).wait_send()
-
-
-def sum_vectors(v):
-    ndp, nctx = lax.axis_size("dp"), lax.axis_size("ctx")
-    f32 = jnp.float32
-    return pl.pallas_call(
-        vectors_kernel,
-        out_shape=jax.ShapeDtypeStruct(v.shape, f32),
-        in_specs=[VMEM],
-        out_specs=VMEM,
-        scratch_shapes=[
-            pltpu.VMEM((nctx,) + v.shape, f32),
-            pltpu.VMEM((ndp,) + v.shape, f32),
-            pltpu.VMEM(v.shape, f32),
-            DMA((nctx - 1,)),
-            DMA((nctx,)),
-            DMA((ndp - 1,)),
-            DMA((ndp,)),
-        ],
-        compiler_params=pltpu.CompilerParams(collective_id=5, has_side_effects=True),
-        cost_estimate=pl.CostEstimate(flops=0, bytes_accessed=30_000_000, transcendentals=0),
-        name="sum_vectors",
-    )(v)
-
-
 HALF = ROT // 2
 PAIR = 256
 
@@ -770,8 +579,9 @@
 
 
 class DepthScatter:
-    def __init__(self, place, part, got, both, width, send, recv):
-        self.place, self.part, self.got, self.both, self.width = place, part, got, both, width
+    def __init__(self, place, source, part, got, both, width, send, recv):
+        self.place, self.source, self.part = place, source, part
+        self.got, self.both, self.width = got, both, width
         self.send, self.recv = send, recv
         self.line = place.ndp == 4
         z = place.z
@@ -782,7 +592,7 @@
         self.near = jnp.clip(3 * (z - 1), 0, 3)
 
     def block(self, z):
-        return self.part.at[:, pl.ds(pl.multiple_of(z * self.width, self.width), self.width)]
+        return self.source.at[:, pl.ds(pl.multiple_of(z * self.width, self.width), self.width)]
 
     def copy(self, src, slot, sem, z):
         return push(src, self.got.at[slot], self.send.at[sem], self.recv.at[slot], {"dp": z, "ctx": self.place.c})
@@ -896,10 +706,10 @@
 def forward_kernel(
     perm_ref, x_ref, cot_ref, gain1_ref, bias1_ref, gain2_ref, bias2_ref, shift_ref,
     qkv_ref, out_ref, gateup_ref, down_ref,
-    resid_ref, q_t, k_t, v_t, attn_t, lse, hidden_ref, gate_side, up_side, down_grads, cos_ref, sin_ref, pos_col, pos_row,
+    resid_ref, q_t, k_t, v_t, attn_t, lse, hidden_ref, gate_side, up_side, first_sums, cos_ref, sin_ref, pos_col, pos_row,
     rows_out, qkv_out, out_out, gateup_out, down_out, grads_out,
     row_block, cot_block, rows_all, cot_all, qkv_all, out_all, gateup_all, down_all,
-    k_n, bias, attn, gate_f, hidden_t, up_t, part, shifts, *sems
+    k_n, bias, attn, gate_f, hidden_t, gate_t, up_t, part, shifts, *sems
 ):
     f32, bf16 = jnp.float32, jnp.bfloat16
     place = Place()
@@ -919,14 +729,20 @@
 
     depth, width = qkv_ref.shape[1], out_ref.shape[1]
 
-    def half(i):
-        return lambda ref, z: ref.at[i, :, pl.ds(pl.multiple_of(z * depth, depth), depth)]
+    ff = gateup_ref.shape[1]
+    half = ff // 2
+
+    def slab(first):
+        return lambda ref, z: ref.at[pl.ds(first, half), pl.ds(pl.multiple_of(z * depth, depth), depth)]
 
     qkv = DepthGather(place, qkv_ref, qkv_all, along_rows(depth), *take(3))
     out = DepthGather(place, out_ref, out_all, along_lanes(width), *take(3), passing=False)
-    gate = DepthGather(place, gateup_ref.at[0], gateup_all, half(0), *take(3))
-    up = DepthGather(place, gateup_ref.at[1], gateup_all, half(1), *take(3))
-    down = DepthGather(place, down_ref, down_all, along_lanes(width), *take(3))
+    gate, up, down = [], [], []
+    for h in range(2):
+        at = pl.ds(h * half, half)
+        gate.append(DepthGather(place, gateup_ref.at[0, at], gateup_all, slab(h * half), *take(3)))
+        up.append(DepthGather(place, gateup_ref.at[1, at], gateup_all, slab(ff + h * half), *take(3)))
+        down.append(DepthGather(place, down_ref.at[at], down_all, slab(h * half), *take(3)))
     rows = row_gather(place, row_block, rows_all, *take(3))
     cots = row_gather(place, cot_block, cot_all, *take(3))
     normeds = row_gather(place, row_block, rows_all, *take(3))
@@ -944,7 +760,7 @@
         save(2, out_all, out_out),
         save(3, gateup_all, gateup_out),
         save(4, down_all, down_out),
-        save(5, gateup_all, grads_out),
+        save(5, gateup_all.at[pl.ds(0, 3 * half)], grads_out),
     ]
 
     qkv.start()
@@ -966,15 +782,18 @@
     cots.forward()
     qkv.forward_far()
     out.start()
-    gate.start()
-    up.start()
+    gate[0].start()
+    up[0].start()
     rows.finish()
     saves[0].start()
     cots.finish()
     qkv.finish()
     saves[1].start()
     attend(rows_all, qkv_all, shifts, cos_ref, sin_ref, pos_col, pos_row, q_t, k_t, v_t, attn_t, lse, k_n, bias, attn)
-    gate.forward_next()
+    gate[0].forward_next()
+    up[0].forward_next()
+    down[0].start()
+    gate[1].start()
     out.finish()
     saves[2].start()
     saves[0].wait()
@@ -986,7 +805,9 @@
         scatter_refs[5:9],
     )
     scatter.run()
-    up.forward_next()
+    gate[0].forward_far()
+    up[0].forward_far()
+    down[0].forward_next()
     gain2, shift2 = gain2_ref[...].astype(f32)[None, :], bias2_ref[...].astype(f32)[None, :]
 
     def norm2(at):
@@ -997,73 +818,88 @@
 
     row_loop(x_ref.shape[0], norm2)
     normeds.start()
-    gate.forward_far()
     normeds.forward()
-    up.forward_far()
-    down.start()
+    down[0].forward_far()
+    gate[1].forward_next()
+    up[1].start()
     normeds.finish()
     scatter.finish()
-    gate.finish()
-
-    def gates(t):
-        at = span(t, PAIR)
-        gate_f[at, :] = dot_nt(rows_all[at, :], gateup_all[0])
-
-    tiles(seq // PAIR, gates)
-    down.forward_next()
-    up.finish()
+
+    def gates(h):
+        def body(t):
+            at = span(t, PAIR)
+            gate_f[at, :] = dot_nt(rows_all[at, :], gateup_all[h * half : (h + 1) * half, :])
+
+        tiles(seq // PAIR, body)
+
+    def ups(h):
+        def body(t):
+            at = span(t, PAIR)
+            value = dot_nt(rows_all[at, :], gateup_all[ff + h * half : ff + (h + 1) * half, :])
+            g = gate_f[at, :]
+            sigma = jax.nn.sigmoid(g)
+            swish = g * sigma
+            hidden = (swish * value).astype(bf16)
+            hidden_ref[h, at, :] = hidden
+            hidden_t[:, at] = hidden.T
+            gate_side[h, at, :] = (value * sigma * (1.0 + g * (1.0 - sigma))).astype(bf16)
+            up_side[h, at, :] = swish.astype(bf16)
+
+        tiles(seq // PAIR, body)
+
+    def sides(h):
+        def body(t):
+            at = span(t, PAIR)
+            grad = dot_nt(cot_all[at, :], down_all[h * half : (h + 1) * half, :])
+            gate_grad = (grad * gate_side[h, at, :].astype(f32)).astype(bf16)
+            up_grad = (grad * up_side[h, at, :].astype(f32)).astype(bf16)
+            gate_side[h, at, :] = gate_grad
+            up_side[h, at, :] = up_grad
+            gate_t[:, at] = gate_grad.T
+            up_t[:, at] = up_grad.T
+
+        tiles(seq // PAIR, body)
+
+    def weights(target):
+        def body(j):
+            cols = span(j, 2 * PAIR)
+            normed = rows_all[:, cols]
+            target[:half, cols] = dot_nn(gate_t[...], normed).astype(bf16)
+            target[half : 2 * half, cols] = dot_nn(up_t[...], normed).astype(bf16)
+            target[2 * half : 3 * half, cols] = dot_nn(hidden_t[...], cot_all[:, cols]).astype(bf16)
+
+        tiles(d // (2 * PAIR), body)
+
+    gate[0].finish()
+    gates(0)
+    up[0].finish()
+    ups(0)
+    gate[1].forward_far()
+    up[1].forward_next()
+    down[1].start()
+    down[0].finish()
+    sides(0)
+    weights(part)
+    summed = DepthScatter(place, part, part, got, both, width, dsend, drecv)
+    summed.start()
+    up[1].forward_far()
+    down[1].forward_next()
+    down[1].forward_far()
+    gate[1].finish()
+    gates(1)
+    summed.hand_on(0)
+    up[1].finish()
     saves[3].start()
-
-    def ups(t):
-        at = span(t, PAIR)
-        value = dot_nt(rows_all[at, :], gateup_all[1])
-        g = gate_f[at, :]
-        sigma = jax.nn.sigmoid(g)
-        swish = g * sigma
-        hidden = (swish * value).astype(bf16)
-        hidden_ref[at, :] = hidden
-        hidden_t[:, at] = hidden.T
-        gate_side[at, :] = (value * sigma * (1.0 + g * (1.0 - sigma))).astype(bf16)
-        up_side[at, :] = swish.astype(bf16)
-
-    tiles(seq // PAIR, ups)
-
-    def down_weights(j):
-        cols = span(j, 2 * PAIR)
-        part[:, cols] = dot_nn(hidden_t[...], cot_all[:, cols]).astype(bf16)
-
-    tiles(d // (2 * PAIR), down_weights)
-    summed = DepthScatter(place, part, got, both, width, dsend, drecv)
-    summed.start()
-    down.forward_far()
-    summed.hand_on(0)
+    ups(1)
     summed.hand_on(1)
-    down.finish()
+    summed.hand_on(2)
+    down[1].finish()
     saves[4].start()
-    summed.hand_on(2)
     saves[3].wait()
-
-    def sides(t):
-        at = span(t, PAIR)
-        grad = dot_nt(cot_all[at, :], down_all[...])
-        gate_grad = (grad * gate_side[at, :].astype(f32)).astype(bf16)
-        up_grad = (grad * up_side[at, :].astype(f32)).astype(bf16)
-        gate_side[at, :] = gate_grad
-        up_side[at, :] = up_grad
-        hidden_t[:, at] = gate_grad.T
-        up_t[:, at] = up_grad.T
-
-    tiles(seq // PAIR, sides)
-
-    def gateup_weights(j):
-        cols = span(j, 2 * PAIR)
-        normed = rows_all[:, cols]
-        gateup_all[0, :, cols] = dot_nn(hidden_t[...], normed).astype(bf16)
-        gateup_all[1, :, cols] = dot_nn(up_t[...], normed).astype(bf16)
-
-    tiles(d // (2 * PAIR), gateup_weights)
+    sides(1)
+    weights(gateup_all)
     saves[5].start()
-    summed.finish(down_grads)
+    summed.finish(first_sums)
     for i in (1, 2, 4, 5):
         saves[i].wait()
 
@@ -1088,10 +924,10 @@
             shaped((width, seq)),
             shaped((width, seq)),
             shaped((8, seq), f32),
-            shaped((seq, ff)),
-            shaped((seq, ff)),
-            shaped((seq, ff)),
-            shaped(down.shape, f32),
+            shaped((2, seq, ff // 2)),
+            shaped((2, seq, ff // 2)),
+            shaped((2, seq, ff // 2)),
+            shaped((3 * ff // 2, d // ndp), f32),
             shaped((8, seq), f32),
             shaped((8, seq), f32),
             shaped((seq, 1), f32),
@@ -1099,9 +935,9 @@
             shaped((seq, d)),
             shaped((3, d, width)),
             shaped((width, d)),
-            shaped((2, ff, d)),
+            shaped((2 * ff, d)),
             shaped((ff, d)),
-            shaped((2, ff, d)),
+            shaped((3 * ff // 2, d)),
         ),
         in_specs=[pl.BlockSpec(memory_space=pltpu.SMEM)] + [VMEM] * 7 + [ANY] * 4,
         out_specs=(VMEM,) * 14 + (ANY,) * 6,
@@ -1112,21 +948,22 @@
             pltpu.VMEM((seq, d), bf16),
             pltpu.VMEM((3, d, width), bf16),
             pltpu.VMEM((width, d), bf16),
-            pltpu.VMEM((2, ff, d), bf16),
+            pltpu.VMEM((2 * ff, d), bf16),
             pltpu.VMEM((ff, d), bf16),
             pltpu.VMEM((heads, seq, HEAD_DIM), bf16),
             pltpu.VMEM((seq, PAIR), f32),
             pltpu.VMEM((seq, width), bf16),
-            pltpu.VMEM((seq, ff), f32),
-            pltpu.VMEM((ff, seq), bf16),
-            pltpu.VMEM((ff, seq), bf16),
-            pltpu.VMEM((ff, d), bf16),
+            pltpu.VMEM((seq, ff // 2), f32),
+            pltpu.VMEM((ff // 2, seq), bf16),
+            pltpu.VMEM((ff // 2, seq), bf16),
+            pltpu.VMEM((ff // 2, seq), bf16),
+            pltpu.VMEM((3 * ff // 2, d), bf16),
             pltpu.VMEM((3, width), f32),
         ]
-        + depth_sems(ndp) * 5
+        + depth_sems(ndp) * 8
         + gather_sems(nctx) * 3
         + scatter_scratch(nctx, rows, d)
-        + depth_scatter_scratch(ndp, ff, d // ndp)
+        + depth_scatter_scratch(ndp, 3 * ff // 2, d // ndp)
         + [DMA((6,))],
         compiler_params=pltpu.CompilerParams(
             collective_id=0, has_side_effects=True, vmem_limit_bytes=67_000_000
@@ -1136,14 +973,19 @@
     )(perm, x, cot, *row, shift, qkv, out, gateup, down)
 
 
-def attend_back_kernel(
+def attend_back(
     grad_ref, w_ref, rows_ref, cos_ref, sin_ref, pos_col, pos_row, q_t, k_t, v_t, attn_t, lse,
-    parts_ref, sums_ref, w_grads, g_t, delta, q_grad, kv_grad, bias, flat
+    parts_ref, sums_ref, w_grads, g_t, delta, q_grad, kv_grad, bias, flat, rows_buf, rows_sem, between
 ):
     seq, d = grad_ref.shape
     width = w_ref.shape[0]
     heads = width // HEAD_DIM
     bf16, f32 = jnp.bfloat16, jnp.float32
+    count = d // (2 * PAIR)
+
+    def load(j):
+        slot = lax.rem(j, 2)
+        return pltpu.make_async_copy(rows_ref.at[:, span(j, 2 * PAIR)], rows_buf.at[slot], rows_sem.at[slot])
 
     def first(t):
         at = span(t, PAIR)
@@ -1154,6 +996,7 @@
         g_t[:, at] = grad.astype(bf16)
 
     tiles(seq // PAIR, first)
+    between()
     q_grad[...] = jnp.zeros_like(q_grad)
 
     def keys(t):
@@ -1170,6 +1013,7 @@
             q_grad[feats, :] += dot_nn(keys_t, scores)
 
     tiles(seq // PAIR, keys)
+    load(0).start()
     sums_ref[...] = jnp.zeros_like(sums_ref)
 
     def part(t):
@@ -1190,43 +1034,311 @@
     tiles(seq // PAIR, part)
 
     def weights(j):
+        pl.when(j + 1 < count)(lambda: load(j + 1).start())
+        load(j).wait()
         cols = span(j, 2 * PAIR)
-        rows = rows_ref[:, cols]
+        rows = rows_buf[lax.rem(j, 2)]
         for i in range(3):
-            w_grads[i, cols, :] = dot_nn(flat[i], rows).T.astype(bf16)
-        w_grads[3, cols, :] = dot_nn(attn_t[...], grad_ref[:, cols]).T.astype(bf16)
-
-    tiles(d // (2 * PAIR), weights)
-
-
-def attention_back(grad_all, w, rows_all, cosine, sine, pos_col, pos_row, q_t, k_t, v_t, attn_t, lse):
-    seq, d = rows_all.shape
-    width = w.shape[0]
+            w_grads[i * width : (i + 1) * width, cols] = dot_nn(flat[i], rows).astype(bf16)
+        w_grads[3 * width : 4 * width, cols] = dot_nn(attn_t[...], grad_ref[:, cols]).astype(bf16)
+
+    tiles(count, weights)
+
+
+def middle_kernel(
+    gate_ref, up_ref, w_hbm, part_ref, resid_ref, cot_ref, gain_ref, out_ref, rows_ref,
+    cos_ref, sin_ref, pos_col, pos_row, q_t, k_t, v_t, attn_t, lse,
+    grad_ref, vec_ref, parts_ref, sums_ref, second_sums, w_out,
+    arena, part_all, block, grad_all, g_t, delta, q_grad, kv_grad, bias, flat, rows_buf, rows_sem, save_sem, *scratch
+):
+    place = Place()
+    greet(place, along_dp=True)
+    scratch = list(scratch)
+
+    def take(n):
+        head = scratch[:n]
+        del scratch[:n]
+        return head
+
+    rows = resid_ref.shape[0]
+    half, d = gate_ref.shape[2], part_ref.shape[1]
+    ff = 2 * half
+    piece = d // place.ndp
+    refs = take(9)
+    sum_refs = take(4)
+    summed = DepthScatter(place, part_ref, part_all, *sum_refs[:2], piece, *sum_refs[2:])
+    summed.start()
+    load = pltpu.make_async_copy(w_hbm, arena, save_sem.at[0])
+    fetch = pltpu.make_async_copy(part_ref, part_all, save_sem.at[1])
+    load.start()
+    fetch.start()
+    load.wait()
+    fetch.wait()
+
+    def product(at, cols):
+        total = dot_nn(gate_ref[0, at, :], arena[:half, cols])
+        total = total + dot_nn(gate_ref[1, at, :], arena[half:ff, cols])
+        total = total + dot_nn(up_ref[0, at, :], arena[ff : ff + half, cols])
+        return total + dot_nn(up_ref[1, at, :], arena[ff + half :, cols])
+
+    scatter = sum_scatter(place, rows, product, *refs[:5], refs[5:9])
+    scatter.run()
+    gain = gain_ref[...].astype(jnp.float32)[None, :]
+    vec_ref[...] = jnp.zeros_like(vec_ref)
+
+    def back(at):
+        grad = scatter.total(at)
+        normed, rscale = normal(resid_ref[at, :])
+        vec_ref[0:1, :] += jnp.sum(grad * normed, axis=0, keepdims=True)
+        vec_ref[1:2, :] += jnp.sum(grad, axis=0, keepdims=True)
+        out = cot_ref[at, :] + normal_back(grad, normed, rscale, gain)
+        grad_ref[at, :] = out
+        block[at, :] = out.astype(jnp.bfloat16)
+
+    row_loop(rows, back)
+    gathered = row_gather(place, block, grad_all, *take(3))
+    gathered.start()
+    summed.hand_on(0)
+    gathered.forward()
+    gathered.finish()
+    scatter.finish()
+
+    def between():
+        summed.hand_on(1)
+        summed.hand_on(2)
+
+    w_grads = arena.at[: w_out.shape[0]]
+    attend_back(
+        grad_all, out_ref, rows_ref, cos_ref, sin_ref, pos_col, pos_row, q_t, k_t, v_t, attn_t, lse,
+        parts_ref, sums_ref, w_grads, g_t, delta, q_grad, kv_grad, bias, flat, rows_buf, rows_sem, between,
+    )
+    keep = pltpu.make_async_copy(w_grads, w_out, save_sem.at[2])
+    keep.start()
+    summed.finish(second_sums)
+    keep.wait()
+
+
+def middle(gate_grad, up_grad, w, part, resid, cot, gain, out, rows_all, cosine, sine, pos_col, pos_row, q_t, k_t, v_t, attn_t, lse):
+    ndp, nctx = lax.axis_size("dp"), lax.axis_size("ctx")
+    rows, d = resid.shape
+    seq, width, ff = rows * nctx, out.shape[0], w.shape[0] // 2
     bf16, f32 = jnp.bfloat16, jnp.float32
     return pl.pallas_call(
-        attend_back_kernel,
+        middle_kernel,
         out_shape=(
+            jax.ShapeDtypeStruct((rows, d), f32),
+            jax.ShapeDtypeStruct((2, d), f32),
             jax.ShapeDtypeStruct((3, seq, width), bf16),
             jax.ShapeDtypeStruct((3, width), f32),
-            jax.ShapeDtypeStruct((4, d, width), bf16),
+            jax.ShapeDtypeStruct((3 * ff // 2, d // ndp), f32),
+            jax.ShapeDtypeStruct((4 * width, d), bf16),
         ),
-        in_specs=[VMEM] * 12,
-        out_specs=(VMEM,) * 3,
+        in_specs=[VMEM] * 2 + [ANY] * 2 + [VMEM] * 4 + [ANY] + [VMEM] * 9,
+        out_specs=(VMEM,) * 5 + (ANY,),
         scratch_shapes=[
+            pltpu.VMEM((2 * ff, d), bf16),
+            pltpu.VMEM((3 * ff // 2, d), bf16),
+            pltpu.VMEM((rows, d), bf16),
+            pltpu.VMEM((seq, d), bf16),
             pltpu.VMEM((width, seq), bf16),
             pltpu.VMEM((8, seq), f32),
             pltpu.VMEM((width, seq), f32),
             pltpu.VMEM((2, width, seq), f32),
             pltpu.VMEM((PAIR, seq), f32),
             pltpu.VMEM((3, width, seq), bf16),
-        ],
-        cost_estimate=pl.CostEstimate(flops=0, bytes_accessed=120_000_000, transcendentals=0),
-        name="attention_back",
-    )(grad_all, w, rows_all, cosine, sine, pos_col, pos_row, q_t, k_t, v_t, attn_t, lse)
-
-
-def shard(grad, dim):
-    return lax.psum_scatter(grad, "dp", scatter_dimension=dim, tiled=True)
+            pltpu.VMEM((2, seq, 2 * PAIR), bf16),
+            DMA((2,)),
+            DMA((4,)),
+        ]
+        + scatter_scratch(nctx, rows, d)
+        + depth_scatter_scratch(ndp, 3 * ff // 2, d // ndp)
+        + gather_sems(nctx),
+        compiler_params=pltpu.CompilerParams(
+            collective_id=2, has_side_effects=True, vmem_limit_bytes=67_000_000
+        ),
+        cost_estimate=pl.CostEstimate(flops=0, bytes_accessed=300_000_000, transcendentals=0),
+        name="middle",
+    )(gate_grad, up_grad, w, part, resid, cot, gain, out, rows_all, cosine, sine, pos_col, pos_row, q_t, k_t, v_t, attn_t, lse)
+
+
+class VectorSum:
+    def __init__(self, place, value, from_ctx, from_dp, plane, ctx_send, ctx_recv, dp_send, dp_recv):
+        self.place, self.value, self.from_ctx, self.from_dp, self.plane = place, value, from_ctx, from_dp, plane
+        self.ctx_send, self.ctx_recv, self.dp_send, self.dp_recv = ctx_send, ctx_recv, dp_send, dp_recv
+
+    def across(self, i):
+        place = self.place
+        return push(
+            self.value, self.from_ctx.at[place.c], self.ctx_send.at[i - 1], self.ctx_recv.at[place.c],
+            place.at(lax.rem(place.c + i, place.nctx)),
+        )
+
+    def along(self, i):
+        place = self.place
+        return push(
+            self.plane, self.from_dp.at[place.z], self.dp_send.at[i - 1], self.dp_recv.at[place.z],
+            {"dp": lax.rem(place.z + i, place.ndp), "ctx": place.c},
+        )
+
+    def start(self):
+        for i in range(1, self.place.nctx):
+            self.across(i).start()
+        self.from_ctx[self.place.c] = self.value[...]
+
+    def turn(self):
+        place = self.place
+        for i in range(1, place.nctx):
+            c = lax.rem(place.c + i, place.nctx)
+            push(self.value, self.from_ctx.at[c], self.ctx_send.at[0], self.ctx_recv.at[c], place.at(c)).wait_recv()
+        total = self.from_ctx[0]
+        for i in range(1, place.nctx):
+            total = total + self.from_ctx[i]
+        self.plane[...] = total
+        self.from_dp[place.z] = total
+        for i in range(1, place.ndp):
+            self.along(i).start()
+
+    def finish(self, out_ref):
+        place = self.place
+        for i in range(1, place.ndp):
+            z = lax.rem(place.z + i, place.ndp)
+            device = {"dp": z, "ctx": place.c}
+            push(self.plane, self.from_dp.at[z], self.dp_send.at[0], self.dp_recv.at[z], device).wait_recv()
+        total = self.from_dp[0]
+        for i in range(1, place.ndp):
+            total = total + self.from_dp[i]
+        out_ref[...] = total
+        for i in range(1, place.nctx):
+            self.across(i).wait_send()
+        for i in range(1, place.ndp):
+            self.along(i).wait_send()
+
+
+def vector_scratch(ndp, nctx, shape):
+    f32 = jnp.float32
+    return [
+        pltpu.VMEM(shape, f32),
+        pltpu.VMEM((nctx,) + shape, f32),
+        pltpu.VMEM((ndp,) + shape, f32),
+        pltpu.VMEM(shape, f32),
+        DMA((nctx - 1,)),
+        DMA((nctx,)),
+        DMA((ndp - 1,)),
+        DMA((ndp,)),
+    ]
+
+
+def tail_kernel(
+    w_grads, parts_ref, qkv_ref, x_ref, grad_ref, gain_ref, hidden_ref, down_ref, resid_ref, vec_ref, sums_ref,
+    block_out, input_grad, small, qkv_grads, out_grads,
+    total, *scratch
+):
+    place = Place()
+    greet(place, all_ctx=True, along_dp=True)
+    scratch = list(scratch)
+
+    def take(n):
+        head = scratch[:n]
+        del scratch[:n]
+        return head
+
+    rows, d = x_ref.shape
+    width = qkv_ref.shape[2]
+    first_refs, second_refs = take(9), take(9)
+    long_refs, short_refs = take(4), take(4)
+    vectors = VectorSum(place, *take(8))
+    w_all, down_all, load_sem = take(3)
+    piece, cut = d // place.ndp, 3 * width
+    upper, lower = pl.ds(0, cut), pl.ds(cut, width)
+    long_sum = DepthScatter(place, w_grads.at[upper], w_all.at[upper], *long_refs[:2], piece, *long_refs[2:])
+    short_sum = DepthScatter(place, w_grads.at[lower], w_all.at[lower], *short_refs[:2], piece, *short_refs[2:])
+    long_sum.start()
+    short_sum.start()
+    loads = [
+        pltpu.make_async_copy(w_grads, w_all, load_sem.at[0]),
+        pltpu.make_async_copy(down_ref, down_all, load_sem.at[1]),
+    ]
+    for copy in loads:
+        copy.start()
+
+    def product(at, cols):
+        part = dot_nt(parts_ref[0, at, :], qkv_ref[0, cols, :])
+        part = part + dot_nt(parts_ref[1, at, :], qkv_ref[1, cols, :])
+        return part + dot_nt(parts_ref[2, at, :], qkv_ref[2, cols, :])
+
+    first = sum_scatter(place, rows, product, *first_refs[:5], first_refs[5:9])
+    half = hidden_ref.shape[2]
+
+    def down_product(at, cols):
+        return dot_nn(hidden_ref[0, at, :], down_all[:half, cols]) + dot_nn(hidden_ref[1, at, :], down_all[half:, cols])
+
+    second = sum_scatter(place, rows, down_product, *second_refs[:5], second_refs[5:9])
+    first.run()
+    gain = gain_ref[...].astype(jnp.float32)[None, :]
+    value = vectors.value
+    value[...] = jnp.zeros_like(value)
+    value[2:4, :] = vec_ref[...]
+    value[4:7, pl.ds(pl.multiple_of(place.c * width, width), width)] = sums_ref[...]
+
+    def back(at):
+        grad = first.total(at)
+        normed, rscale = normal(x_ref[at, :].astype(jnp.float32))
+        value[0:1, :] += jnp.sum(grad * normed, axis=0, keepdims=True)
+        value[1:2, :] += jnp.sum(grad, axis=0, keepdims=True)
+        input_grad[at, :] = grad_ref[at, :] + normal_back(grad, normed, rscale, gain)
+
+    row_loop(rows, back)
+    vectors.start()
+    for copy in loads:
+        copy.wait()
+    long_sum.hand_on(0)
+    second.run((lambda: long_sum.hand_on(1), lambda: long_sum.hand_on(2)))
+
+    def add(at):
+        block_out[at, :] = (resid_ref[at, :] + second.total(at)).astype(jnp.bfloat16)
+
+    row_loop(rows, add)
+    vectors.turn()
+    short_sum.hand_on(0)
+    short_sum.hand_on(1)
+    short_sum.hand_on(2)
+    first.finish()
+    second.finish()
+    vectors.finish(small)
+    long_sum.finish(total.at[upper])
+    short_sum.finish(out_grads)
+    for i in range(3):
+        qkv_grads[i] = total[i * width : (i + 1) * width, :].T
+
+
+def tail(w_grads, parts, qkv, x, grad, gain, hidden, down, resid, vec, sums):
+    ndp, nctx = lax.axis_size("dp"), lax.axis_size("ctx")
+    rows, d = x.shape
+    width = qkv.shape[2]
+    bf16, f32 = jnp.bfloat16, jnp.float32
+    return pl.pallas_call(
+        tail_kernel,
+        out_shape=(
+            jax.ShapeDtypeStruct((rows, d), bf16),
+            jax.ShapeDtypeStruct((rows, d), f32),
+            jax.ShapeDtypeStruct((8, d), f32),
+            jax.ShapeDtypeStruct((3, d // ndp, width), f32),
+            jax.ShapeDtypeStruct((width, d // ndp), f32),
+        ),
+        in_specs=[ANY] + [VMEM] * 6 + [ANY] + [VMEM] * 3,
+        out_specs=(VMEM,) * 5,
+        scratch_shapes=[pltpu.VMEM((3 * width, d // ndp), f32)]
+        + scatter_scratch(nctx, rows, d) * 2
+        + depth_scatter_scratch(ndp, 3 * width, d // ndp)
+        + depth_scatter_scratch(ndp, width, d // ndp)
+        + vector_scratch(ndp, nctx, (8, d))
+        + [pltpu.VMEM((4 * width, d), bf16), pltpu.VMEM(down.shape, bf16), DMA((2,))],
+        compiler_params=pltpu.CompilerParams(
+            collective_id=3, has_side_effects=True, vmem_limit_bytes=67_000_000
+        ),
+        cost_estimate=pl.CostEstimate(flops=0, bytes_accessed=300_000_000, transcendentals=0),
+        name="tail",
+    )(w_grads, parts, qkv, x, grad, gain, hidden, down, resid, vec, sums)
 
 
 def per_device(
@@ -1245,42 +1357,37 @@
 ):
     width_local = qkv_weight.shape[2]
     (
-        residual_stream, q_t, k_t, v_t, attn_t, lse, hidden_b, gate_grad, up_grad, down_grads, cos_all, sin_all, pos_col, pos_row,
-        rows_all, qkv_local, out_local, gateup_local, down_local, gateup_grads,
+        residual_stream, q_t, k_t, v_t, attn_t, lse, hidden_b, gate_grad, up_grad, first_sums, cos_all, sin_all, pos_col, pos_row,
+        rows_all, qkv_local, out_local, gateup_local, down_local, mlp_grads,
     ) = forward(
         group_perm, block_input, out_cotangent, attn_norm_gain, attn_norm_bias, mlp_norm_gain, mlp_norm_bias, qkv_bias,
         qkv_weight, out_weight, gateup_weight.transpose(0, 2, 1), down_weight,
     )
-    gateup_grads = shard(gateup_grads, 2)
-    resid_grad, second_vectors, resid_all = mlp_back(
-        gate_grad, up_grad, gateup_local, residual_stream, out_cotangent, mlp_norm_gain
+    resid_grad, second_vectors, grad_parts_b, shift_part, second_sums, attn_grads = middle(
+        gate_grad, up_grad, gateup_local, mlp_grads, residual_stream, out_cotangent, mlp_norm_gain, out_local,
+        rows_all, cos_all, sin_all, pos_col, pos_row, q_t, k_t, v_t, attn_t, lse,
     )
-    grad_parts_b, shift_part, attn_grads = attention_back(
-        resid_all, out_local, rows_all, cos_all, sin_all, pos_col, pos_row, q_t, k_t, v_t, attn_t, lse
+    block_output, input_grad, small, qkv_grads, out_grads = tail(
+        attn_grads, grad_parts_b, qkv_local, block_input, resid_grad, attn_norm_gain,
+        hidden_b, down_local, residual_stream, second_vectors, shift_part,
     )
-    head_first = lax.axis_index("ctx") * width_local
-    f32 = jnp.float32
-    shift_grad = lax.dynamic_update_slice_in_dim(jnp.zeros((3, D), f32), shift_part, head_first, 1)
-    attn_grads = shard(attn_grads, 1)
-    input_grad, first_vectors = attn_back(grad_parts_b, qkv_local, block_input, resid_grad, attn_norm_gain)
-    hidden_late, first_vectors, gateup_grads = lax.optimization_barrier((hidden_b, first_vectors, gateup_grads))
-    block_output = down(hidden_late, down_local, residual_stream)
-    small = sum_vectors(
-        jnp.concatenate([first_vectors, second_vectors, shift_grad, jnp.zeros((1, D), f32)], axis=0)
-    )
-    small, block_output, attn_grads = lax.optimization_barrier((small, block_output, attn_grads))
-    attn_grads = attn_grads.astype(f32)
+    half = first_sums.shape[0] // 3
+    both = [
+        jnp.concatenate([first_sums[i * half : (i + 1) * half], second_sums[i * half : (i + 1) * half]])
+        for i in range(3)
+    ]
+    gateup_grads, down_grads = jnp.stack(both[:2]), both[2]
     return (
         block_output,
         input_grad,
         small[0],
         small[1],
-        attn_grads[:3],
+        qkv_grads,
         small[4:7],
-        attn_grads[3].T,
+        out_grads,
         small[2],
         small[3],
-        gateup_grads.astype(f32).transpose(0, 2, 1),
+        gateup_grads.transpose(0, 2, 1),
         down_grads,
     )
 

time: 458 us -> 443 us (0.967)
  waiting for transfers between devices: 23.9 us -> 0 us
  Pallas kernels: 408 us -> 429 us
  between operations: 14.2 us -> 0.7 us
    reduce_scatter x2 -> x0, waiting for transfers between devices: 23.9 us -> none  [shard(): return lax.psum_scatter(grad, 'dp', scatter_dimension=dim, tiled=True)]
    pallas_call x5 -> x2, Pallas kernels: 159 us -> 171 us  [the longest x1 86.8 us: middle(): pl.pallas_call(middle_kernel, out_shape=(jax.ShapeDtypeStruct((rows, d),...]
    pallas_call x1, Pallas kernels: 250 us -> 258 us  [forward(): pl.pallas_call(forward_kernel, out_shape=(shaped((rows, d), f32), shaped(...]
  transfers between devices with their start and end apart: 2 -> 0, of which waited for: 1 -> 0; matrix products, arithmetic and copies ran while one was open for 0% -> 0% of each run, Pallas kernels for 35% -> 0%
where the time goes in v5:
time: 443 us
  Pallas kernels  429 us (97%)
  local copies, waits for them, and re-layouts  9.48 us (2%)
    pallas_call x1, Pallas kernels, forward(): pl.pallas_call(forward_kernel, out_shape=(shaped((rows, d), f32), shaped(...  258 us
    pallas_call x1, Pallas kernels, middle(): pl.pallas_call(middle_kernel, out_shape=(jax.ShapeDtypeStruct((rows, d),...  86.8 us
    pallas_call x1, Pallas kernels, tail(): pl.pallas_call(tail_kernel, out_shape=(jax.ShapeDtypeStruct((rows, d), bf...  84.3 us

profile of v5, /device:TPU:0, one launch (start us, length us, event | category | flops | bytes accessed | tf_op | source)
XLA Modules:
  0.0 442.7 jit_solution(16238811859749133340)
XLA Ops:
  0.6 258.1 %forward.1 = (f32[128,2048]{1,0:T(8,128)}, bf16[256,1024]{1,0:T(8,128)(2,1)}, bf16[256,1024]{1,0:T(8,128)(2,1)}, bf16[256,1024]{1,0:T(8,128)(2,1)}, bf16[256,102...) custom-call(s32[1,16]{1,0:T(1,128)} %perm_ref.1, ...), custom_call_target="tpu_custom_call" | custom-call | bytes 700000000 | tf_op jit(solution)/shard_map/forward/pallas_call | solution.py:918
  258.7 86.8 %middle.1 = (f32[128,2048]{1,0:T(8,128)}, f32[2,2048]{1,0:T(2,128)}, bf16[3,1024,256]{2,1,0:T(8,128)(2,1)}, f32[3,256]{1,0:T(4,128)}, f32[1056,512]{1,0:T(8,128)}, /*index=5*/bf16[1024,2048]{1,0:T(8,128)(2,1)}) custom-call(bf16[2,1024,352]{2,1,0:T(8,128)(2,1)} %get-tuple-element.42.gate_ref, bf16[2,1024,352]{2,1,0:T(8,128)(2,1)} %get-tuple-element.43.up_ref, ...), custom_call_target="tpu_custom_call" | custom-call | bytes 300000000 | tf_op jit(solution)/shard_map/middle/pallas_call | solution.py:1126
  345.5 84.3 %tail.1 = (bf16[128,2048]{1,0:T(8,128)(2,1)}, f32[128,2048]{1,0:T(8,128)}, f32[8,2048]{1,0:T(8,128)}, f32[3,512,256]{2,1,0:T(8,128)}, f32[256,512]{1,0:T(8,128)}) custom-call(bf16[1024,2048]{1,0:T(8,128)(2,1)} %get-tuple-element.58.w_grads, bf16[3,1024,256]{2,1,0:T(8,128)(2,1)} %get-tuple-element.59.parts_ref, ...), custom_call_target="tpu_custom_call" | custom-call | bytes 300000000 | tf_op jit(solution)/shard_map/tail/pallas_call | solution.py:1319
  429.8 1.5 slice.35
  431.3 1.6 fusion.2
  432.9 0.0 copy-start
  432.9 1.9 fusion.1
  434.8 0.4 copy-done
  435.2 0.2 fusion
  435.4 1.2 pad_maximum_fusion
  436.6 0.3 maximum_bitcast_fusion.1
  436.8 0.0 copy-start.4
  436.8 0.0 copy-start.2
  436.9 1.9 maximum_bitcast_fusion
  438.7 0.0 copy-done.4
  438.7 0.0 copy-start.1
  438.7 0.8 copy.27
  439.5 0.0 copy-done.2
  439.5 1.0 copy.28
  440.5 0.0 copy-done.1
  440.5 0.0 copy-start.3
  440.5 1.1 copy.29
  441.6 0.3 copy-done.3
  441.9 0.8 copy.30
Async XLA Ops:
  432.9 2.3 copy-start
  436.8 1.9 copy-start.4
  436.8 2.7 copy-start.2
  438.7 1.8 copy-start.1
  440.5 1.4 copy-start.3

commit v6 on v5

--- a/solution.py
+++ b/solution.py
@@ -617,6 +617,10 @@
         return [self.copy(self.block(lax.rem(z + i, n)), i - 1, i - 1, lax.rem(z + i, n)) for i in range(1, n)]
 
     def start(self):
+        self.start_first()
+        self.start_last()
+
+    def start_first(self):
         if not self.line:
             for copy in self.across():
                 copy.start()
@@ -624,8 +628,12 @@
 
         @pl.when(self.end)
         def _():
-            for copy in self.from_end():
+            for copy in self.from_end()[:2]:
                 copy.start()
+
+    def start_last(self):
+        if self.line:
+            pl.when(self.end)(self.from_end()[2].start)
 
     def hand_on(self, n):
         if not self.line:
@@ -706,10 +714,12 @@
 def forward_kernel(
     perm_ref, x_ref, cot_ref, gain1_ref, bias1_ref, gain2_ref, bias2_ref, shift_ref,
     qkv_ref, out_ref, gateup_ref, down_ref,
-    resid_ref, q_t, k_t, v_t, attn_t, lse, hidden_ref, gate_side, up_side, first_sums, cos_ref, sin_ref, pos_col, pos_row,
+    lse, first_sums, cos_ref, sin_ref, pos_col, pos_row,
+    resid_out, q_out, k_out, v_out, attn_out, hidden_out, gate_side_out, up_side_out,
     rows_out, qkv_out, out_out, gateup_out, down_out, grads_out,
     row_block, cot_block, rows_all, cot_all, qkv_all, out_all, gateup_all, down_all,
-    k_n, bias, attn, gate_f, hidden_t, gate_t, up_t, part, shifts, *sems
+    k_n, bias, attn, gate_f, hidden_t, gate_t, up_t, part, shifts,
+    resid_ref, q_t, k_t, v_t, attn_t, hidden_ref, gate_side, up_side, *sems
 ):
     f32, bf16 = jnp.float32, jnp.bfloat16
     place = Place()
@@ -761,7 +771,16 @@
         save(3, gateup_all, gateup_out),
         save(4, down_all, down_out),
         save(5, gateup_all.at[pl.ds(0, 3 * half)], grads_out),
+        save(6, q_t, q_out),
+        save(7, k_t, k_out),
+        save(8, v_t, v_out),
+        save(9, attn_t, attn_out),
+        save(10, resid_ref, resid_out),
     ]
+    for h in range(2):
+        saves.append(save(11 + 3 * h, hidden_ref.at[h], hidden_out.at[h]))
+        saves.append(save(12 + 3 * h, gate_side.at[h], gate_side_out.at[h]))
+        saves.append(save(13 + 3 * h, up_side.at[h], up_side_out.at[h]))
 
     qkv.start()
     gain, shift = gain1_ref[...].astype(f32)[None, :], bias1_ref[...].astype(f32)[None, :]
@@ -790,6 +809,8 @@
     qkv.finish()
     saves[1].start()
     attend(rows_all, qkv_all, shifts, cos_ref, sin_ref, pos_col, pos_row, q_t, k_t, v_t, attn_t, lse, k_n, bias, attn)
+    for i in range(6, 10):
+        saves[i].start()
     gate[0].forward_next()
     up[0].forward_next()
     down[0].start()
@@ -818,6 +839,7 @@
 
     row_loop(x_ref.shape[0], norm2)
     normeds.start()
+    saves[10].start()
     normeds.forward()
     down[0].forward_far()
     gate[1].forward_next()
@@ -879,6 +901,8 @@
     down[1].start()
     down[0].finish()
     sides(0)
+    for i in range(11, 14):
+        saves[i].start()
     weights(part)
     summed = DepthScatter(place, part, part, got, both, width, dsend, drecv)
     summed.start()
@@ -897,10 +921,12 @@
     saves[4].start()
     saves[3].wait()
     sides(1)
+    for i in range(14, 17):
+        saves[i].start()
     weights(gateup_all)
     saves[5].start()
     summed.finish(first_sums)
-    for i in (1, 2, 4, 5):
+    for i in (1, 2, *range(4, 17)):
         saves[i].wait()
 
 
@@ -918,20 +944,20 @@
     return pl.pallas_call(
         forward_kernel,
         out_shape=(
+            shaped((8, seq), f32),
+            shaped((3 * ff // 2, d // ndp), f32),
+            shaped((8, seq), f32),
+            shaped((8, seq), f32),
+            shaped((seq, 1), f32),
+            shaped((1, seq), f32),
             shaped((rows, d), f32),
             shaped((width, seq)),
             shaped((width, seq)),
             shaped((width, seq)),
             shaped((width, seq)),
-            shaped((8, seq), f32),
             shaped((2, seq, ff // 2)),
             shaped((2, seq, ff // 2)),
             shaped((2, seq, ff // 2)),
-            shaped((3 * ff // 2, d // ndp), f32),
-            shaped((8, seq), f32),
-            shaped((8, seq), f32),
-            shaped((seq, 1), f32),
-            shaped((1, seq), f32),
             shaped((seq, d)),
             shaped((3, d, width)),
             shaped((width, d)),
@@ -940,7 +966,7 @@
             shaped((3 * ff // 2, d)),
         ),
         in_specs=[pl.BlockSpec(memory_space=pltpu.SMEM)] + [VMEM] * 7 + [ANY] * 4,
-        out_specs=(VMEM,) * 14 + (ANY,) * 6,
+        out_specs=(VMEM,) * 6 + (ANY,) * 14,
         scratch_shapes=[
             pltpu.VMEM((rows, d), bf16),
             pltpu.VMEM((rows, d), bf16),
@@ -959,12 +985,20 @@
             pltpu.VMEM((ff // 2, seq), bf16),
             pltpu.VMEM((3 * ff // 2, d), bf16),
             pltpu.VMEM((3, width), f32),
+            pltpu.VMEM((rows, d), f32),
+            pltpu.VMEM((width, seq), bf16),
+            pltpu.VMEM((width, seq), bf16),
+            pltpu.VMEM((width, seq), bf16),
+            pltpu.VMEM((width, seq), bf16),
+            pltpu.VMEM((2, seq, ff // 2), bf16),
+            pltpu.VMEM((2, seq, ff // 2), bf16),
+            pltpu.VMEM((2, seq, ff // 2), bf16),
         ]
         + depth_sems(ndp) * 8
         + gather_sems(nctx) * 3
         + scatter_scratch(nctx, rows, d)
         + depth_scatter_scratch(ndp, 3 * ff // 2, d // ndp)
-        + [DMA((6,))],
+        + [DMA((17,))],
         compiler_params=pltpu.CompilerParams(
             collective_id=0, has_side_effects=True, vmem_limit_bytes=67_000_000
         ),
@@ -1046,10 +1080,10 @@
 
 
 def middle_kernel(
-    gate_ref, up_ref, w_hbm, part_ref, resid_ref, cot_ref, gain_ref, out_ref, rows_ref,
-    cos_ref, sin_ref, pos_col, pos_row, q_t, k_t, v_t, attn_t, lse,
+    gate_ref, up_ref, w_hbm, part_ref, resid_ref, cot_ref, gain_ref, out_hbm, rows_ref,
+    cos_ref, sin_ref, pos_col, pos_row, q_hbm, k_hbm, v_hbm, attn_hbm, lse,
     grad_ref, vec_ref, parts_ref, sums_ref, second_sums, w_out,
-    arena, part_all, block, grad_all, g_t, delta, q_grad, kv_grad, bias, flat, rows_buf, rows_sem, save_sem, *scratch
+    arena, part_all, block, out_ref, q_t, k_t, v_t, attn_t, grad_all, g_t, delta, q_grad, kv_grad, bias, flat, rows_buf, rows_sem, save_sem, *scratch
 ):
     place = Place()
     greet(place, along_dp=True)
@@ -1070,10 +1104,17 @@
     summed.start()
     load = pltpu.make_async_copy(w_hbm, arena, save_sem.at[0])
     fetch = pltpu.make_async_copy(part_ref, part_all, save_sem.at[1])
+    later = [
+        pltpu.make_async_copy(src, dst, save_sem.at[4 + i])
+        for i, (src, dst) in enumerate(
+            ((out_hbm, out_ref), (q_hbm, q_t), (k_hbm, k_t), (v_hbm, v_t), (attn_hbm, attn_t))
+        )
+    ]
     load.start()
     fetch.start()
+    for copy in later:
+        copy.start()
     load.wait()
-    fetch.wait()
 
     def product(at, cols):
         total = dot_nn(gate_ref[0, at, :], arena[:half, cols])
@@ -1098,9 +1139,12 @@
     row_loop(rows, back)
     gathered = row_gather(place, block, grad_all, *take(3))
     gathered.start()
+    fetch.wait()
     summed.hand_on(0)
     gathered.forward()
     gathered.finish()
+    for copy in later:
+        copy.wait()
     scatter.finish()
 
     def between():
@@ -1133,12 +1177,17 @@
             jax.ShapeDtypeStruct((3 * ff // 2, d // ndp), f32),
             jax.ShapeDtypeStruct((4 * width, d), bf16),
         ),
-        in_specs=[VMEM] * 2 + [ANY] * 2 + [VMEM] * 4 + [ANY] + [VMEM] * 9,
+        in_specs=[VMEM] * 2 + [ANY] * 2 + [VMEM] * 3 + [ANY] * 2 + [VMEM] * 4 + [ANY] * 4 + [VMEM],
         out_specs=(VMEM,) * 5 + (ANY,),
         scratch_shapes=[
             pltpu.VMEM((2 * ff, d), bf16),
             pltpu.VMEM((3 * ff // 2, d), bf16),
             pltpu.VMEM((rows, d), bf16),
+            pltpu.VMEM((width, d), bf16),
+            pltpu.VMEM((width, seq), bf16),
+            pltpu.VMEM((width, seq), bf16),
+            pltpu.VMEM((width, seq), bf16),
+            pltpu.VMEM((width, seq), bf16),
             pltpu.VMEM((seq, d), bf16),
             pltpu.VMEM((width, seq), bf16),
             pltpu.VMEM((8, seq), f32),
@@ -1148,7 +1197,7 @@
             pltpu.VMEM((3, width, seq), bf16),
             pltpu.VMEM((2, seq, 2 * PAIR), bf16),
             DMA((2,)),
-            DMA((4,)),
+            DMA((9,)),
         ]
         + scatter_scratch(nctx, rows, d)
         + depth_scatter_scratch(ndp, 3 * ff // 2, d // ndp)
@@ -1229,7 +1278,7 @@
 
 
 def tail_kernel(
-    w_grads, parts_ref, qkv_ref, x_ref, grad_ref, gain_ref, hidden_ref, down_ref, resid_ref, vec_ref, sums_ref,
+    w_grads, parts_hbm, qkv_hbm, x_ref, grad_ref, gain_ref, hidden_hbm, down_ref, resid_ref, vec_ref, sums_ref,
     block_out, input_grad, small, qkv_grads, out_grads,
     total, *scratch
 ):
@@ -1243,20 +1292,24 @@
         return head
 
     rows, d = x_ref.shape
-    width = qkv_ref.shape[2]
+    width = qkv_hbm.shape[2]
     first_refs, second_refs = take(9), take(9)
     long_refs, short_refs = take(4), take(4)
     vectors = VectorSum(place, *take(8))
-    w_all, down_all, load_sem = take(3)
+    w_all, down_all, parts_ref, qkv_ref, hidden_ref, load_sem = take(6)
     piece, cut = d // place.ndp, 3 * width
     upper, lower = pl.ds(0, cut), pl.ds(cut, width)
     long_sum = DepthScatter(place, w_grads.at[upper], w_all.at[upper], *long_refs[:2], piece, *long_refs[2:])
     short_sum = DepthScatter(place, w_grads.at[lower], w_all.at[lower], *short_refs[:2], piece, *short_refs[2:])
-    long_sum.start()
-    short_sum.start()
+    long_sum.start_first()
+    short_sum.start_first()
+    long_sum.start_last()
+    short_sum.start_last()
     loads = [
-        pltpu.make_async_copy(w_grads, w_all, load_sem.at[0]),
-        pltpu.make_async_copy(down_ref, down_all, load_sem.at[1]),
+        pltpu.make_async_copy(src, dst, load_sem.at[i])
+        for i, (src, dst) in enumerate(
+            ((parts_hbm, parts_ref), (qkv_hbm, qkv_ref), (w_grads, w_all), (hidden_hbm, hidden_ref), (down_ref, down_all))
+        )
     ]
     for copy in loads:
         copy.start()
@@ -1273,6 +1326,8 @@
         return dot_nn(hidden_ref[0, at, :], down_all[:half, cols]) + dot_nn(hidden_ref[1, at, :], down_all[half:, cols])
 
     second = sum_scatter(place, rows, down_product, *second_refs[:5], second_refs[5:9])
+    for copy in loads[:2]:
+        copy.wait()
     first.run()
     gain = gain_ref[...].astype(jnp.float32)[None, :]
     value = vectors.value
@@ -1289,19 +1344,26 @@
 
     row_loop(rows, back)
     vectors.start()
-    for copy in loads:
+    for copy in loads[2:]:
         copy.wait()
     long_sum.hand_on(0)
-    second.run((lambda: long_sum.hand_on(1), lambda: long_sum.hand_on(2)))
+
+    def between_first():
+        long_sum.hand_on(1)
+        short_sum.hand_on(0)
+
+    def between_second():
+        long_sum.hand_on(2)
+        short_sum.hand_on(1)
+
+    second.run((between_first, between_second))
+    short_sum.hand_on(2)
 
     def add(at):
         block_out[at, :] = (resid_ref[at, :] + second.total(at)).astype(jnp.bfloat16)
 
     row_loop(rows, add)
     vectors.turn()
-    short_sum.hand_on(0)
-    short_sum.hand_on(1)
-    short_sum.hand_on(2)
     first.finish()
     second.finish()
     vectors.finish(small)
@@ -1325,14 +1387,15 @@
             jax.ShapeDtypeStruct((3, d // ndp, width), f32),
             jax.ShapeDtypeStruct((width, d // ndp), f32),
         ),
-        in_specs=[ANY] + [VMEM] * 6 + [ANY] + [VMEM] * 3,
+        in_specs=[ANY] * 3 + [VMEM] * 3 + [ANY] * 2 + [VMEM] * 3,
         out_specs=(VMEM,) * 5,
         scratch_shapes=[pltpu.VMEM((3 * width, d // ndp), f32)]
         + scatter_scratch(nctx, rows, d) * 2
         + depth_scatter_scratch(ndp, 3 * width, d // ndp)
         + depth_scatter_scratch(ndp, width, d // ndp)
         + vector_scratch(ndp, nctx, (8, d))
-        + [pltpu.VMEM((4 * width, d), bf16), pltpu.VMEM(down.shape, bf16), DMA((2,))],
+        + [pltpu.VMEM(v.shape, bf16) for v in (w_grads, down, parts, qkv, hidden)]
+        + [DMA((5,))],
         compiler_params=pltpu.CompilerParams(
             collective_id=3, has_side_effects=True, vmem_limit_bytes=67_000_000
         ),
@@ -1357,7 +1420,8 @@
 ):
     width_local = qkv_weight.shape[2]
     (
-        residual_stream, q_t, k_t, v_t, attn_t, lse, hidden_b, gate_grad, up_grad, first_sums, cos_all, sin_all, pos_col, pos_row,
+        lse, first_sums, cos_all, sin_all, pos_col, pos_row,
+        residual_stream, q_t, k_t, v_t, attn_t, hidden_b, gate_grad, up_grad,
         rows_all, qkv_local, out_local, gateup_local, down_local, mlp_grads,
     ) = forward(
         group_perm, block_input, out_cotangent, attn_norm_gain, attn_norm_bias, mlp_norm_gain, mlp_norm_bias, qkv_bias,

time: 443 us -> 440 us (level)
  no operation moved by 1% of the time
where the time goes in v6:
time: 440 us; the launch traced here: 439 us
  Pallas kernels  426 us (97%)
  local copies, waits for them, and re-layouts  9.48 us (2%)
    pallas_call x1, Pallas kernels, forward(): pl.pallas_call(forward_kernel, out_shape=(shaped((8, seq), f32), shaped((...  256 us
    pallas_call x1, Pallas kernels, tail(): pl.pallas_call(tail_kernel, out_shape=(jax.ShapeDtypeStruct((rows, d), bf...  85.4 us
    pallas_call x1, Pallas kernels, middle(): pl.pallas_call(middle_kernel, out_shape=(jax.ShapeDtypeStruct((rows, d),...  84.7 us

profile of v6, /device:TPU:0, one launch (start us, length us, event | category | flops | bytes accessed | tf_op | source)
XLA Modules:
  0.0 439.4 jit_solution(2445686843015341796)
XLA Ops:
  0.6 255.9 %forward.1 = (f32[8,1024]{1,0:T(8,128)}, f32[1056,512]{1,0:T(8,128)}, f32[8,1024]{1,0:T(8,128)}, f32[8,1024]{1,0:T(8,128)}, f32[1024,1]{1,0:T(8,128)}, /*index=5...) custom-call(s32[1,16]{1,0:T(1,128)} %perm_ref.1, ...), custom_call_target="tpu_custom_call" | custom-call | bytes 700000000 | tf_op jit(solution)/shard_map/forward/pallas_call | solution.py:944
  256.5 84.7 %middle.1 = (f32[128,2048]{1,0:T(8,128)}, f32[2,2048]{1,0:T(2,128)}, bf16[3,1024,256]{2,1,0:T(8,128)(2,1)}, f32[3,256]{1,0:T(4,128)}, f32[1056,512]{1,0:T(8,128)}, /*index=5*/bf16[1024,2048]{1,0:T(8,128)(2,1)}) custom-call(bf16[2,1024,352]{2,1,0:T(8,128)(2,1)} %get-tuple-element.42.gate_ref, bf16[2,1024,352]{2,1,0:T(8,128)(2,1)} %get-tuple-element.43.up_ref, ...), custom_call_target="tpu_custom_call" | custom-call | bytes 300000000 | tf_op jit(solution)/shard_map/middle/pallas_call | solution.py:1170
  341.2 85.4 %tail.1 = (bf16[128,2048]{1,0:T(8,128)(2,1)}, f32[128,2048]{1,0:T(8,128)}, f32[8,2048]{1,0:T(8,128)}, f32[3,512,256]{2,1,0:T(8,128)}, f32[256,512]{1,0:T(8,128)}) custom-call(bf16[1024,2048]{1,0:T(8,128)(2,1)} %get-tuple-element.58.w_grads, bf16[3,1024,256]{2,1,0:T(8,128)(2,1)} %get-tuple-element.59.parts_hbm, ...), custom_call_target="tpu_custom_call" | custom-call | bytes 300000000 | tf_op jit(solution)/shard_map/tail/pallas_call | solution.py:1381
  426.6 1.5 slice.35
  428.0 1.6 fusion.2
  429.7 0.0 copy-start
  429.7 1.9 fusion.1
  431.5 0.4 copy-done
  431.9 0.2 fusion
  432.1 1.2 pad_maximum_fusion
  433.3 0.3 maximum_bitcast_fusion.1
  433.6 0.0 copy-start.4
  433.6 0.0 copy-start.2
  433.6 1.9 maximum_bitcast_fusion
  435.5 0.0 copy-done.4
  435.5 0.0 copy-start.1
  435.5 0.8 copy.27
  436.3 0.0 copy-done.2
  436.3 1.0 copy.28
  437.2 0.0 copy-done.1
  437.2 0.0 copy-start.3
  437.2 1.1 copy.29
  438.4 0.3 copy-done.3
  438.6 0.8 copy.30
Async XLA Ops:
  429.7 2.3 copy-start
  433.6 1.9 copy-start.4
  433.6 2.7 copy-start.2
  435.5 1.8 copy-start.1
  437.2 1.4 copy-start.3

commit v7 on v6

--- a/solution.py
+++ b/solution.py
@@ -1009,7 +1009,7 @@
 
 def attend_back(
     grad_ref, w_ref, rows_ref, cos_ref, sin_ref, pos_col, pos_row, q_t, k_t, v_t, attn_t, lse,
-    parts_ref, sums_ref, w_grads, g_t, delta, q_grad, kv_grad, bias, flat, rows_buf, rows_sem, between
+    parts_ref, sums_ref, w_grads, g_t, delta, q_grad, kv_grad, bias, flat, rows_buf, rows_sem, between, w_out, w_sem
 ):
     seq, d = grad_ref.shape
     width = w_ref.shape[0]
@@ -1075,15 +1075,21 @@
         for i in range(3):
             w_grads[i * width : (i + 1) * width, cols] = dot_nn(flat[i], rows).astype(bf16)
         w_grads[3 * width : 4 * width, cols] = dot_nn(attn_t[...], grad_ref[:, cols]).astype(bf16)
+        keep(j).start()
+
+    def keep(j):
+        cols = span(j, 2 * PAIR)
+        return pltpu.make_async_copy(w_grads.at[:, cols], w_out.at[:, cols], w_sem.at[j])
 
     tiles(count, weights)
+    return lambda: tiles(count, lambda j: keep(j).wait())
 
 
 def middle_kernel(
     gate_ref, up_ref, w_hbm, part_ref, resid_ref, cot_ref, gain_ref, out_hbm, rows_ref,
     cos_ref, sin_ref, pos_col, pos_row, q_hbm, k_hbm, v_hbm, attn_hbm, lse,
     grad_ref, vec_ref, parts_ref, sums_ref, second_sums, w_out,
-    arena, part_all, block, out_ref, q_t, k_t, v_t, attn_t, grad_all, g_t, delta, q_grad, kv_grad, bias, flat, rows_buf, rows_sem, save_sem, *scratch
+    arena, part_all, block, out_ref, q_t, k_t, v_t, attn_t, grad_all, g_t, delta, q_grad, kv_grad, bias, flat, rows_buf, rows_sem, save_sem, w_sem, *scratch
 ):
     place = Place()
     greet(place, along_dp=True)
@@ -1152,14 +1158,12 @@
         summed.hand_on(2)
 
     w_grads = arena.at[: w_out.shape[0]]
-    attend_back(
+    kept = attend_back(
         grad_all, out_ref, rows_ref, cos_ref, sin_ref, pos_col, pos_row, q_t, k_t, v_t, attn_t, lse,
-        parts_ref, sums_ref, w_grads, g_t, delta, q_grad, kv_grad, bias, flat, rows_buf, rows_sem, between,
+        parts_ref, sums_ref, w_grads, g_t, delta, q_grad, kv_grad, bias, flat, rows_buf, rows_sem, between, w_out, w_sem,
     )
-    keep = pltpu.make_async_copy(w_grads, w_out, save_sem.at[2])
-    keep.start()
     summed.finish(second_sums)
-    keep.wait()
+    kept()
 
 
 def middle(gate_grad, up_grad, w, part, resid, cot, gain, out, rows_all, cosine, sine, pos_col, pos_row, q_t, k_t, v_t, attn_t, lse):
@@ -1198,6 +1202,7 @@
             pltpu.VMEM((2, seq, 2 * PAIR), bf16),
             DMA((2,)),
             DMA((9,)),
+            DMA((d // (2 * PAIR),)),
         ]
         + scatter_scratch(nctx, rows, d)
         + depth_scatter_scratch(ndp, 3 * ff // 2, d // ndp)

time: 440 us -> 440 us (level)
  no operation moved by 1% of the time
where the time goes in v7:
time: 440 us; the launch traced here: 439 us
  Pallas kernels  426 us (97%)
  local copies, waits for them, and re-layouts  9.48 us (2%)
    pallas_call x1, Pallas kernels, forward(): pl.pallas_call(forward_kernel, out_shape=(shaped((8, seq), f32), shaped((...  256 us
    pallas_call x1, Pallas kernels, tail(): pl.pallas_call(tail_kernel, out_shape=(jax.ShapeDtypeStruct((rows, d), bf...  85.4 us
    pallas_call x1, Pallas kernels, middle(): pl.pallas_call(middle_kernel, out_shape=(jax.ShapeDtypeStruct((rows, d),...  84.7 us

profile of v7, /device:TPU:0, one launch (start us, length us, event | category | flops | bytes accessed | tf_op | source)
XLA Modules:
  0.0 439.5 jit_solution(1140372269860043273)
XLA Ops:
  0.6 255.9 %forward.1 = (f32[8,1024]{1,0:T(8,128)}, f32[1056,512]{1,0:T(8,128)}, f32[8,1024]{1,0:T(8,128)}, f32[8,1024]{1,0:T(8,128)}, f32[1024,1]{1,0:T(8,128)}, /*index=5...) custom-call(s32[1,16]{1,0:T(1,128)} %perm_ref.1, ...), custom_call_target="tpu_custom_call" | custom-call | bytes 700000000 | tf_op jit(solution)/shard_map/forward/pallas_call | solution.py:944
  256.5 84.7 %middle.1 = (f32[128,2048]{1,0:T(8,128)}, f32[2,2048]{1,0:T(2,128)}, bf16[3,1024,256]{2,1,0:T(8,128)(2,1)}, f32[3,256]{1,0:T(4,128)}, f32[1056,512]{1,0:T(8,128)}, /*index=5*/bf16[1024,2048]{1,0:T(8,128)(2,1)}) custom-call(bf16[2,1024,352]{2,1,0:T(8,128)(2,1)} %get-tuple-element.42.gate_ref, bf16[2,1024,352]{2,1,0:T(8,128)(2,1)} %get-tuple-element.43.up_ref, ...), custom_call_target="tpu_custom_call" | custom-call | bytes 300000000 | tf_op jit(solution)/shard_map/middle/pallas_call | solution.py:1174
  341.2 85.4 %tail.1 = (bf16[128,2048]{1,0:T(8,128)(2,1)}, f32[128,2048]{1,0:T(8,128)}, f32[8,2048]{1,0:T(8,128)}, f32[3,512,256]{2,1,0:T(8,128)}, f32[256,512]{1,0:T(8,128)}) custom-call(bf16[1024,2048]{1,0:T(8,128)(2,1)} %get-tuple-element.58.w_grads, bf16[3,1024,256]{2,1,0:T(8,128)(2,1)} %get-tuple-element.59.parts_hbm, ...), custom_call_target="tpu_custom_call" | custom-call | bytes 300000000 | tf_op jit(solution)/shard_map/tail/pallas_call | solution.py:1386
  426.6 1.5 slice.35
  428.1 1.6 fusion.2
  429.7 0.0 copy-start
  429.7 1.9 fusion.1
  431.6 0.4 copy-done
  432.0 0.2 fusion
  432.1 1.2 pad_maximum_fusion
  433.3 0.3 maximum_bitcast_fusion.1
  433.6 0.0 copy-start.4
  433.6 0.0 copy-start.2
  433.6 1.9 maximum_bitcast_fusion
  435.5 0.0 copy-done.4
  435.5 0.0 copy-start.1
  435.5 0.8 copy.27
  436.3 0.0 copy-done.2
  436.3 1.0 copy.28
  437.3 0.0 copy-done.1
  437.3 0.0 copy-start.3
  437.3 1.1 copy.29
  438.4 0.3 copy-done.3
  438.7 0.8 copy.30
Async XLA Ops:
  429.7 2.3 copy-start
  433.6 1.9 copy-start.4
  433.6 2.7 copy-start.2
  435.5 1.8 copy-start.1
  437.3 1.4 copy-start.3
